TPU v7x, 128 devices: a whole 4x4x4 slice. The times are simulated.
128 devices in a mesh: pts: 32 (over x, y, core), head: 4 (over z).
Axes of the slice: x: 4, y: 4, z: 4, core: 2. Of those that a mesh axis runs over, the one named last changes fastest.
Arguments:
- tokens: bfloat16 [65536, 1024], P(('pts', 'head')), may hold values from -6 to 6
- w_query: bfloat16 [1024, 1024], replicated, may hold values from -0.1875 to 0.1875
- w_key: bfloat16 [1024, 256], replicated, may hold values from -0.1875 to 0.1875
- w_value: bfloat16 [1024, 256], replicated, may hold values from -0.1875 to 0.1875
- w_out: bfloat16 [1024, 1024], replicated, may hold values from -0.1875 to 0.1875
- logit_scale: float32 [16], replicated, may hold values from 1 to 64
- w_gate: bfloat16 [1024, 2048], replicated, may hold values from -0.1875 to 0.1875
- w_up: bfloat16 [1024, 2048], replicated, may hold values from -0.1875 to 0.1875
- w_down: bfloat16 [2048, 1024], replicated, may hold values from -0.125 to 0.125
- picks: int32 [512, 4], P('pts'), may hold values from 0 to 511, as said below
Outputs:
- mixed: bfloat16 [65536, 1024], P(('pts', 'head'))
Inputs may be any that keep to these rules, and one draw needn't show every extreme that they name: `picks`: each row names 4 different blocks, none of them held by the row's own index of pts (block id // 16). Among the rows of one index of pts, at most 2 different blocks of any other index are named, and exactly 2 for some index.
All inputs are finite; a program needn't handle non-finite values.
Results may differ from a plain program's by a relative error of at most 0.0095.
The roundings to bfloat16 on the way count: a program that leaves them out, or rounds other values in their place, can miss the bound.
Values may be sent and summed in bfloat16 or wider, within the bound.
No kernel may reach another device: no remote copies, remote signals or barrier semaphores. Data moves between devices by JAX's collectives and lax.ppermute only.
A program may use at most 128 MiB of HBM per device.

v0:
```python
import math

import jax
import jax.numpy as jnp
from jax import lax
from jax.sharding import PartitionSpec as P

HEADS = 16
KV_HEADS = 4
HEAD_DIM = 64
BALL = 256
BLOCK = 128
CMP = 64
PICKS = 4
CAP = 2


EPS = 1e-06


def copy_for_each(array, axis):
    copies = jnp.broadcast_to(array, (lax.axis_size(axis), *array.shape))
    return lax.all_to_all(copies, axis, split_axis=0, concat_axis=0, tiled=True)


def laid_out(pieces, dim):
    lengths = list(pieces.shape[1:])
    lengths[dim] *= pieces.shape[0]
    return jnp.moveaxis(pieces, 0, dim).reshape(lengths)


def gather_directly(array, axis, dim):
    pieces = copy_for_each(array, axis)
    return laid_out(pieces, dim)


def rms_rows(values_in):
    return values_in * lax.rsqrt(jnp.mean(values_in * values_in, axis=-1, keepdims=True) + EPS)


def slot_table(flat_ids, owners_count, per_owner):
    all_ids = jnp.arange(owners_count * per_owner, dtype=jnp.int32)
    present = (
        jnp.any(flat_ids[:, None] == all_ids[None, :], axis=0)
        .reshape(owners_count, per_owner)
        .astype(jnp.int32)
    )
    slot_of = jnp.cumsum(present, axis=1) - 1
    offsets = jnp.arange(per_owner, dtype=jnp.int32)
    wanted = jnp.stack(
        [
            jnp.sum(jnp.where((present == 1) & (slot_of == number), offsets[None, :], 0), axis=1)
            for number in range(CAP)
        ],
        axis=1,
    )
    return (wanted, slot_of)


def on_device(tokens, w_query, w_key, w_value, w_out, logit_scale, w_gate, w_up, w_down, picks):
    heads_count = lax.axis_size("head")
    head_index = lax.axis_index("head")
    pts_count = lax.axis_size("pts")
    own_rows = tokens.shape[0]
    local_heads = HEADS // heads_count
    local_groups = KV_HEADS // heads_count
    ratio = HEADS // KV_HEADS
    query_width = local_heads * HEAD_DIM
    pair_width = local_groups * 2 * HEAD_DIM
    per_ball = BALL // BLOCK
    normed = rms_rows(tokens.astype(jnp.float32)).astype(jnp.bfloat16)
    queries = jnp.dot(normed, w_query, preferred_element_type=jnp.float32).reshape(
        own_rows, HEADS, HEAD_DIM
    )
    query_all = rms_rows(queries).astype(jnp.bfloat16).reshape(own_rows, HEADS * HEAD_DIM)
    keys_raw = jnp.dot(normed, w_key, preferred_element_type=jnp.float32).reshape(
        own_rows, KV_HEADS, HEAD_DIM
    )
    key_all = rms_rows(keys_raw).astype(jnp.bfloat16)
    value_all = (
        jnp.dot(normed, w_value, preferred_element_type=jnp.float32)
        .astype(jnp.bfloat16)
        .reshape(own_rows, KV_HEADS, HEAD_DIM)
    )
    pairs_all = jnp.stack([key_all, value_all], axis=2).reshape(own_rows, KV_HEADS * 2 * HEAD_DIM)
    query_hat, pairs = (
        lax.all_to_all(query_all, "head", split_axis=1, concat_axis=0, tiled=True),
        lax.all_to_all(pairs_all, "head", split_axis=1, concat_axis=0, tiled=True),
    )
    group_rows_n = query_hat.shape[0]
    blocks_here = group_rows_n // BLOCK
    balls_here = group_rows_n // BALL
    pair_four = pairs.reshape(group_rows_n, local_groups, 2, HEAD_DIM)
    means = jnp.mean(
        pair_four.astype(jnp.float32).reshape(group_rows_n // CMP, CMP, local_groups, 2, HEAD_DIM),
        axis=1,
    )
    summary_key = rms_rows(means[:, :, 0]).astype(jnp.bfloat16)
    summary_value = means[:, :, 1].astype(jnp.bfloat16)
    summary = jnp.stack([summary_key, summary_value], axis=2).reshape(
        group_rows_n // CMP, pair_width
    )
    summaries = gather_directly(summary, "pts", 0)
    summaries = summaries.reshape(-1, local_groups, 2, HEAD_DIM)
    summary_keys = summaries[:, :, 0]
    summary_values = summaries[:, :, 1]
    local_blocks = pairs.reshape(blocks_here, BLOCK, pair_width)
    flat_ids = picks.reshape(-1)
    owner_dev = flat_ids // blocks_here
    wanted, slot_of = slot_table(flat_ids, pts_count, blocks_here)
    asked_for = lax.all_to_all(wanted, "pts", split_axis=0, concat_axis=0, tiled=True)
    replies = local_blocks[asked_for.reshape(-1)].reshape(pts_count, CAP, BLOCK, pair_width)
    fetched = lax.all_to_all(replies, "pts", split_axis=0, concat_axis=0, tiled=True).reshape(
        pts_count * CAP, BLOCK, pair_width
    )
    where_slot = slot_of.reshape(-1)[flat_ids]
    chosen = fetched[owner_dev * CAP + where_slot]
    chosen = chosen.reshape(balls_here, per_ball, PICKS * BLOCK, local_groups, 2, HEAD_DIM)
    own_scale = lax.dynamic_slice_in_dim(logit_scale, head_index * local_heads, local_heads, 0)
    factor = (own_scale / math.sqrt(HEAD_DIM)).reshape(local_groups, ratio, 1, 1)
    query_balls = query_hat.reshape(balls_here, BALL, local_groups, ratio, HEAD_DIM)
    pair_balls = pair_four.reshape(balls_here, BALL, local_groups, 2, HEAD_DIM)

    def one_ball(items):
        here, near, picked = items
        score_ball = (
            jnp.einsum("tgrd,kgd->grtk", here, near[:, :, 0], preferred_element_type=jnp.float32)
            * factor
        )
        score_cmp = (
            jnp.einsum("tgrd,kgd->grtk", here, summary_keys, preferred_element_type=jnp.float32)
            * factor
        )
        grouped = here.reshape(per_ball, BLOCK, local_groups, ratio, HEAD_DIM)
        score_far = (
            jnp.einsum(
                "cqgrd,ckgd->grcqk", grouped, picked[:, :, :, 0], preferred_element_type=jnp.float32
            ).reshape(local_groups, ratio, BALL, PICKS * BLOCK)
            * factor
        )
        peak = jnp.maximum(
            jnp.maximum(jnp.max(score_ball, axis=-1), jnp.max(score_cmp, axis=-1)),
            jnp.max(score_far, axis=-1),
        )[..., None]
        expo_ball = jnp.exp(score_ball - peak)
        expo_cmp = jnp.exp(score_cmp - peak)
        expo_far = jnp.exp(score_far - peak)
        totals = (
            jnp.sum(expo_ball, axis=-1) + jnp.sum(expo_cmp, axis=-1) + jnp.sum(expo_far, axis=-1)
        )
        weight_far = expo_far.astype(jnp.bfloat16).reshape(
            local_groups, ratio, per_ball, BLOCK, PICKS * BLOCK
        )
        summed = jnp.einsum(
            "grtk,kgd->tgrd",
            expo_ball.astype(jnp.bfloat16),
            near[:, :, 1],
            preferred_element_type=jnp.float32,
        )
        summed = summed + jnp.einsum(
            "grtk,kgd->tgrd",
            expo_cmp.astype(jnp.bfloat16),
            summary_values,
            preferred_element_type=jnp.float32,
        )
        summed = summed + jnp.einsum(
            "grcqk,ckgd->cqgrd", weight_far, picked[:, :, :, 1], preferred_element_type=jnp.float32
        ).reshape(BALL, local_groups, ratio, HEAD_DIM)
        result = summed / jnp.transpose(totals, (2, 0, 1))[..., None]
        return result.reshape(BALL, query_width).astype(jnp.bfloat16)

    attended = lax.map(one_ball, (query_balls, pair_balls, chosen)).reshape(
        group_rows_n, query_width
    )
    merged = lax.all_to_all(attended, "head", split_axis=0, concat_axis=1, tiled=True)
    mid = tokens.astype(jnp.float32) + jnp.dot(merged, w_out, preferred_element_type=jnp.float32)
    normed_mid = rms_rows(mid).astype(jnp.bfloat16)
    gate = jnp.dot(normed_mid, w_gate, preferred_element_type=jnp.float32)
    upward = jnp.dot(normed_mid, w_up, preferred_element_type=jnp.float32)
    hidden = (jax.nn.silu(gate) * upward).astype(jnp.bfloat16)
    return (mid + jnp.dot(hidden, w_down, preferred_element_type=jnp.float32)).astype(jnp.bfloat16)


def solution(mesh):
    placed = (P(("pts", "head"), None), P(), P(), P(), P(), P(), P(), P(), P(), P("pts", None))
    return jax.shard_map(
        on_device, mesh=mesh, in_specs=placed, out_specs=P(("pts", "head"), None), check_vma=False
    )
```

profile of v0, /device:TPU:0, one launch (start us, length us, event | category | flops | bytes accessed | tf_op | source)
XLA Modules:
  0.0 221.0 jit_solution(12578649187828459514)
XLA Ops:
  0.0 1.7 fusion.36
  1.7 1.9 convolution_convert_fusion
  5.1 5.4 %all-to-all-start = ((bf16[512,4,128]{0,2,1:T(8,128)(2,1)}), bf16[512,4,128]{0,2,1:T(8,128)(2,1)S(1)}, u32[]{:S(2)}, u32[]{:S(2)}) async-start(bf16[512,4,128]{0,2,1:T(8,128)(2,1)} %bitcast.45), calls=%async_computation | async-start | bytes 1048576 | tf_op jit(solution)/shard_map/all_to_all | solution.py:88
  11.9 4.4 %fusion.52 = (f32[512,1024]{1,0:T(8,128)}, f32[512,1024]{1,0:T(8,128)}) fusion(bf16[1024,1024]{1,0:T(8,128)(2,1)S(1)} %copy-done, bf16[512,1024]{1,0:T(8,128)(2,1)} %param.12, f32[512]{0:T(512)S(1)} %add_rsqrt_fusion.3), kind=kOutput, calls=%fused_computation.109 | convolution fusion | flops 1075838976 | bytes 7342080 | tf_op jit(solution)/shard_map/dot_general | solution.py:72
  16.4 1.9 copy.99
  18.9 1.8 copy.100
  20.7 7.3 %all-to-all-start.3 = ((s32[32,1,2]{2,1,0:T(1,128)}), s32[32,1,2]{2,1,0:T(1,128)S(1)}, u32[]{:S(2)}, u32[]{:S(2)}) async-start(s32[32,1,2]{2,1,0:T(1,128)} %copy.108), calls=%async_computation.3 | async-start | bytes 32768 | tf_op jit(solution)/shard_map/all_to_all | solution.py:111
  28.2 1.7 copy.103
  29.8 1.8 reshape.474
  32.4 3.0 %all-to-all-done.3 = s32[32,1,2]{2,1,0:T(1,128)S(1)} async-done(((s32[32,1,2]{2,1,0:T(1,128)}), s32[32,1,2]{2,1,0:T(1,128)S(1)}, u32[]{:S(2)}, u32[]{:S(2)}) %all-to-all-start.3) | async-done | bytes 288 | tf_op jit(solution)/shard_map/all_to_all | solution.py:111
  36.1 4.4 %all-to-all-start.2 = ((bf16[32,32,128]{2,1,0:T(8,128)(2,1)}), bf16[32,32,128]{2,1,0:T(8,128)(2,1)S(1)}, u32[]{:S(2)}, u32[]{:S(2)}) async-start(bf16[32,32,128]{2,1,0:T(8,128)(2,1)} %broadcast_in_dim.22), calls=%async_computation.2 | async-start | bytes 524288 | tf_op jit(solution)/shard_map/all_to_all | solution.py:23
  40.6 2.5 %multiply_convert_fusion.2 = bf16[512,1024]{1,0:T(8,128)(2,1)S(1)} fusion(f32[512,1024]{1,0:T(8,128)} %get-tuple-element.110, f32[512,1024]{1,0:T(8,128)} %copy.100), kind=kLoop, calls=%fused_computation.64 | loop fusion | flops 1048576 | bytes 5242880 | tf_op jit(solution)/shard_map/convert_element_type | solution.py:75
  43.1 1.3 copy.121
  44.4 5.0 %all-to-all-done.2 = bf16[32,32,128]{2,1,0:T(8,128)(2,1)S(1)} async-done(((bf16[32,32,128]{2,1,0:T(8,128)(2,1)}), bf16[32,32,128]{2,1,0:T(8,128)(2,1)S(1)}, u32[]{:S(2)}, u32[]{:S(2)}) %all-to-all-start.2) | async-done | bytes 262176 | tf_op jit(solution)/shard_map/all_to_all | solution.py:23
  49.5 4.8 %all-to-all-start.1 = ((bf16[512,4,256]{0,2,1:T(8,128)(2,1)}), bf16[512,4,256]{0,2,1:T(8,128)(2,1)S(1)}, u32[]{:S(2)}, u32[]{:S(2)}) async-start(bf16[512,4,256]{0,2,1:T(8,128)(2,1)} %bitcast.306), calls=%async_computation.1 | async-start | bytes 2097152 | tf_op jit(solution)/shard_map/all_to_all | solution.py:87
  56.0 2.1 gather_fusion
  58.1 11.7 %all-to-all-done.1 = bf16[512,4,256]{0,2,1:T(8,128)(2,1)S(1)} async-done(((bf16[512,4,256]{0,2,1:T(8,128)(2,1)}), bf16[512,4,256]{0,2,1:T(8,128)(2,1)S(1)}, u32[]{:S(2)}, u32[]{:S(2)}) %all-to-all-start.1) | async-done | bytes 1048608 | tf_op jit(solution)/shard_map/all_to_all | solution.py:87
  69.9 5.1 %all-to-all-start.4 = ((bf16[32,2,128,128]{3,2,1,0:T(8,128)(2,1)}), bf16[32,2,128,128]{3,2,1,0:T(8,128)(2,1)}, u32[]{:S(2)}, u32[]{:S(2)}) async-start(bf16[32,2,128,128]{3,2,1,0:T(8,128)(2,1)} %bitcast.301), calls=%async_computation.4 | async-start | bytes 4194304 | tf_op jit(solution)/shard_map/all_to_all | solution.py:113
  76.6 0.9 copy.112
  80.5 23.1 %all-to-all-done.4 = bf16[32,2,128,128]{3,2,1,0:T(8,128)(2,1)} async-done(((bf16[32,2,128,128]{3,2,1,0:T(8,128)(2,1)}), bf16[32,2,128,128]{3,2,1,0:T(8,128)(2,1)}, u32[]{:S(2)}, u32[]{:S(2)}) %all-to-all-start.4) | async-done | bytes 2097184 | tf_op jit(solution)/shard_map/all_to_all | solution.py:113
  103.6 2.5 %gather_fusion.2 = bf16[64,128,128]{2,1,0:T(8,128)(2,1)S(1)} fusion(bf16[64,128,128]{2,1,0:T(8,128)(2,1)} %bitcast.61, s32[1024]{0:T(1024)S(1)} %pad_clamp_fusion), kind=kCustom, calls=%fused_computation.2 | custom fusion | bytes 4194560 | tf_op jit(solution)/shard_map/gather | solution.py:117
  106.2 3.3 %reshape.506 = bf16[8,2,512,1,2,64]{5,4,2,1,0,3:T(2,128)(2,1)} reshape(bf16[64,128,128]{2,1,0:T(8,128)(2,1)S(1)} %gather_fusion.2) | data formatting | bytes 4194304 | tf_op jit(solution)/shard_map/reshape | solution.py:118
  109.5 10.6 %copy.114 = bf16[8,2,512,1,2,64]{2,5,1,4,3,0:T(8,128)(2,1)} copy(bf16[8,2,512,1,2,64]{5,4,2,1,0,3:T(2,128)(2,1)} %reshape.506) | data formatting | bytes 4194304 | tf_op jit(solution)/shard_map/while | solution.py:172
  120.1 61.2 %while.10 = (s32[]{:T(128)}, bf16[8,256,256]{2,1,0:T(8,128)(2,1)}, bf16[8,256,1,2,64]{1,4,3,2,0:T(8,128)(2,1)}, bf16[8,256,1,4,64]{1,4,3,2,0:T(8,128)(2,1)S(1)},...) while((s32[]{:T(128)}, bf16[8,256,256]{2,1,0:T(8,128)(2,1)}, ...), condition=%wide.region_16.17_spmd, body=%wide.region_9.16_spmd.sunk | while | flops 484179968 | bytes 25990836 | solution.py:172
  121.0 1.0 dynamic-slice_bitcast_fusion.4
  125.5 0.9 fusion.79
  128.6 1.0 dynamic-slice_bitcast_fusion.4
  132.3 0.9 fusion.82
  133.2 0.9 fusion.79
  136.3 1.0 dynamic-slice_bitcast_fusion.4
  139.9 0.9 fusion.82
  140.8 0.9 fusion.79
  143.9 1.0 dynamic-slice_bitcast_fusion.4
  147.6 0.9 fusion.82
  148.5 0.9 fusion.79
  151.6 1.0 dynamic-slice_bitcast_fusion.4
  156.1 0.9 fusion.79
  159.2 1.0 dynamic-slice_bitcast_fusion.4
  163.8 0.9 fusion.79
  166.8 1.0 dynamic-slice_bitcast_fusion.4
  171.4 0.9 fusion.79
  174.5 1.0 dynamic-slice_bitcast_fusion.4
  179.1 0.9 fusion.79
  181.2 18.8 %all_to_all.70 = bf16[4,512,256]{2,1,0:T(8,128)(2,1)S(1)} all-to-all(bf16[4,512,256]{2,1,0:T(8,128)(2,1)} %bitcast.309), channel_id=1, replica_groups=mesh['pts'=32,'head'=4] {'head'}, dimensions={0} | all-to-all | bytes 2097152 | tf_op jit(solution)/shard_map/all_to_all | solution.py:175
  200.6 3.1 %multiply_reduce_fusion = (f32[512]{0:T(512)S(1)}, f32[512,1024]{1,0:T(8,128)S(1)}) fusion(bf16[512,1024]{0,1:T(8,128)(2,1)S(1)} %bitcast.308, bf16[1024,1024]{1,0:T(8,128)(2,1)} %param.16, bf16[512,1024]{1,0:T(8,128)(2,1)S(1)} %copy-done.3), kind=kOutput, calls=%fused_computation.63 | convolution fusion | flops 1075838464 | bytes 6293504 | tf_op jit(solution)/shard_map/dot_general | solution.py:176
  203.8 1.3 copy-done.4
  205.1 4.3 %fusion.39 = f32[512,2048]{1,0:T(8,128)} fusion(bf16[1024,2048]{1,0:T(8,128)(2,1)S(1)} %copy-done.6, f32[512,1024]{1,0:T(8,128)S(1)} %get-tuple-element.112, f32[512]{0:T(512)S(1)} %add_rsqrt_fusion.2), kind=kOutput, calls=%fused_computation.67 | convolution fusion | flops 2148532224 | bytes 10487808 | tf_op jit(solution)/shard_map/dot_general | solution.py:178
  209.4 11.5 %add_convert_fusion = bf16[512,1024]{1,0:T(8,128)(2,1)} fusion(f32[512,1024]{1,0:T(8,128)} %copy-done.4, bf16[2048,1024]{1,0:T(8,128)(2,1)} %param.20, f32[512,2048]{1,0:T(8,128)} %fusion.39, bf16[1024,2048]{1,0:T(8,128)(2,1)} %param.19, f32[512]{0:T(512)S(1)} %add_rsqrt_fusion.2), kind=kOutput, calls=%fused_computation.61 | convolution fusion | flops 4303355904 | bytes 15730688 | tf_op jit(solution)/shard_map/dot_general | solution.py:181
  (196 shorter events, 54.7 us)
Async XLA Ops:
  0.0 11.9 %copy-start = (bf16[1024,1024]{1,0:T(8,128)(2,1)S(1)}, bf16[1024,1024]{1,0:T(8,128)(2,1)}, u32[]{:S(2)}) copy-start(bf16[1024,1024]{1,0:T(8,128)(2,1)} %param.13) | copy-start | bytes 6291460
  0.0 3.6 %copy-start.2 = (bf16[512,1024]{1,0:T(8,128)(2,1)S(1)}, bf16[512,1024]{1,0:T(8,128)(2,1)}, u32[]{:S(2)}) copy-start(bf16[512,1024]{1,0:T(8,128)(2,1)} %param.12) | copy-start | bytes 3145732
  0.0 3.6 %copy-start.7 = (bf16[1024,256]{1,0:T(8,128)(2,1)S(1)}, bf16[1024,256]{1,0:T(8,128)(2,1)}, u32[]{:S(2)}) copy-start(bf16[1024,256]{1,0:T(8,128)(2,1)} %param.14) | copy-start | bytes 1572868
  3.6 7.0 %copy-start.5 = (s32[16,4]{0,1:T(4,128)S(1)}, s32[16,4]{0,1:T(4,128)}, u32[]{:S(2)}) copy-start(s32[16,4]{0,1:T(4,128)} %param.21) | copy-start | bytes 772
  5.1 15.6 %all-to-all-start = ((bf16[512,4,128]{0,2,1:T(8,128)(2,1)}), bf16[512,4,128]{0,2,1:T(8,128)(2,1)S(1)}, u32[]{:S(2)}, u32[]{:S(2)}) async-start(bf16[512,4,128]{0,2,1:T(8,128)(2,1)} %bitcast.45), calls=%async_computation | async-start | bytes 1048576 | tf_op jit(solution)/shard_map/all_to_all | solution.py:88
  20.7 14.7 %all-to-all-start.3 = ((s32[32,1,2]{2,1,0:T(1,128)}), s32[32,1,2]{2,1,0:T(1,128)S(1)}, u32[]{:S(2)}, u32[]{:S(2)}) async-start(s32[32,1,2]{2,1,0:T(1,128)} %copy.108), calls=%async_computation.3 | async-start | bytes 32768 | tf_op jit(solution)/shard_map/all_to_all | solution.py:111
  36.1 13.3 %all-to-all-start.2 = ((bf16[32,32,128]{2,1,0:T(8,128)(2,1)}), bf16[32,32,128]{2,1,0:T(8,128)(2,1)S(1)}, u32[]{:S(2)}, u32[]{:S(2)}) async-start(bf16[32,32,128]{2,1,0:T(8,128)(2,1)} %broadcast_in_dim.22), calls=%async_computation.2 | async-start | bytes 524288 | tf_op jit(solution)/shard_map/all_to_all | solution.py:23
  49.5 20.4 %all-to-all-start.1 = ((bf16[512,4,256]{0,2,1:T(8,128)(2,1)}), bf16[512,4,256]{0,2,1:T(8,128)(2,1)S(1)}, u32[]{:S(2)}, u32[]{:S(2)}) async-start(bf16[512,4,256]{0,2,1:T(8,128)(2,1)} %bitcast.306), calls=%async_computation.1 | async-start | bytes 2097152 | tf_op jit(solution)/shard_map/all_to_all | solution.py:87
  69.8 6.1 %copy-start.8 = (f32[16]{0:T(128)S(1)}, f32[16]{0:T(128)}, u32[]{:S(2)}) copy-start(f32[16]{0:T(128)} %param.17) | copy-start | bytes 196
  69.9 33.8 %all-to-all-start.4 = ((bf16[32,2,128,128]{3,2,1,0:T(8,128)(2,1)}), bf16[32,2,128,128]{3,2,1,0:T(8,128)(2,1)}, u32[]{:S(2)}, u32[]{:S(2)}) async-start(bf16[32,2,128,128]{3,2,1,0:T(8,128)(2,1)} %bitcast.301), calls=%async_computation.4 | async-start | bytes 4194304 | tf_op jit(solution)/shard_map/all_to_all | solution.py:113
  181.2 19.4 %copy-start.3 = (bf16[512,1024]{1,0:T(8,128)(2,1)S(1)}, bf16[512,1024]{1,0:T(8,128)(2,1)}, u32[]{:S(2)}) copy-start(bf16[512,1024]{1,0:T(8,128)(2,1)} %param.12) | copy-start | bytes 3145732
  200.6 4.5 %copy-start.6 = (bf16[1024,2048]{1,0:T(8,128)(2,1)S(1)}, bf16[1024,2048]{1,0:T(8,128)(2,1)}, u32[]{:S(2)}) copy-start(bf16[1024,2048]{1,0:T(8,128)(2,1)} %param.18) | copy-start | bytes 12582916
  203.7 1.3 copy-start.4
  209.4 11.5 %copy-start.1 = (bf16[1024,1024]{1,0:T(8,128)(2,1)S(1)}, bf16[1024,1024]{1,0:T(8,128)(2,1)}, u32[]{:S(2)}) copy-start(bf16[1024,1024]{1,0:T(8,128)(2,1)} %param.13) | copy-start | bytes 6291460
where the time goes:
time: 222 us; the launch traced here: 221 us
  local copies, waits for them, and re-layouts  58.4 us (26%)
  matrix products  53.5 us (24%)
  waiting for transfers between devices  42.9 us (19%)
  starting transfers between devices  27 us (12%)
  other arithmetic  19.6 us (9%)
  blocking collectives  18.8 us (8%)
    all_to_all x1, waiting for transfers between devices, on_device(): lax.all_to_all(replies, 'pts', split_axis=0, concat_axis=0, tiled=True)  23.1 us
    all_to_all x1, blocking collectives, on_device(): lax.all_to_all(attended, 'head', split_axis=0, concat_axis=1, tiled=True)  18.8 us
    squeeze x16, local copies, waits for them, and re-layouts, on_device(): lax.map(one_ball, (query_balls, pair_balls, chosen))  14.5 us
    while x3, local copies, waits for them, and re-layouts, on_device(): lax.map(one_ball, (query_balls, pair_balls, chosen))  11.7 us
    all_to_all x1, waiting for transfers between devices, on_device(): lax.all_to_all(query_all, 'head', split_axis=1, concat_axis=0, tiled=True)  11.7 us
    dot_general x1, matrix products, on_device(): jnp.dot(hidden, w_down, preferred_element_type=jnp.float32)  11.5 us
    dot_general x8, matrix products, one_ball(): jnp.einsum('grtk,kgd->tgrd', expo_cmp.astype(jnp.bfloat16), summary_value...  7.45 us
    all_to_all x1, starting transfers between devices, on_device(): lax.all_to_all(wanted, 'pts', split_axis=0, concat_axis=0, tiled=True)  7.32 us
  transfers between devices with their start and end apart: 5, of which 4 were waited for; matrix products, arithmetic and copies ran while one was open for 12% of the time, Pallas kernels for 0%

commit v1 on v0

v1 whole, which is shorter than its diff:
```python
import functools
import math

import jax
import jax.numpy as jnp
from jax import lax
from jax.experimental import pallas as pl
from jax.experimental.pallas import tpu as pltpu
from jax.sharding import PartitionSpec as P


HEADS = 16
KV_HEADS = 4
HEAD_DIM = 64
BALL = 256
BLOCK = 128
CMP = 64
PICKS = 4
CAP = 2
EPS = 1e-06
LOG2E = math.log2(math.e)

ROWS = 512
PTS = 32
ZS = 4
BLK_DEV = 16
GROUP_W = 256
PAIR_W = 128
RATIO = HEADS // KV_HEADS
SUM_LOCAL = ROWS // CMP
SUM_ROWS = KV_HEADS * SUM_LOCAL
PAY_ROWS = SUM_ROWS + 16
PER = ROWS // BLOCK
BALLS = ROWS // BALL
FFN = 2048
UNIT = 256
STEPS = 2


bf16 = jnp.bfloat16
f32 = jnp.float32
VMEM = pltpu.VMEM
SMEM = pltpu.SMEM
NT = (((1,), (1,)), ((), ()))


def whole(space):
    return pl.BlockSpec(memory_space=space)


def near_core(array):
    return pltpu.with_memory_space_constraint(array, VMEM)


def far_core(array):
    return pltpu.with_memory_space_constraint(array, pltpu.HBM)


def params(mib):
    return pltpu.CompilerParams(vmem_limit_bytes=mib * 1024 * 1024)


def cost(flops, moved):
    return pl.CostEstimate(flops=flops, bytes_accessed=moved, transcendentals=0)


def head_ones(width):
    r = lax.broadcasted_iota(jnp.int32, (width, width), 0) // HEAD_DIM
    c = lax.broadcasted_iota(jnp.int32, (width, width), 1) // HEAD_DIM
    return jnp.where(r == c, 1.0, 0.0).astype(bf16)


def head_norm(raw, ones):
    squares = raw * raw
    high = squares.astype(bf16)
    low = (squares - high.astype(f32)).astype(bf16)
    sums = jnp.dot(high, ones, preferred_element_type=f32) + jnp.dot(
        low, ones, preferred_element_type=f32
    )
    return raw * lax.rsqrt(sums * (1.0 / HEAD_DIM) + EPS)


def row_norm(x):
    return x * lax.rsqrt(jnp.mean(x * x, axis=-1, keepdims=True) + EPS)


def first_body(
    z, picks, tokens_in, key_in, value_in, query_in,
    c0, c1, c2, c3, q0, q1, q2, q3, payload_out, slots,
    table, tokens, w_key, w_value, w_query, normed, pairs, queries, payload, sems, out_sems,
):
    rows_n = ROWS // STEPS
    weight_copies = [
        pltpu.make_async_copy(key_in, w_key, sems.at[0]),
        pltpu.make_async_copy(value_in, w_value, sems.at[1]),
        pltpu.make_async_copy(query_in, w_query, sems.at[2]),
    ]
    token_copies = [
        pltpu.make_async_copy(
            tokens_in.at[pl.ds(i * rows_n, rows_n)],
            tokens.at[pl.ds(i * rows_n, rows_n)],
            sems.at[3 + i],
        )
        for i in range(STEPS)
    ]
    token_copies[0].start()
    weight_copies[0].start()
    weight_copies[1].start()
    for c in token_copies[1:]:
        c.start()
    weight_copies[2].start()

    def clear(i, _):
        table[i] = -1
        return 0

    lax.fori_loop(0, PTS * CAP, clear, 0, unroll=8)

    def assign(i, _):
        row = i // PICKS
        col = i % PICKS
        pick = picks[col, row]
        owner = pick // BLK_DEV
        offset = pick % BLK_DEV
        first = table[owner * CAP]
        slot = jnp.where((first == offset) | (first == -1), 0, 1)
        table[owner * CAP + slot] = offset
        slots[row, col] = owner * CAP + slot
        return 0

    lax.fori_loop(0, BLK_DEV * PICKS, assign, 0, unroll=4)

    ones = head_ones(GROUP_W)
    key_means, value_means = [], []
    for i in range(STEPS):
        rows = slice(i * rows_n, (i + 1) * rows_n)
        token_copies[i].wait()
        here = row_norm(tokens[rows].astype(f32)).astype(bf16)
        normed[rows] = here
        if i == 0:
            weight_copies[0].wait()
        keys = jnp.dot(here, w_key[...], preferred_element_type=f32)
        keys = head_norm(keys, ones).astype(bf16)
        if i == 0:
            weight_copies[1].wait()
        values = jnp.dot(here, w_value[...], preferred_element_type=f32).astype(bf16)
        runs = (rows_n // CMP, CMP, GROUP_W)
        key_means.append(jnp.mean(keys.astype(f32).reshape(runs), axis=1))
        value_means.append(jnp.mean(values.astype(f32).reshape(runs), axis=1))
        for g in range(KV_HEADS):
            lanes = slice(g * HEAD_DIM, (g + 1) * HEAD_DIM)
            pairs[g, rows] = jnp.concatenate([keys[:, lanes], values[:, lanes]], axis=1)
    for k, c in enumerate((c0, c1, c2, c3)):
        c[...] = pairs[(z[0] + k) % ZS]
    summary_key = head_norm(jnp.concatenate(key_means, axis=0), ones)
    summary_value = jnp.concatenate(value_means, axis=0)
    summary = jnp.concatenate(
        [
            jnp.concatenate(
                [
                    summary_key[:, g * HEAD_DIM : (g + 1) * HEAD_DIM],
                    summary_value[:, g * HEAD_DIM : (g + 1) * HEAD_DIM],
                ],
                axis=1,
            )
            for g in range(KV_HEADS)
        ],
        axis=0,
    ).astype(bf16)
    lane = lax.broadcasted_iota(jnp.int32, (16, PAIR_W), 1)
    for o in range(PTS):
        payload[o, :SUM_ROWS, :] = summary
        first = jnp.maximum(table[o * CAP], 0)
        second = jnp.maximum(table[o * CAP + 1], 0)
        payload[o, SUM_ROWS:, :] = jnp.where(lane == 0, first, second).astype(f32).astype(bf16)
    outs = [pltpu.make_async_copy(payload, payload_out, out_sems.at[ZS])]
    outs[0].start()
    weight_copies[2].wait()
    for k, out in enumerate((q0, q1, q2, q3)):
        start = pl.multiple_of(((z[0] + k) % ZS) * GROUP_W, GROUP_W)
        raw = jnp.dot(normed[...], w_query[:, pl.ds(start, GROUP_W)], preferred_element_type=f32)
        queries[k] = head_norm(raw, ones).astype(bf16)
        outs.append(pltpu.make_async_copy(queries.at[k], out, out_sems.at[k]))
        outs[-1].start()
    for c in outs:
        c.wait()


def first_stage(z, picks, tokens, w_key, w_value, w_query):
    hbm = whole(pltpu.HBM)
    return pl.pallas_call(
        first_body,
        name="first_stage",
        in_specs=[whole(SMEM), whole(SMEM), hbm, hbm, hbm, hbm],
        out_specs=[whole(VMEM)] * ZS + [hbm] * (ZS + 1) + [whole(SMEM)],
        out_shape=[VMEM((ROWS, PAIR_W), bf16)] * ZS
        + [pltpu.HBM((ROWS, GROUP_W), bf16)] * ZS
        + [
            pltpu.HBM((PTS, PAY_ROWS, PAIR_W), bf16),
            jax.ShapeDtypeStruct((BLK_DEV, PICKS), jnp.int32),
        ],
        scratch_shapes=[
            SMEM((PTS * CAP,), jnp.int32),
            VMEM((ROWS, 1024), bf16),
            VMEM((1024, GROUP_W), bf16),
            VMEM((1024, GROUP_W), bf16),
            VMEM((1024, 1024), bf16),
            VMEM((ROWS, 1024), bf16),
            VMEM((KV_HEADS, ROWS, PAIR_W), bf16),
            VMEM((ZS, ROWS, GROUP_W), bf16),
            VMEM((PTS, PAY_ROWS, PAIR_W), bf16),
            pltpu.SemaphoreType.DMA((3 + STEPS,)),
            pltpu.SemaphoreType.DMA((ZS + 1,)),
        ],
        compiler_params=params(24),
        cost_estimate=cost(2 * ROWS * 1024 * 1536, 8 << 20),
    )(z, picks, *[far_core(a) for a in (tokens, w_key, w_value, w_query)])


def reply_body(
    z, told, c0, c1, c2, c3, replies, s0, s1, s2, s3, kv_out, held, sums, asked_v, asked, sems, sum_sems
):
    asked_v[...] = told[:, SUM_ROWS, :].astype(f32).astype(jnp.int32)
    fetch = pltpu.make_async_copy(asked_v, asked, sum_sems.at[ZS])
    fetch.start()
    for k, c in enumerate((c0, c1, c2, c3)):
        held[k] = c[...].reshape(PER, BLOCK, PAIR_W)
    outs = [pltpu.make_async_copy(held, kv_out, sum_sems.at[ZS + 1])]
    fetch.wait()

    def copy(i):
        b = asked[i // CAP, i % CAP]
        k = (z[0] - b // PER + ZS) % ZS
        return pltpu.make_async_copy(held.at[k, b % PER], replies.at[i], sems.at[i])

    def start_one(i, _):
        copy(i).start()
        return 0

    def wait_one(i, _):
        copy(i).wait()
        return 0

    lax.fori_loop(0, PTS * CAP, start_one, 0, unroll=4)
    for k, s in enumerate((s0, s1, s2, s3)):
        start = pl.multiple_of(((z[0] + k) % ZS) * SUM_LOCAL, SUM_LOCAL)
        sums[k] = told[:, pl.ds(start, SUM_LOCAL), :].reshape(PTS * SUM_LOCAL, PAIR_W)
        outs.append(pltpu.make_async_copy(sums.at[k], s, sum_sems.at[k]))
    for c in outs:
        c.start()
    lax.fori_loop(0, PTS * CAP, wait_one, 0, unroll=4)
    for c in outs:
        c.wait()


def reply_stage(z, told, chunks):
    hbm = whole(pltpu.HBM)
    return pl.pallas_call(
        reply_body,
        name="reply_stage",
        in_specs=[whole(SMEM)] + [whole(VMEM)] * 5,
        out_specs=[hbm] * (ZS + 2),
        out_shape=[pltpu.HBM((PTS * CAP, BLOCK, PAIR_W), bf16)]
        + [pltpu.HBM((PTS * SUM_LOCAL, PAIR_W), bf16)] * ZS
        + [pltpu.HBM((ZS, PER, BLOCK, PAIR_W), bf16)],
        scratch_shapes=[
            VMEM((ZS, PER, BLOCK, PAIR_W), bf16),
            VMEM((ZS, PTS * SUM_LOCAL, PAIR_W), bf16),
            VMEM((PTS, PAIR_W), jnp.int32),
            SMEM((PTS, PAIR_W), jnp.int32),
            pltpu.SemaphoreType.DMA((PTS * CAP,)),
            pltpu.SemaphoreType.DMA((ZS + 2,)),
        ],
        compiler_params=params(8),
    )(z, near_core(told), *[near_core(c) for c in chunks])


def ones_beside(kv):
    return jnp.concatenate([jnp.ones((kv.shape[0], HEAD_DIM), kv.dtype), kv[:, HEAD_DIM:]], axis=1)


def near_body(chunk, z, scale, q, kv, s0, s1, s2, s3, *rest):
    state_out, held, state, sems = rest[-4:]
    lane = lax.broadcasted_iota(jnp.int32, (BALL, PAIR_W), 1)
    sums = jnp.concatenate([s0[...], s1[...], s2[...], s3[...]], axis=0)
    sum_keys = sums[:, :HEAD_DIM]
    sum_values = ones_beside(sums)
    half = BALL // BLOCK

    def ball_of(b):
        return kv[chunk, pl.ds(b * half, half)].reshape(BALL, PAIR_W)

    def scores(b, r, keys):
        here = q[pl.ds(b * BALL, BALL), r * HEAD_DIM : (r + 1) * HEAD_DIM]
        ball = lax.dot_general(here, keys, NT, preferred_element_type=f32)
        far = lax.dot_general(here, sum_keys, NT, preferred_element_type=f32)
        held[r % 2, :, :BALL] = ball
        held[r % 2, :, BALL:] = far
        return jnp.maximum(
            jnp.max(ball, axis=1, keepdims=True), jnp.max(far, axis=1, keepdims=True)
        )

    def copy(b, r):
        return pltpu.make_async_copy(state.at[b, r], state_out.at[b, r], sems.at[b, r])

    def one_ball(b, peak):
        ball = ball_of(b)
        values = ones_beside(ball)
        after = jnp.minimum(b + 1, BALLS - 1)
        for r in range(RATIO):
            if r + 1 < RATIO:
                coming = scores(b, r + 1, ball[:, :HEAD_DIM])
            else:
                coming = scores(after, 0, ball_of(after)[:, :HEAD_DIM])
            factor = scale[z[0] * RATIO + r] * (LOG2E / math.sqrt(HEAD_DIM))
            w = jnp.exp2((held[r % 2] - peak) * factor).astype(bf16)
            summed = jnp.dot(w[:, :BALL], values, preferred_element_type=f32) + jnp.dot(
                w[:, BALL:], sum_values, preferred_element_type=f32
            )
            state[b, r] = jnp.where(lane < HEAD_DIM // 2, peak, summed)
            copy(b, r).start()
            peak = coming
        return peak

    lax.fori_loop(0, BALLS, one_ball, scores(0, 0, ball_of(0)[:, :HEAD_DIM]))
    for b in range(BALLS):
        for r in range(RATIO):
            copy(b, r).wait()


def near_stage(chunk, z, scale, q, kv, sums, others):
    return pl.pallas_call(
        functools.partial(near_body, chunk),
        name="near_stage",
        in_specs=[whole(SMEM)] * 2 + [whole(VMEM)] * 6 + [whole(pl.ANY)] * len(others),
        out_specs=whole(pltpu.HBM),
        out_shape=pltpu.HBM((BALLS, RATIO, BALL, PAIR_W), f32),
        scratch_shapes=[
            VMEM((2, BALL, BALL + PTS * SUM_LOCAL * ZS), f32),
            VMEM((BALLS, RATIO, BALL, PAIR_W), f32),
            pltpu.SemaphoreType.DMA((BALLS, RATIO)),
        ],
        compiler_params=params(12),
        cost_estimate=cost(8 * 4 * ROWS * 1280 * 64, 2 << 20),
    )(z, scale, near_core(q), near_core(kv), *[near_core(s) for s in sums], *[far_core(a) for a in others])


def far_body(shift_by, z, slots, scale, q, state, fetched, *rest):
    out, held = rest[-2:]
    lane = lax.broadcasted_iota(jnp.int32, (BLOCK, PAIR_W), 1)
    first_row = ((z[0] - shift_by + ZS) % ZS) * PER

    def part(r):
        return slice(r * BLOCK, (r + 1) * BLOCK)

    def keys_of(i):
        return jnp.concatenate([fetched[slots[first_row + i, j]] for j in range(PICKS)], axis=0)

    def scores(i, slot):
        here = jnp.concatenate(
            [q[pl.ds(i * BLOCK, BLOCK), r * HEAD_DIM : (r + 1) * HEAD_DIM] for r in range(RATIO)],
            axis=0,
        )
        s = lax.dot_general(here, keys_of(i)[:, :HEAD_DIM], NT, preferred_element_type=f32)
        held[slot] = s
        return jnp.max(s, axis=1, keepdims=True)

    def finish(b, i, slot, peak):
        rows = slice(slot * BLOCK, (slot + 1) * BLOCK)
        weights, keeps = [], []
        for r in range(RATIO):
            factor = scale[z[0] * RATIO + r] * (LOG2E / math.sqrt(HEAD_DIM))
            before = jnp.broadcast_to(state[b, r, rows, :1], (BLOCK, PAIR_W))
            new = jnp.maximum(before, peak[part(r)])
            s = held[slot, part(r), :]
            weights.append(
                jnp.concatenate(
                    [
                        jnp.exp2((s[:, part(j)] - new) * factor).astype(bf16)
                        for j in range(PICKS)
                    ],
                    axis=1,
                )
            )
            keeps.append(jnp.exp2((before - new) * factor))
        o = jnp.dot(
            jnp.concatenate(weights, axis=0), ones_beside(keys_of(i)), preferred_element_type=f32
        )
        for r in range(0, RATIO, 2):
            even = state[b, r, rows, :] * keeps[r] + o[part(r)]
            odd = state[b, r + 1, rows, :] * keeps[r + 1] + o[part(r + 1)]
            at = HEAD_DIM // 2
            total = jnp.where(
                lane < HEAD_DIM,
                jnp.broadcast_to(even[:, at : at + 1], (BLOCK, PAIR_W)),
                jnp.broadcast_to(odd[:, at : at + 1], (BLOCK, PAIR_W)),
            )
            summed = jnp.where(lane < HEAD_DIM, pltpu.roll(even, HEAD_DIM, 1), odd)
            out[pl.ds(i * BLOCK, BLOCK), r * HEAD_DIM : (r + 2) * HEAD_DIM] = (
                summed / total
            ).astype(bf16)

    def one_ball(b, peak):
        coming = scores(2 * b + 1, 1)
        finish(b, 2 * b, 0, peak)
        after = scores(jnp.minimum(2 * b + 2, PER - 2), 0)
        finish(b, 2 * b + 1, 1, coming)
        return after

    lax.fori_loop(0, BALLS, one_ball, scores(0, 0))


def far_stage(shift_by, z, slots, scale, q, state, fetched, others):
    return pl.pallas_call(
        functools.partial(far_body, shift_by),
        name="far_stage",
        in_specs=[whole(SMEM)] * 3 + [whole(VMEM)] * 3 + [whole(pl.ANY)] * len(others),
        out_specs=whole(VMEM),
        out_shape=VMEM((ROWS, GROUP_W), bf16),
        scratch_shapes=[VMEM((2, RATIO * BLOCK, PICKS * BLOCK), f32)],
        compiler_params=params(12),
        cost_estimate=cost(8 * 4 * ROWS * 512 * 64, 4 << 20),
    )(z, slots, scale, near_core(q), near_core(state), near_core(fetched), *[far_core(a) for a in others])


def ffn_body(
    z, tokens, a0, a1, a2, a3, w_out, w_gate, w_up, down_in, out, mid_held, held, hidden, w_down, sem
):
    down = pltpu.make_async_copy(down_in, w_down, sem.at[0])
    down.start()
    mid = tokens[...].astype(f32)
    for k, a in enumerate((a0, a1, a2, a3)):
        start = pl.multiple_of(((z[0] + k) % ZS) * GROUP_W, GROUP_W)
        mid = mid + jnp.dot(a[...], w_out[pl.ds(start, GROUP_W), :], preferred_element_type=f32)
    mid_held[...] = mid
    held[...] = row_norm(mid).astype(bf16)
    for j in range(FFN // UNIT):
        cols = slice(j * UNIT, (j + 1) * UNIT)
        gate = jnp.dot(held[...], w_gate[:, cols], preferred_element_type=f32)
        upward = jnp.dot(held[...], w_up[:, cols], preferred_element_type=f32)
        hidden[:, cols] = (gate / (1.0 + jnp.exp(-gate)) * upward).astype(bf16)
    down.wait()
    out[...] = (
        mid_held[...] + jnp.dot(hidden[...], w_down[...], preferred_element_type=f32)
    ).astype(bf16)


def ffn_stage(z, tokens, parts, w_out, w_gate, w_up, w_down):
    return pl.pallas_call(
        ffn_body,
        name="ffn_stage",
        in_specs=[whole(SMEM)] + [whole(VMEM)] * 8 + [whole(pltpu.HBM)],
        out_specs=whole(VMEM),
        out_shape=jax.ShapeDtypeStruct((ROWS, 1024), bf16),
        scratch_shapes=[
            VMEM((ROWS, 1024), f32),
            VMEM((ROWS, 1024), bf16),
            VMEM((ROWS, FFN), bf16),
            VMEM((FFN, 1024), bf16),
            pltpu.SemaphoreType.DMA((1,)),
        ],
        compiler_params=params(24),
        cost_estimate=cost(2 * ROWS * 1024 * 7168, 18 << 20),
    )(z, *[near_core(a) for a in (tokens, *parts, w_out, w_gate, w_up)], far_core(w_down))


def shift(array, k):
    return lax.ppermute(array, "head", [(i, (i + k) % ZS) for i in range(ZS)])


def body(tokens, w_query, w_key, w_value, w_out, logit_scale, w_gate, w_up, w_down, picks):
    z = lax.axis_index("head").astype(jnp.int32).reshape(1)
    first = first_stage(z, picks.T, tokens, w_key, w_value, w_query)
    pairs, query, payload, slots = first[:ZS], first[ZS : 2 * ZS], first[2 * ZS], first[2 * ZS + 1]
    chunks = [pairs[0]] + [shift(pairs[k], k) for k in (1, 2, 3)]
    told = lax.all_to_all(payload, "pts", split_axis=0, concat_axis=0, tiled=True)
    replies, *sums, kv = reply_stage(z, told, chunks)
    replies = replies.reshape(PTS, CAP * BLOCK, PAIR_W)
    fetched = lax.all_to_all(replies, "pts", split_axis=0, concat_axis=0, tiled=True)
    fetched = fetched.reshape(PTS * CAP, BLOCK, PAIR_W)
    sums = [sums[0]] + [shift(sums[k], k) for k in (1, 2, 3)]
    q = [query[0], None, None, None]
    for k in (1, 3, 2):
        q[k] = shift(query[k], k)
    states = [None] * ZS
    done = []
    for k in (0, 1, 3, 2):
        states[k] = near_stage(k, z, logit_scale, q[k], kv, sums, done)
        done = [states[k]]
    parts = [None] * ZS
    for k in (2, 1, 3, 0):
        others = [states[2]] if k != 2 else []
        attended = far_stage(k, z, slots, logit_scale, q[k], states[k], fetched, others)
        parts[k] = shift(attended, ZS - k) if k else attended
    return ffn_stage(z, tokens, parts, w_out, w_gate, w_up, w_down)


def solution(mesh):
    placed = (P(("pts", "head"), None), P(), P(), P(), P(), P(), P(), P(), P(), P("pts", None))
    return jax.shard_map(
        body, mesh=mesh, in_specs=placed, out_specs=P(("pts", "head"), None), check_vma=False
    )
```

time: 222 us -> 110 us (0.50)
  Pallas kernels: 0 us -> 58.6 us
  local copies, waits for them, and re-layouts: 58.4 us -> 3.02 us
  matrix products: 53.5 us -> 0 us
  waiting for transfers between devices: 42.9 us -> 14.4 us
  other arithmetic: 19.6 us -> 0 us
  blocking collectives: 18.8 us -> 0 us
  starting transfers between devices: 27 us -> 33.2 us
    pallas_call x0 -> x11, Pallas kernels: none -> 58.6 us  [the longest x4 19.8 us: near_stage(): pl.pallas_call(functools.partial(near_body, chunk), name='near_stage', in...]
    dot_general x54 -> x0, matrix products: 53.5 us -> none  [the longest x1 11.5 us: on_device(): jnp.dot(hidden, w_down, preferred_element_type=jnp.float32)]
    all_to_all x5 -> x2, waiting for transfers between devices: 42.9 us -> 0.01 us  [the longest x1 0.01 us: body(): lax.all_to_all(payload, 'pts', split_axis=0, concat_axis=0, tiled=True)]
    all_to_all x1 -> x0, blocking collectives: 18.8 us -> none  [on_device(): lax.all_to_all(attended, 'head', split_axis=0, concat_axis=1, tiled=True)]
    ppermute x0 -> x12, starting transfers between devices: none -> 18.3 us  [shift(): return lax.ppermute(array, 'head', [(i, (i + k) % ZS) for i in range(ZS)])]
    reduce_sum x29 -> x0, other arithmetic: 14.7 us -> none  [the longest x8 7.18 us: one_ball(): jnp.sum(expo_cmp, axis=-1)]
    squeeze x16 -> x0, local copies, waits for them, and re-layouts: 14.5 us -> none  [on_device(): lax.map(one_ball, (query_balls, pair_balls, chosen))]
    ppermute x0 -> x12, waiting for transfers between devices: none -> 14.4 us  [shift(): return lax.ppermute(array, 'head', [(i, (i + k) % ZS) for i in range(ZS)])]
  transfers between devices with their start and end apart: 5 -> 14, of which waited for: 4 -> 5; matrix products, arithmetic and copies ran while one was open for 12% -> 0% of each run, Pallas kernels for 0% -> 29%
where the time goes in v1:
time: 110 us
  Pallas kernels  58.6 us (53%)
  starting transfers between devices  33.2 us (30%)
  waiting for transfers between devices  14.4 us (13%)
  local copies, waits for them, and re-layouts  3.02 us (3%)
    pallas_call x4, Pallas kernels, near_stage(): pl.pallas_call(functools.partial(near_body, chunk), name='near_stage', in...  19.8 us
    ppermute x12, starting transfers between devices, shift(): return lax.ppermute(array, 'head', [(i, (i + k) % ZS) for i in range(ZS)])  18.3 us
    pallas_call x4, Pallas kernels, far_stage(): pl.pallas_call(functools.partial(far_body, shift_by), name='far_stage', i...  15.3 us
    ppermute x12, waiting for transfers between devices, shift(): return lax.ppermute(array, 'head', [(i, (i + k) % ZS) for i in range(ZS)])  14.4 us
    pallas_call x1, Pallas kernels, ffn_stage(): pl.pallas_call(ffn_body, name='ffn_stage', in_specs=[whole(SMEM)] + [whol...  11 us
    pallas_call x1, Pallas kernels, first_stage(): pl.pallas_call(first_body, name='first_stage', in_specs=[whole(SMEM), who...  8.93 us
    all_to_all x1, starting transfers between devices, body(): lax.all_to_all(payload, 'pts', split_axis=0, concat_axis=0, tiled=True)  7.44 us
    all_to_all x1, starting transfers between devices, body(): lax.all_to_all(replies, 'pts', split_axis=0, concat_axis=0, tiled=True)  7.37 us
  transfers between devices with their start and end apart: 14, of which 5 were waited for; matrix products, arithmetic and copies ran while one was open for 0% of the time, Pallas kernels for 29%

profile of v1, /device:TPU:0, one launch (start us, length us, event | category | flops | bytes accessed | tf_op | source)
XLA Modules:
  0.0 109.7 jit_solution(1533139540162482224)
XLA Ops:
  0.0 0.7 copy-done.18
  0.7 8.9 %first_stage.1 = (bf16[512,128]{1,0:T(8,128)(2,1)S(1)}, bf16[512,128]{1,0:T(8,128)(2,1)S(1)}, bf16[512,128]{1,0:T(8,128)(2,1)S(1)}, bf16[512,128]{1,0:T(8,128)(2...) custom-call(s32[1]{0:T(128)} %bitcast.z, ...), custom_call_target="tpu_custom_call" | custom-call | flops 1610612736 | bytes 8388608 | tf_op jit(solution)/shard_map/first_stage/pallas_call | solution.py:191
  9.6 7.4 %all-to-all-start = ((bf16[32,48,128]{2,1,0:T(8,128)(2,1)}), bf16[32,48,128]{2,1,0:T(8,128)(2,1)S(1)}, u32[]{:S(2)}, u32[]{:S(2)}) async-start(bf16[32,48,128]{2,1,0:T(8,128)(2,1)} %get-tuple-element.23), calls=%async_computation | async-start | bytes 786432 | tf_op jit(solution)/shard_map/all_to_all | solution.py:476
  17.1 2.0 %collective-permute-start = (bf16[512,128]{1,0:T(8,128)(2,1)S(1)}, bf16[512,128]{1,0:T(8,128)(2,1)S(1)}, u32[]{:S(2)}, u32[]{:S(2)}) collective-permute-start(bf16[512,128]{1,0:T(8,128)(2,1)S(1)} %get-tuple-element.25), channel_id=1, source_target_pairs={{0,1},{1,2},{2,3},{3,0},{4,5},{5,6},{6,7},{7,4},{8,9},{9,10},{10,1... | collective-permute-start | bytes 393224 | tf_op jit(solution)/shard_map/ppermute | solution.py:468
  19.0 3.6 %collective-permute-start.1 = (bf16[512,128]{1,0:T(8,128)(2,1)S(1)}, bf16[512,128]{1,0:T(8,128)(2,1)S(1)}, u32[]{:S(2)}, u32[]{:S(2)}) collective-permute-start(bf16[512,128]{1,0:T(8,128)(2,1)S(1)} %get-tuple-element.26), channel_id=1, source_target_pairs={{0,2},{1,3},{2,0},{3,1},{4,6},{5,7},{6,4},{7,5},{8,10},{9,11},{10,... | collective-permute-start | bytes 393224 | tf_op jit(solution)/shard_map/ppermute | solution.py:468
  22.6 1.0 collective-permute-start.2
  23.6 1.5 %collective-permute-done.c1 = bf16[512,128]{1,0:T(8,128)(2,1)S(1)} collective-permute-done((bf16[512,128]{1,0:T(8,128)(2,1)S(1)}, bf16[512,128]{1,0:T(8,128)(2,1)S(1)}, u32[]{:S(2)}, u32[]{:S(2)}) %collective-permute-start) | collective-permute-done | bytes 131104 | tf_op jit(solution)/shard_map/ppermute | solution.py:468
  25.1 4.0 %collective-permute-done.1.c2 = bf16[512,128]{1,0:T(8,128)(2,1)S(1)} collective-permute-done((bf16[512,128]{1,0:T(8,128)(2,1)S(1)}, bf16[512,128]{1,0:T(8,128)(2,1)S(1)}, u32[]{:S(2)}, u32[]{:S(2)}) %collective-permute-start.1) | collective-permute-done | bytes 131104 | tf_op jit(solution)/shard_map/ppermute | solution.py:468
  29.1 0.0 collective-permute-done.2.c3
  29.1 0.0 all-to-all-done.told
  29.1 3.6 %reply_stage.1 = (bf16[64,128,128]{2,1,0:T(8,128)(2,1)}, bf16[256,128]{1,0:T(8,128)(2,1)}, bf16[256,128]{1,0:T(8,128)(2,1)}, bf16[256,128]{1,0:T(8,128)(2,1)}, b...) custom-call(s32[1]{0:T(128)} %bitcast.z, bf16[32,48,128]{2,1,0:T(8,128)(2,1)S(1)} %all-to-all-done.told, ...), custom_call_target="tpu_custom_call" | custom-call | tf_op jit(solution)/shard_map/reply_stage/pallas_call | solution.py:258
  32.7 0.0 copy-start.10
  32.7 0.0 copy-start.17
  32.8 7.4 %all-to-all-start.1 = ((bf16[32,256,128]{2,1,0:T(8,128)(2,1)}), bf16[32,256,128]{2,1,0:T(8,128)(2,1)S(1)}, u32[]{:S(2)}, u32[]{:S(2)}) async-start(bf16[32,256,128]{2,1,0:T(8,128)(2,1)} %bitcast.9), calls=%async_computation.1 | async-start | bytes 4194304 | tf_op jit(solution)/shard_map/all_to_all | solution.py:479
  40.1 1.3 %collective-permute-start.8 = (bf16[512,256]{1,0:T(8,128)(2,1)}, bf16[512,256]{1,0:T(8,128)(2,1)S(1)}, u32[]{:S(2)}, u32[]{:S(2)}) collective-permute-start(bf16[512,256]{1,0:T(8,128)(2,1)} %get-tuple-element.36), channel_id=1, source_target_pairs={{0,1},{1,2},{2,3},{3,0},{4,5},{5,6},{6,7},{7,4},{8,9},{9,10},{10,1... | collective-permute-start | bytes 786440 | tf_op jit(solution)/shard_map/ppermute | solution.py:468
  41.4 1.0 collective-permute-start.3
  42.4 2.5 %collective-permute-start.4 = (bf16[256,128]{1,0:T(8,128)(2,1)}, bf16[256,128]{1,0:T(8,128)(2,1)S(1)}, u32[]{:S(2)}, u32[]{:S(2)}) collective-permute-start(bf16[256,128]{1,0:T(8,128)(2,1)} %get-tuple-element.31), channel_id=1, source_target_pairs={{0,2},{1,3},{2,0},{3,1},{4,6},{5,7},{6,4},{7,5},{8,10},{9,11},{10,... | collective-permute-start | bytes 196616 | tf_op jit(solution)/shard_map/ppermute | solution.py:468
  44.9 0.0 copy-done.20
  44.9 1.6 %collective-permute-start.5 = (bf16[256,128]{1,0:T(8,128)(2,1)S(1)}, bf16[256,128]{1,0:T(8,128)(2,1)S(1)}, u32[]{:S(2)}, u32[]{:S(2)}) collective-permute-start(bf16[256,128]{1,0:T(8,128)(2,1)S(1)} %copy-done.20), channel_id=1, source_target_pairs={{0,3},{1,0},{2,1},{3,2},{4,7},{5,4},{6,5},{7,6},{8,11},{9,8},{10,9... | collective-permute-start | bytes 196616 | tf_op jit(solution)/shard_map/ppermute | solution.py:468
  46.5 0.0 collective-permute-start.7
  46.5 5.3 %collective-permute-done.3.s1 = bf16[256,128]{1,0:T(8,128)(2,1)S(1)} collective-permute-done((bf16[256,128]{1,0:T(8,128)(2,1)S(1)}, bf16[256,128]{1,0:T(8,128)(2,1)S(1)}, u32[]{:S(2)}, u32[]{:S(2)}) %collective-permute-start.3) | collective-permute-done | bytes 65568 | tf_op jit(solution)/shard_map/ppermute | solution.py:468
  51.8 0.9 collective-permute-start.6
  52.7 0.6 collective-permute-done.4.s2
  53.3 0.0 collective-permute-done.5.s3
  53.3 0.0 copy-done.4
  53.3 1.0 copy-done.15
  54.4 5.0 %near_stage.4.rest_0_.state = f32[2,4,256,128]{3,2,1,0:T(8,128)} custom-call(s32[1]{0:T(128)} %bitcast.z, f32[16]{0:T(128)S(1)} %copy-done.10, bf16[512,256]{1,0:T(8,128)(2,1)S(1)} %copy-done.4, bf16[4,4,128,128]{3,2,1,0:T(8,128)(2,1)S(1)} %copy-done.15, bf16[256,128]{1,0:T(8,128)(2,1)S(1)} %copy-done.17, bf16[256,128]{1,0:T(8,128)(2,1)S(1)} %collective-permute-done.3.s1, ...), custom_call_target="tpu_custom_call" | custom-call | flops 1342177280 | bytes 2097152 | tf_op jit(solution)/shard_map/near_stage/pallas_call | solution.py:332
  59.3 0.0 collective-permute-done.8.q
  59.4 5.0 %near_stage.5.rest_0_.state = f32[2,4,256,128]{3,2,1,0:T(8,128)} custom-call(s32[1]{0:T(128)} %bitcast.z, f32[16]{0:T(128)S(1)} %copy-done.10, bf16[512,256]{1,0:T(8,128)(2,1)S(1)} %collective-permute-done.8.q, bf16[4,4,128,128]{3,2,1,0:T(8,128)(2,1)S(1)} %copy-done.16, bf16[256,128]{1,0:T(8,128)(2,1)S(1)} %copy-done.17, ...), custom_call_target="tpu_custom_call" | custom-call | flops 1342177280 | bytes 2097152 | tf_op jit(solution)/shard_map/near_stage/pallas_call | solution.py:332
  64.3 0.0 collective-permute-done.7.q
  64.4 5.0 %near_stage.6.rest_0_.state = f32[2,4,256,128]{3,2,1,0:T(8,128)} custom-call(s32[1]{0:T(128)} %bitcast.z, f32[16]{0:T(128)S(1)} %copy-done.10, bf16[512,256]{1,0:T(8,128)(2,1)S(1)} %collective-permute-done.7.q, bf16[4,4,128,128]{3,2,1,0:T(8,128)(2,1)S(1)} %copy-done.16, bf16[256,128]{1,0:T(8,128)(2,1)S(1)} %copy-done.17, ...), custom_call_target="tpu_custom_call" | custom-call | flops 1342177280 | bytes 2097152 | tf_op jit(solution)/shard_map/near_stage/pallas_call | solution.py:332
  69.3 0.0 collective-permute-done.6.q
  69.4 4.9 %near_stage.7.rest_0_.state = f32[2,4,256,128]{3,2,1,0:T(8,128)} custom-call(s32[1]{0:T(128)} %bitcast.z, f32[16]{0:T(128)S(1)} %copy-done.10, bf16[512,256]{1,0:T(8,128)(2,1)S(1)} %collective-permute-done.6.q, bf16[4,4,128,128]{3,2,1,0:T(8,128)(2,1)S(1)} %copy-done.16, bf16[256,128]{1,0:T(8,128)(2,1)S(1)} %copy-done.17, ...), custom_call_target="tpu_custom_call" | custom-call | flops 1342177280 | bytes 2097152 | tf_op jit(solution)/shard_map/near_stage/pallas_call | solution.py:332
  74.3 0.0 all-to-all-done.1
  74.3 1.2 %copy-done = f32[2,4,256,128]{3,2,1,0:T(8,128)S(1)} copy-done((f32[2,4,256,128]{3,2,1,0:T(8,128)S(1)}, f32[2,4,256,128]{3,2,1,0:T(8,128)}, u32[]{:S(2)}) %copy-start) | copy-done | bytes 1048600
  75.6 3.8 %far_stage.6 = bf16[512,256]{1,0:T(8,128)(2,1)S(1)} custom-call(s32[1]{0:T(128)} %bitcast.z, s32[16,4]{1,0:T(8,128)S(1)} %get-tuple-element.21.slots, f32[16]{0:T(128)S(1)} %copy-done.10, bf16[512,256]{1,0:T(8,128)(2,1)S(1)} %collective-permute-done.6.q, f32[2,4,256,128]{3,2,1,0:T(8,128)S(1)} %copy-done, bf16[64,128,128]{2,1,0:T(8,128)(2,1)S(1)} %bitcast.4), custom_call_target="tpu_custom_call" | custom-call | flops 536870912 | bytes 4194304 | tf_op jit(solution)/shard_map/far_stage/pallas_call | solution.py:414
  79.4 2.1 %collective-permute-start.10 = (bf16[512,256]{1,0:T(8,128)(2,1)S(1)}, bf16[512,256]{1,0:T(8,128)(2,1)S(1)}, u32[]{:S(2)}, u32[]{:S(2)}) collective-permute-start(bf16[512,256]{1,0:T(8,128)(2,1)S(1)} %far_stage.6), channel_id=1, source_target_pairs={{0,2},{1,3},{2,0},{3,1},{4,6},{5,7},{6,4},{7,5},{8,10},{9,11},{10,... | collective-permute-start | bytes 786440 | tf_op jit(solution)/shard_map/ppermute | solution.py:468
  81.5 3.8 %far_stage.5 = bf16[512,256]{1,0:T(8,128)(2,1)S(1)} custom-call(s32[1]{0:T(128)} %bitcast.z, s32[16,4]{1,0:T(8,128)S(1)} %get-tuple-element.21.slots, f32[16]{0:T(128)S(1)} %copy-done.10, bf16[512,256]{1,0:T(8,128)(2,1)S(1)} %copy-done.7, f32[2,4,256,128]{3,2,1,0:T(8,128)S(1)} %copy-done.3, bf16[64,128,128]{2,1,0:T(8,128)(2,1)S(1)} %bitcast.5, ...), custom_call_target="tpu_custom_call" | custom-call | flops 536870912 | bytes 4194304 | tf_op jit(solution)/shard_map/far_stage/pallas_call | solution.py:414
  85.4 0.0 copy-start.1
  85.4 1.6 %collective-permute-start.9 = (bf16[512,256]{1,0:T(8,128)(2,1)S(1)}, bf16[512,256]{1,0:T(8,128)(2,1)S(1)}, u32[]{:S(2)}, u32[]{:S(2)}) collective-permute-start(bf16[512,256]{1,0:T(8,128)(2,1)S(1)} %far_stage.5), channel_id=1, source_target_pairs={{0,3},{1,0},{2,1},{3,2},{4,7},{5,4},{6,5},{7,6},{8,11},{9,8},{10,9... | collective-permute-start | bytes 786440 | tf_op jit(solution)/shard_map/ppermute | solution.py:468
  87.0 3.8 %far_stage.7 = bf16[512,256]{1,0:T(8,128)(2,1)S(1)} custom-call(s32[1]{0:T(128)} %bitcast.z, s32[16,4]{1,0:T(8,128)S(1)} %get-tuple-element.21.slots, f32[16]{0:T(128)S(1)} %copy-done.10, bf16[512,256]{1,0:T(8,128)(2,1)S(1)} %copy-done.9, f32[2,4,256,128]{3,2,1,0:T(8,128)S(1)} %copy-done.2, bf16[64,128,128]{2,1,0:T(8,128)(2,1)S(1)} %bitcast.6, ...), custom_call_target="tpu_custom_call" | custom-call | flops 536870912 | bytes 4194304 | tf_op jit(solution)/shard_map/far_stage/pallas_call | solution.py:414
  90.9 0.0 copy-start.11
  90.9 0.8 collective-permute-start.11
  91.7 3.8 %far_stage.4.a0 = bf16[512,256]{1,0:T(8,128)(2,1)S(1)} custom-call(s32[1]{0:T(128)} %bitcast.z, s32[16,4]{1,0:T(8,128)S(1)} %get-tuple-element.21.slots, f32[16]{0:T(128)S(1)} %copy-done.10, bf16[512,256]{1,0:T(8,128)(2,1)S(1)} %copy-done.5, f32[2,4,256,128]{3,2,1,0:T(8,128)S(1)} %copy-done.1, bf16[64,128,128]{2,1,0:T(8,128)(2,1)S(1)} %bitcast.7, ...), custom_call_target="tpu_custom_call" | custom-call | flops 536870912 | bytes 4194304 | tf_op jit(solution)/shard_map/far_stage/pallas_call | solution.py:414
  95.5 0.0 collective-permute-done.10.a2
  95.5 0.0 collective-permute-done.9.a1
  95.5 3.0 %collective-permute-done.11.a3 = bf16[512,256]{1,0:T(8,128)(2,1)S(1)} collective-permute-done((bf16[512,256]{1,0:T(8,128)(2,1)S(1)}, bf16[512,256]{1,0:T(8,128)(2,1)S(1)}, u32[]{:S(2)}, u32[]{:S(2)}) %collective-permute-start.11) | collective-permute-done | bytes 262176 | tf_op jit(solution)/shard_map/ppermute | solution.py:468
  98.5 11.0 %ffn_stage.1 = bf16[512,1024]{1,0:T(8,128)(2,1)} custom-call(s32[1]{0:T(128)} %bitcast.z, bf16[512,1024]{1,0:T(8,128)(2,1)S(1)} %copy-done.14, bf16[512,256]{1,0:T(8,128)(2,1)S(1)} %far_stage.4.a0, bf16[512,256]{1,0:T(8,128)(2,1)S(1)} %collective-permute-done.9.a1, bf16[512,256]{1,0:T(8,128)(2,1)S(1)} %collective-permute-done.10.a2, ...), custom_call_target="tpu_custom_call" | custom-call | flops 7516192768 | bytes 18874368 | tf_op jit(solution)/shard_map/ffn_stage/pallas_call | solution.py:449
  (35 shorter events, 0.1 us)
Async XLA Ops:
  0.0 0.7 copy-start.18
  9.6 19.5 %all-to-all-start = ((bf16[32,48,128]{2,1,0:T(8,128)(2,1)}), bf16[32,48,128]{2,1,0:T(8,128)(2,1)S(1)}, u32[]{:S(2)}, u32[]{:S(2)}) async-start(bf16[32,48,128]{2,1,0:T(8,128)(2,1)} %get-tuple-element.23), calls=%async_computation | async-start | bytes 786432 | tf_op jit(solution)/shard_map/all_to_all | solution.py:476
  17.1 8.0 %collective-permute-start = (bf16[512,128]{1,0:T(8,128)(2,1)S(1)}, bf16[512,128]{1,0:T(8,128)(2,1)S(1)}, u32[]{:S(2)}, u32[]{:S(2)}) collective-permute-start(bf16[512,128]{1,0:T(8,128)(2,1)S(1)} %get-tuple-element.25), channel_id=1, source_target_pairs={{0,1},{1,2},{2,3},{3,0},{4,5},{5,6},{6,7},{7,4},{8,9},{9,10},{10,1... | collective-permute-start | bytes 393224 | tf_op jit(solution)/shard_map/ppermute | solution.py:468
  19.0 10.0 %collective-permute-start.1 = (bf16[512,128]{1,0:T(8,128)(2,1)S(1)}, bf16[512,128]{1,0:T(8,128)(2,1)S(1)}, u32[]{:S(2)}, u32[]{:S(2)}) collective-permute-start(bf16[512,128]{1,0:T(8,128)(2,1)S(1)} %get-tuple-element.26), channel_id=1, source_target_pairs={{0,2},{1,3},{2,0},{3,1},{4,6},{5,7},{6,4},{7,5},{8,10},{9,11},{10,... | collective-permute-start | bytes 393224 | tf_op jit(solution)/shard_map/ppermute | solution.py:468
  22.6 6.5 %collective-permute-start.2 = (bf16[512,128]{1,0:T(8,128)(2,1)S(1)}, bf16[512,128]{1,0:T(8,128)(2,1)S(1)}, u32[]{:S(2)}, u32[]{:S(2)}) collective-permute-start(bf16[512,128]{1,0:T(8,128)(2,1)S(1)} %get-tuple-element.27), channel_id=1, source_target_pairs={{0,3},{1,0},{2,1},{3,2},{4,7},{5,4},{6,5},{7,6},{8,11},{9,8},{10,9... | collective-permute-start | bytes 393224 | tf_op jit(solution)/shard_map/ppermute | solution.py:468
  32.7 8.7 %copy-start.21 = (bf16[256,128]{1,0:T(8,128)(2,1)S(1)}, bf16[256,128]{1,0:T(8,128)(2,1)}, u32[]{:S(2)}) copy-start(bf16[256,128]{1,0:T(8,128)(2,1)} %get-tuple-element.30) | copy-start | bytes 196612
  32.7 12.2 %copy-start.20 = (bf16[256,128]{1,0:T(8,128)(2,1)S(1)}, bf16[256,128]{1,0:T(8,128)(2,1)}, u32[]{:S(2)}) copy-start(bf16[256,128]{1,0:T(8,128)(2,1)} %get-tuple-element.32) | copy-start | bytes 196612
  32.7 19.1 %copy-start.19 = (bf16[512,256]{1,0:T(8,128)(2,1)S(1)}, bf16[512,256]{1,0:T(8,128)(2,1)}, u32[]{:S(2)}) copy-start(bf16[512,256]{1,0:T(8,128)(2,1)} %get-tuple-element.34) | copy-start | bytes 786436
  32.7 20.6 %copy-start.4 = (bf16[512,256]{1,0:T(8,128)(2,1)S(1)}, bf16[512,256]{1,0:T(8,128)(2,1)}, u32[]{:S(2)}) copy-start(bf16[512,256]{1,0:T(8,128)(2,1)} %get-tuple-element.22.q) | copy-start | bytes 786436
  32.7 20.6 %copy-start.10 = (f32[16]{0:T(128)S(1)}, f32[16]{0:T(128)}, u32[]{:S(2)}) copy-start(f32[16]{0:T(128)} %scale.15) | copy-start | bytes 196
  32.7 20.6 %copy-start.17 = (bf16[256,128]{1,0:T(8,128)(2,1)S(1)}, bf16[256,128]{1,0:T(8,128)(2,1)}, u32[]{:S(2)}) copy-start(bf16[256,128]{1,0:T(8,128)(2,1)} %get-tuple-element.29.s0) | copy-start | bytes 196612
  32.8 41.6 %all-to-all-start.1 = ((bf16[32,256,128]{2,1,0:T(8,128)(2,1)}), bf16[32,256,128]{2,1,0:T(8,128)(2,1)S(1)}, u32[]{:S(2)}, u32[]{:S(2)}) async-start(bf16[32,256,128]{2,1,0:T(8,128)(2,1)} %bitcast.9), calls=%async_computation.1 | async-start | bytes 4194304 | tf_op jit(solution)/shard_map/all_to_all | solution.py:479
  40.1 19.2 %collective-permute-start.8 = (bf16[512,256]{1,0:T(8,128)(2,1)}, bf16[512,256]{1,0:T(8,128)(2,1)S(1)}, u32[]{:S(2)}, u32[]{:S(2)}) collective-permute-start(bf16[512,256]{1,0:T(8,128)(2,1)} %get-tuple-element.36), channel_id=1, source_target_pairs={{0,1},{1,2},{2,3},{3,0},{4,5},{5,6},{6,7},{7,4},{8,9},{9,10},{10,1... | collective-permute-start | bytes 786440 | tf_op jit(solution)/shard_map/ppermute | solution.py:468
  41.4 10.4 %collective-permute-start.3 = (bf16[256,128]{1,0:T(8,128)(2,1)S(1)}, bf16[256,128]{1,0:T(8,128)(2,1)S(1)}, u32[]{:S(2)}, u32[]{:S(2)}) collective-permute-start(bf16[256,128]{1,0:T(8,128)(2,1)S(1)} %copy-done.21), channel_id=1, source_target_pairs={{0,1},{1,2},{2,3},{3,0},{4,5},{5,6},{6,7},{7,4},{8,9},{9,10},{10,1... | collective-permute-start | bytes 196616 | tf_op jit(solution)/shard_map/ppermute | solution.py:468
  42.4 10.9 %collective-permute-start.4 = (bf16[256,128]{1,0:T(8,128)(2,1)}, bf16[256,128]{1,0:T(8,128)(2,1)S(1)}, u32[]{:S(2)}, u32[]{:S(2)}) collective-permute-start(bf16[256,128]{1,0:T(8,128)(2,1)} %get-tuple-element.31), channel_id=1, source_target_pairs={{0,2},{1,3},{2,0},{3,1},{4,6},{5,7},{6,4},{7,5},{8,10},{9,11},{10,... | collective-permute-start | bytes 196616 | tf_op jit(solution)/shard_map/ppermute | solution.py:468
  44.9 8.4 %collective-permute-start.5 = (bf16[256,128]{1,0:T(8,128)(2,1)S(1)}, bf16[256,128]{1,0:T(8,128)(2,1)S(1)}, u32[]{:S(2)}, u32[]{:S(2)}) collective-permute-start(bf16[256,128]{1,0:T(8,128)(2,1)S(1)} %copy-done.20), channel_id=1, source_target_pairs={{0,3},{1,0},{2,1},{3,2},{4,7},{5,4},{6,5},{7,6},{8,11},{9,8},{10,9... | collective-permute-start | bytes 196616 | tf_op jit(solution)/shard_map/ppermute | solution.py:468
  46.5 17.9 %collective-permute-start.7 = (bf16[512,256]{1,0:T(8,128)(2,1)}, bf16[512,256]{1,0:T(8,128)(2,1)S(1)}, u32[]{:S(2)}, u32[]{:S(2)}) collective-permute-start(bf16[512,256]{1,0:T(8,128)(2,1)} %get-tuple-element.35), channel_id=1, source_target_pairs={{0,3},{1,0},{2,1},{3,2},{4,7},{5,4},{6,5},{7,6},{8,11},{9,8},{10,9... | collective-permute-start | bytes 786440 | tf_op jit(solution)/shard_map/ppermute | solution.py:468
  51.8 17.5 %collective-permute-start.6 = (bf16[512,256]{1,0:T(8,128)(2,1)S(1)}, bf16[512,256]{1,0:T(8,128)(2,1)S(1)}, u32[]{:S(2)}, u32[]{:S(2)}) collective-permute-start(bf16[512,256]{1,0:T(8,128)(2,1)S(1)} %copy-done.19), channel_id=1, source_target_pairs={{0,2},{1,3},{2,0},{3,1},{4,6},{5,7},{6,4},{7,5},{8,10},{9,11},{10,... | collective-permute-start | bytes 786440 | tf_op jit(solution)/shard_map/ppermute | solution.py:468
  53.3 1.0 copy-start.15
  54.4 5.0 %copy-start.16 = (bf16[4,4,128,128]{3,2,1,0:T(8,128)(2,1)S(1)}, bf16[4,4,128,128]{3,2,1,0:T(8,128)(2,1)}, u32[]{:S(2)}) copy-start(bf16[4,4,128,128]{3,2,1,0:T(8,128)(2,1)} %get-tuple-element.28.kv) | copy-start | bytes 1572868
  59.4 5.0 %copy-start.6 = (bf16[512,256]{1,0:T(8,128)(2,1)}, bf16[512,256]{1,0:T(8,128)(2,1)S(1)}, u32[]{:S(2)}) copy-start(bf16[512,256]{1,0:T(8,128)(2,1)S(1)} %collective-permute-done.8.q) | copy-start | bytes 786436
  64.4 5.0 %copy-start.8 = (bf16[512,256]{1,0:T(8,128)(2,1)}, bf16[512,256]{1,0:T(8,128)(2,1)S(1)}, u32[]{:S(2)}) copy-start(bf16[512,256]{1,0:T(8,128)(2,1)S(1)} %collective-permute-done.7.q) | copy-start | bytes 786436
  69.4 12.2 %copy-start.3 = (f32[2,4,256,128]{3,2,1,0:T(8,128)S(1)}, f32[2,4,256,128]{3,2,1,0:T(8,128)}, u32[]{:S(2)}) copy-start(f32[2,4,256,128]{3,2,1,0:T(8,128)} %near_stage.5.rest_0_.state) | copy-start | bytes 3145732
  74.3 1.2 %copy-start = (f32[2,4,256,128]{3,2,1,0:T(8,128)S(1)}, f32[2,4,256,128]{3,2,1,0:T(8,128)}, u32[]{:S(2)}) copy-start(f32[2,4,256,128]{3,2,1,0:T(8,128)} %near_stage.7.rest_0_.state) | copy-start | bytes 3145732
  75.6 6.0 %copy-start.7 = (bf16[512,256]{1,0:T(8,128)(2,1)S(1)}, bf16[512,256]{1,0:T(8,128)(2,1)}, u32[]{:S(2)}) copy-start(bf16[512,256]{1,0:T(8,128)(2,1)} %copy-done.6) | copy-start | bytes 786436
  79.4 7.6 %copy-start.2 = (f32[2,4,256,128]{3,2,1,0:T(8,128)S(1)}, f32[2,4,256,128]{3,2,1,0:T(8,128)}, u32[]{:S(2)}) copy-start(f32[2,4,256,128]{3,2,1,0:T(8,128)} %near_stage.6.rest_0_.state) | copy-start | bytes 3145732
  79.4 7.6 %copy-start.9 = (bf16[512,256]{1,0:T(8,128)(2,1)S(1)}, bf16[512,256]{1,0:T(8,128)(2,1)}, u32[]{:S(2)}) copy-start(bf16[512,256]{1,0:T(8,128)(2,1)} %copy-done.8) | copy-start | bytes 786436
  79.4 16.1 %collective-permute-start.10 = (bf16[512,256]{1,0:T(8,128)(2,1)S(1)}, bf16[512,256]{1,0:T(8,128)(2,1)S(1)}, u32[]{:S(2)}, u32[]{:S(2)}) collective-permute-start(bf16[512,256]{1,0:T(8,128)(2,1)S(1)} %far_stage.6), channel_id=1, source_target_pairs={{0,2},{1,3},{2,0},{3,1},{4,6},{5,7},{6,4},{7,5},{8,10},{9,11},{10,... | collective-permute-start | bytes 786440 | tf_op jit(solution)/shard_map/ppermute | solution.py:468
  81.5 17.0 %copy-start.12 = (bf16[1024,2048]{1,0:T(8,128)(2,1)S(1)}, bf16[1024,2048]{1,0:T(8,128)(2,1)}, u32[]{:S(2)}) copy-start(bf16[1024,2048]{1,0:T(8,128)(2,1)} %w_up.1) | copy-start | bytes 12582916
  85.4 6.3 %copy-start.1 = (f32[2,4,256,128]{3,2,1,0:T(8,128)S(1)}, f32[2,4,256,128]{3,2,1,0:T(8,128)}, u32[]{:S(2)}) copy-start(f32[2,4,256,128]{3,2,1,0:T(8,128)} %near_stage.4.rest_0_.state) | copy-start | bytes 3145732
  85.4 6.3 %copy-start.5 = (bf16[512,256]{1,0:T(8,128)(2,1)S(1)}, bf16[512,256]{1,0:T(8,128)(2,1)}, u32[]{:S(2)}) copy-start(bf16[512,256]{1,0:T(8,128)(2,1)} %get-tuple-element.22.q) | copy-start | bytes 786436
  85.4 10.1 %collective-permute-start.9 = (bf16[512,256]{1,0:T(8,128)(2,1)S(1)}, bf16[512,256]{1,0:T(8,128)(2,1)S(1)}, u32[]{:S(2)}, u32[]{:S(2)}) collective-permute-start(bf16[512,256]{1,0:T(8,128)(2,1)S(1)} %far_stage.5), channel_id=1, source_target_pairs={{0,3},{1,0},{2,1},{3,2},{4,7},{5,4},{6,5},{7,6},{8,11},{9,8},{10,9... | collective-permute-start | bytes 786440 | tf_op jit(solution)/shard_map/ppermute | solution.py:468
  87.0 11.5 %copy-start.13 = (bf16[1024,1024]{1,0:T(8,128)(2,1)S(1)}, bf16[1024,1024]{1,0:T(8,128)(2,1)}, u32[]{:S(2)}) copy-start(bf16[1024,1024]{1,0:T(8,128)(2,1)} %w_out.1) | copy-start | bytes 6291460
  87.0 11.5 %copy-start.14 = (bf16[512,1024]{1,0:T(8,128)(2,1)S(1)}, bf16[512,1024]{1,0:T(8,128)(2,1)}, u32[]{:S(2)}) copy-start(bf16[512,1024]{1,0:T(8,128)(2,1)} %tokens.1) | copy-start | bytes 3145732
  90.9 7.7 %copy-start.11 = (bf16[1024,2048]{1,0:T(8,128)(2,1)S(1)}, bf16[1024,2048]{1,0:T(8,128)(2,1)}, u32[]{:S(2)}) copy-start(bf16[1024,2048]{1,0:T(8,128)(2,1)} %w_gate.1) | copy-start | bytes 12582916
  90.9 7.7 %collective-permute-start.11 = (bf16[512,256]{1,0:T(8,128)(2,1)S(1)}, bf16[512,256]{1,0:T(8,128)(2,1)S(1)}, u32[]{:S(2)}, u32[]{:S(2)}) collective-permute-start(bf16[512,256]{1,0:T(8,128)(2,1)S(1)} %far_stage.7), channel_id=1, source_target_pairs={{0,1},{1,2},{2,3},{3,0},{4,5},{5,6},{6,7},{7,4},{8,9},{9,10},{10,1... | collective-permute-start | bytes 786440 | tf_op jit(solution)/shard_map/ppermute | solution.py:468

commit v2 on v1

--- a/solution.py
+++ b/solution.py
@@ -85,21 +85,20 @@
 
 
 def first_body(
-    z, picks, tokens_in, key_in, value_in, query_in,
-    c0, c1, c2, c3, q0, q1, q2, q3, payload_out, slots,
-    table, tokens, w_key, w_value, w_query, normed, pairs, queries, payload, sems, out_sems,
+    z, picks, tokens_in, key_in, value_in,
+    c0, c1, c2, c3, payload_out, normed_out, slots,
+    table, tokens, w_key, w_value, normed, pairs, payload, sems, out_sems,
 ):
     rows_n = ROWS // STEPS
     weight_copies = [
         pltpu.make_async_copy(key_in, w_key, sems.at[0]),
         pltpu.make_async_copy(value_in, w_value, sems.at[1]),
-        pltpu.make_async_copy(query_in, w_query, sems.at[2]),
     ]
     token_copies = [
         pltpu.make_async_copy(
             tokens_in.at[pl.ds(i * rows_n, rows_n)],
             tokens.at[pl.ds(i * rows_n, rows_n)],
-            sems.at[3 + i],
+            sems.at[2 + i],
         )
         for i in range(STEPS)
     ]
@@ -108,7 +107,6 @@
     weight_copies[1].start()
     for c in token_copies[1:]:
         c.start()
-    weight_copies[2].start()
 
     def clear(i, _):
         table[i] = -1
@@ -131,12 +129,16 @@
     lax.fori_loop(0, BLK_DEV * PICKS, assign, 0, unroll=4)
 
     ones = head_ones(GROUP_W)
-    key_means, value_means = [], []
+    key_means, value_means, outs = [], [], []
     for i in range(STEPS):
-        rows = slice(i * rows_n, (i + 1) * rows_n)
+        rows = pl.ds(i * rows_n, rows_n)
         token_copies[i].wait()
         here = row_norm(tokens[rows].astype(f32)).astype(bf16)
         normed[rows] = here
+        outs.append(
+            pltpu.make_async_copy(normed.at[rows], normed_out.at[rows], out_sems.at[i])
+        )
+        outs[-1].start()
         if i == 0:
             weight_copies[0].wait()
         keys = jnp.dot(here, w_key[...], preferred_element_type=f32)
@@ -173,12 +175,56 @@
         first = jnp.maximum(table[o * CAP], 0)
         second = jnp.maximum(table[o * CAP + 1], 0)
         payload[o, SUM_ROWS:, :] = jnp.where(lane == 0, first, second).astype(f32).astype(bf16)
-    outs = [pltpu.make_async_copy(payload, payload_out, out_sems.at[ZS])]
-    outs[0].start()
-    weight_copies[2].wait()
+    outs.append(pltpu.make_async_copy(payload, payload_out, out_sems.at[STEPS]))
+    outs[-1].start()
+    for c in outs:
+        c.wait()
+
+
+def first_stage(z, picks, tokens, w_key, w_value):
+    hbm = whole(pltpu.HBM)
+    return pl.pallas_call(
+        first_body,
+        name="first_stage",
+        in_specs=[whole(SMEM), whole(SMEM), hbm, hbm, hbm],
+        out_specs=[whole(VMEM)] * ZS + [hbm] * 2 + [whole(SMEM)],
+        out_shape=[VMEM((ROWS, PAIR_W), bf16)] * ZS
+        + [
+            pltpu.HBM((PTS, PAY_ROWS, PAIR_W), bf16),
+            pltpu.HBM((ROWS, 1024), bf16),
+            jax.ShapeDtypeStruct((BLK_DEV, PICKS), jnp.int32),
+        ],
+        scratch_shapes=[
+            SMEM((PTS * CAP,), jnp.int32),
+            VMEM((ROWS, 1024), bf16),
+            VMEM((1024, GROUP_W), bf16),
+            VMEM((1024, GROUP_W), bf16),
+            VMEM((ROWS, 1024), bf16),
+            VMEM((KV_HEADS, ROWS, PAIR_W), bf16),
+            VMEM((PTS, PAY_ROWS, PAIR_W), bf16),
+            pltpu.SemaphoreType.DMA((2 + STEPS,)),
+            pltpu.SemaphoreType.DMA((STEPS + 1,)),
+        ],
+        compiler_params=params(16),
+        cost_estimate=cost(2 * ROWS * 1024 * 512, 4 << 20),
+    )(z, picks, *[far_core(a) for a in (tokens, w_key, w_value)])
+
+
+def q_body(z, normed_in, query_in, q0, q1, q2, q3, normed, w_query, queries, sems, out_sems):
+    def columns(k):
+        return pl.ds(pl.multiple_of(((z[0] + k) % ZS) * GROUP_W, GROUP_W), GROUP_W)
+
+    ins = [pltpu.make_async_copy(normed_in, normed, sems.at[ZS])]
+    for k in range(ZS):
+        ins.append(pltpu.make_async_copy(query_in.at[:, columns(k)], w_query.at[k], sems.at[k]))
+    for c in ins:
+        c.start()
+    ones = head_ones(GROUP_W)
+    ins[0].wait()
+    outs = []
     for k, out in enumerate((q0, q1, q2, q3)):
-        start = pl.multiple_of(((z[0] + k) % ZS) * GROUP_W, GROUP_W)
-        raw = jnp.dot(normed[...], w_query[:, pl.ds(start, GROUP_W)], preferred_element_type=f32)
+        ins[k + 1].wait()
+        raw = jnp.dot(normed[...], w_query[k], preferred_element_type=f32)
         queries[k] = head_norm(raw, ones).astype(bf16)
         outs.append(pltpu.make_async_copy(queries.at[k], out, out_sems.at[k]))
         outs[-1].start()
@@ -186,35 +232,24 @@
         c.wait()
 
 
-def first_stage(z, picks, tokens, w_key, w_value, w_query):
+def q_stage(z, normed, w_query):
     hbm = whole(pltpu.HBM)
     return pl.pallas_call(
-        first_body,
-        name="first_stage",
-        in_specs=[whole(SMEM), whole(SMEM), hbm, hbm, hbm, hbm],
-        out_specs=[whole(VMEM)] * ZS + [hbm] * (ZS + 1) + [whole(SMEM)],
-        out_shape=[VMEM((ROWS, PAIR_W), bf16)] * ZS
-        + [pltpu.HBM((ROWS, GROUP_W), bf16)] * ZS
-        + [
-            pltpu.HBM((PTS, PAY_ROWS, PAIR_W), bf16),
-            jax.ShapeDtypeStruct((BLK_DEV, PICKS), jnp.int32),
-        ],
+        q_body,
+        name="q_stage",
+        in_specs=[whole(SMEM), hbm, hbm],
+        out_specs=[hbm] * ZS,
+        out_shape=[pltpu.HBM((ROWS, GROUP_W), bf16)] * ZS,
         scratch_shapes=[
-            SMEM((PTS * CAP,), jnp.int32),
             VMEM((ROWS, 1024), bf16),
-            VMEM((1024, GROUP_W), bf16),
-            VMEM((1024, GROUP_W), bf16),
-            VMEM((1024, 1024), bf16),
-            VMEM((ROWS, 1024), bf16),
-            VMEM((KV_HEADS, ROWS, PAIR_W), bf16),
+            VMEM((ZS, 1024, GROUP_W), bf16),
             VMEM((ZS, ROWS, GROUP_W), bf16),
-            VMEM((PTS, PAY_ROWS, PAIR_W), bf16),
-            pltpu.SemaphoreType.DMA((3 + STEPS,)),
             pltpu.SemaphoreType.DMA((ZS + 1,)),
-        ],
-        compiler_params=params(24),
-        cost_estimate=cost(2 * ROWS * 1024 * 1536, 8 << 20),
-    )(z, picks, *[far_core(a) for a in (tokens, w_key, w_value, w_query)])
+            pltpu.SemaphoreType.DMA((ZS,)),
+        ],
+        compiler_params=params(16),
+        cost_estimate=cost(2 * ROWS * 1024 * 1024, 4 << 20),
+    )(z, far_core(normed), far_core(w_query))
 
 
 def reply_body(
@@ -280,8 +315,7 @@
 
 
 def near_body(chunk, z, scale, q, kv, s0, s1, s2, s3, *rest):
-    state_out, held, state, sems = rest[-4:]
-    lane = lax.broadcasted_iota(jnp.int32, (BALL, PAIR_W), 1)
+    state_out, peak_out, held, state, peaks, sems, peak_sems = rest[-7:]
     sums = jnp.concatenate([s0[...], s1[...], s2[...], s3[...]], axis=0)
     sum_keys = sums[:, :HEAD_DIM]
     sum_values = ones_beside(sums)
@@ -296,12 +330,16 @@
         far = lax.dot_general(here, sum_keys, NT, preferred_element_type=f32)
         held[r % 2, :, :BALL] = ball
         held[r % 2, :, BALL:] = far
-        return jnp.maximum(
+        peak = jnp.maximum(
             jnp.max(ball, axis=1, keepdims=True), jnp.max(far, axis=1, keepdims=True)
         )
-
-    def copy(b, r):
-        return pltpu.make_async_copy(state.at[b, r], state_out.at[b, r], sems.at[b, r])
+        return peak.astype(bf16).astype(f32)
+
+    def copies(b, r):
+        return (
+            pltpu.make_async_copy(state.at[b, r], state_out.at[b, r], sems.at[b, r]),
+            pltpu.make_async_copy(peaks.at[b, r], peak_out.at[b, r], peak_sems.at[b, r]),
+        )
 
     def one_ball(b, peak):
         ball = ball_of(b)
@@ -314,18 +352,20 @@
                 coming = scores(after, 0, ball_of(after)[:, :HEAD_DIM])
             factor = scale[z[0] * RATIO + r] * (LOG2E / math.sqrt(HEAD_DIM))
             w = jnp.exp2((held[r % 2] - peak) * factor).astype(bf16)
-            summed = jnp.dot(w[:, :BALL], values, preferred_element_type=f32) + jnp.dot(
+            peaks[b, r] = jnp.broadcast_to(peak, (BALL, PAIR_W)).astype(bf16)
+            state[b, r] = jnp.dot(w[:, :BALL], values, preferred_element_type=f32) + jnp.dot(
                 w[:, BALL:], sum_values, preferred_element_type=f32
             )
-            state[b, r] = jnp.where(lane < HEAD_DIM // 2, peak, summed)
-            copy(b, r).start()
+            for c in copies(b, r):
+                c.start()
             peak = coming
         return peak
 
     lax.fori_loop(0, BALLS, one_ball, scores(0, 0, ball_of(0)[:, :HEAD_DIM]))
     for b in range(BALLS):
         for r in range(RATIO):
-            copy(b, r).wait()
+            for c in copies(b, r):
+                c.wait()
 
 
 def near_stage(chunk, z, scale, q, kv, sums, others):
@@ -333,11 +373,16 @@
         functools.partial(near_body, chunk),
         name="near_stage",
         in_specs=[whole(SMEM)] * 2 + [whole(VMEM)] * 6 + [whole(pl.ANY)] * len(others),
-        out_specs=whole(pltpu.HBM),
-        out_shape=pltpu.HBM((BALLS, RATIO, BALL, PAIR_W), f32),
+        out_specs=[whole(pltpu.HBM)] * 2,
+        out_shape=[
+            pltpu.HBM((BALLS, RATIO, BALL, PAIR_W), f32),
+            pltpu.HBM((BALLS, RATIO, BALL, PAIR_W), bf16),
+        ],
         scratch_shapes=[
             VMEM((2, BALL, BALL + PTS * SUM_LOCAL * ZS), f32),
             VMEM((BALLS, RATIO, BALL, PAIR_W), f32),
+            VMEM((BALLS, RATIO, BALL, PAIR_W), bf16),
+            pltpu.SemaphoreType.DMA((BALLS, RATIO)),
             pltpu.SemaphoreType.DMA((BALLS, RATIO)),
         ],
         compiler_params=params(12),
@@ -345,7 +390,7 @@
     )(z, scale, near_core(q), near_core(kv), *[near_core(s) for s in sums], *[far_core(a) for a in others])
 
 
-def far_body(shift_by, z, slots, scale, q, state, fetched, *rest):
+def far_body(shift_by, z, slots, scale, q, state, peaks, fetched, *rest):
     out, held = rest[-2:]
     lane = lax.broadcasted_iota(jnp.int32, (BLOCK, PAIR_W), 1)
     first_row = ((z[0] - shift_by + ZS) % ZS) * PER
@@ -370,7 +415,7 @@
         weights, keeps = [], []
         for r in range(RATIO):
             factor = scale[z[0] * RATIO + r] * (LOG2E / math.sqrt(HEAD_DIM))
-            before = jnp.broadcast_to(state[b, r, rows, :1], (BLOCK, PAIR_W))
+            before = peaks[b, r, rows, :].astype(f32)
             new = jnp.maximum(before, peak[part(r)])
             s = held[slot, part(r), :]
             weights.append(
@@ -389,12 +434,7 @@
         for r in range(0, RATIO, 2):
             even = state[b, r, rows, :] * keeps[r] + o[part(r)]
             odd = state[b, r + 1, rows, :] * keeps[r + 1] + o[part(r + 1)]
-            at = HEAD_DIM // 2
-            total = jnp.where(
-                lane < HEAD_DIM,
-                jnp.broadcast_to(even[:, at : at + 1], (BLOCK, PAIR_W)),
-                jnp.broadcast_to(odd[:, at : at + 1], (BLOCK, PAIR_W)),
-            )
+            total = jnp.where(lane < HEAD_DIM, even, pltpu.roll(odd, HEAD_DIM, 1))
             summed = jnp.where(lane < HEAD_DIM, pltpu.roll(even, HEAD_DIM, 1), odd)
             out[pl.ds(i * BLOCK, BLOCK), r * HEAD_DIM : (r + 2) * HEAD_DIM] = (
                 summed / total
@@ -403,24 +443,26 @@
     def one_ball(b, peak):
         coming = scores(2 * b + 1, 1)
         finish(b, 2 * b, 0, peak)
-        after = scores(jnp.minimum(2 * b + 2, PER - 2), 0)
+        after = scores(2 * b + 2, 0) if b + 1 < BALLS else None
         finish(b, 2 * b + 1, 1, coming)
         return after
 
-    lax.fori_loop(0, BALLS, one_ball, scores(0, 0))
+    peak = scores(0, 0)
+    for b in range(BALLS):
+        peak = one_ball(b, peak)
 
 
 def far_stage(shift_by, z, slots, scale, q, state, fetched, others):
     return pl.pallas_call(
         functools.partial(far_body, shift_by),
         name="far_stage",
-        in_specs=[whole(SMEM)] * 3 + [whole(VMEM)] * 3 + [whole(pl.ANY)] * len(others),
+        in_specs=[whole(SMEM)] * 3 + [whole(VMEM)] * 4 + [whole(pl.ANY)] * len(others),
         out_specs=whole(VMEM),
         out_shape=VMEM((ROWS, GROUP_W), bf16),
         scratch_shapes=[VMEM((2, RATIO * BLOCK, PICKS * BLOCK), f32)],
         compiler_params=params(12),
         cost_estimate=cost(8 * 4 * ROWS * 512 * 64, 4 << 20),
-    )(z, slots, scale, near_core(q), near_core(state), near_core(fetched), *[far_core(a) for a in others])
+    )(z, slots, scale, near_core(q), *[near_core(a) for a in state], near_core(fetched), *[far_core(a) for a in others])
 
 
 def ffn_body(
@@ -470,10 +512,10 @@
 
 def body(tokens, w_query, w_key, w_value, w_out, logit_scale, w_gate, w_up, w_down, picks):
     z = lax.axis_index("head").astype(jnp.int32).reshape(1)
-    first = first_stage(z, picks.T, tokens, w_key, w_value, w_query)
-    pairs, query, payload, slots = first[:ZS], first[ZS : 2 * ZS], first[2 * ZS], first[2 * ZS + 1]
+    *pairs, payload, normed, slots = first_stage(z, picks.T, tokens, w_key, w_value)
     chunks = [pairs[0]] + [shift(pairs[k], k) for k in (1, 2, 3)]
     told = lax.all_to_all(payload, "pts", split_axis=0, concat_axis=0, tiled=True)
+    query = q_stage(z, normed, w_query)
     replies, *sums, kv = reply_stage(z, told, chunks)
     replies = replies.reshape(PTS, CAP * BLOCK, PAIR_W)
     fetched = lax.all_to_all(replies, "pts", split_axis=0, concat_axis=0, tiled=True)
@@ -486,10 +528,10 @@
     done = []
     for k in (0, 1, 3, 2):
         states[k] = near_stage(k, z, logit_scale, q[k], kv, sums, done)
-        done = [states[k]]
+        done = states[k]
     parts = [None] * ZS
     for k in (2, 1, 3, 0):
-        others = [states[2]] if k != 2 else []
+        others = states[2] if k != 2 else []
         attended = far_stage(k, z, slots, logit_scale, q[k], states[k], fetched, others)
         parts[k] = shift(attended, ZS - k) if k else attended
     return ffn_stage(z, tokens, parts, w_out, w_gate, w_up, w_down)

time: 110 us -> 110 us (level)
  Pallas kernels: 58.6 us -> 55.9 us
  waiting for transfers between devices: 14.4 us -> 15.9 us
    pallas_call x0 -> x1, Pallas kernels: none -> 6.07 us  [q_stage(): pl.pallas_call(q_body, name='q_stage', in_specs=[whole(SMEM), hbm, hbm],...]
    pallas_call x4, Pallas kernels: 15.3 us -> 9.38 us  [far_stage(): pl.pallas_call(functools.partial(far_body, shift_by), name='far_stage', i...]
    pallas_call x1, Pallas kernels: 8.93 us -> 5.57 us  [first_stage(): pl.pallas_call(first_body, name='first_stage', in_specs=[whole(SMEM), who...]
    ppermute x12, waiting for transfers between devices: 14.4 us -> 15.9 us  [shift(): return lax.ppermute(array, 'head', [(i, (i + k) % ZS) for i in range(ZS)])]
    unnamed x44 -> x42, local copies, waits for them, and re-layouts: 3.02 us -> 3.96 us
  transfers between devices with their start and end apart: 14 -> 14, of which waited for: 5 -> 6; matrix products, arithmetic and copies ran while one was open for 0% -> 0% of each run, Pallas kernels for 29% -> 31%
where the time goes in v2:
time: 110 us; the launch traced here: 109 us
  Pallas kernels  55.9 us (51%)
  starting transfers between devices  33.1 us (30%)
  waiting for transfers between devices  15.9 us (14%)
  local copies, waits for them, and re-layouts  3.96 us (4%)
    pallas_call x4, Pallas kernels, near_stage(): pl.pallas_call(functools.partial(near_body, chunk), name='near_stage', in...  20.2 us
    ppermute x12, starting transfers between devices, shift(): return lax.ppermute(array, 'head', [(i, (i + k) % ZS) for i in range(ZS)])  18.4 us
    ppermute x12, waiting for transfers between devices, shift(): return lax.ppermute(array, 'head', [(i, (i + k) % ZS) for i in range(ZS)])  15.9 us
    pallas_call x1, Pallas kernels, ffn_stage(): pl.pallas_call(ffn_body, name='ffn_stage', in_specs=[whole(SMEM)] + [whol...  11 us
    pallas_call x4, Pallas kernels, far_stage(): pl.pallas_call(functools.partial(far_body, shift_by), name='far_stage', i...  9.38 us
    all_to_all x1, starting transfers between devices, body(): lax.all_to_all(payload, 'pts', split_axis=0, concat_axis=0, tiled=True)  7.44 us
    all_to_all x1, starting transfers between devices, body(): lax.all_to_all(replies, 'pts', split_axis=0, concat_axis=0, tiled=True)  7.24 us
    pallas_call x1, Pallas kernels, q_stage(): pl.pallas_call(q_body, name='q_stage', in_specs=[whole(SMEM), hbm, hbm],...  6.07 us
  transfers between devices with their start and end apart: 14, of which 6 were waited for; matrix products, arithmetic and copies ran while one was open for 0% of the time, Pallas kernels for 31%

profile of v2, /device:TPU:0, one launch (start us, length us, event | category | flops | bytes accessed | tf_op | source)
XLA Modules:
  0.0 109.2 jit_solution(10719987226437599959)
XLA Ops:
  0.0 0.7 copy-done.12
  0.7 5.6 %first_stage.1 = (bf16[512,128]{1,0:T(8,128)(2,1)S(1)}, bf16[512,128]{1,0:T(8,128)(2,1)S(1)}, bf16[512,128]{1,0:T(8,128)(2,1)S(1)}, bf16[512,128]{1,0:T(8,128)(2...) custom-call(s32[1]{0:T(128)} %bitcast.z, s32[4,16]{1,0:T(4,128)S(1)} %bitcast.8, ...), custom_call_target="tpu_custom_call" | custom-call | flops 536870912 | bytes 4194304 | tf_op jit(solution)/shard_map/first_stage/pallas_call | solution.py:186
  6.3 7.4 %all-to-all-start = ((bf16[32,48,128]{2,1,0:T(8,128)(2,1)}), bf16[32,48,128]{2,1,0:T(8,128)(2,1)S(1)}, u32[]{:S(2)}, u32[]{:S(2)}) async-start(bf16[32,48,128]{2,1,0:T(8,128)(2,1)} %get-tuple-element.33), calls=%async_computation | async-start | bytes 786432 | tf_op jit(solution)/shard_map/all_to_all | solution.py:517
  13.7 2.0 %collective-permute-start = (bf16[512,128]{1,0:T(8,128)(2,1)S(1)}, bf16[512,128]{1,0:T(8,128)(2,1)S(1)}, u32[]{:S(2)}, u32[]{:S(2)}) collective-permute-start(bf16[512,128]{1,0:T(8,128)(2,1)S(1)} %get-tuple-element.35), channel_id=1, source_target_pairs={{0,1},{1,2},{2,3},{3,0},{4,5},{5,6},{6,7},{7,4},{8,9},{9,10},{10,1... | collective-permute-start | bytes 393224 | tf_op jit(solution)/shard_map/ppermute | solution.py:510
  15.7 3.6 %collective-permute-start.1 = (bf16[512,128]{1,0:T(8,128)(2,1)S(1)}, bf16[512,128]{1,0:T(8,128)(2,1)S(1)}, u32[]{:S(2)}, u32[]{:S(2)}) collective-permute-start(bf16[512,128]{1,0:T(8,128)(2,1)S(1)} %get-tuple-element.36), channel_id=1, source_target_pairs={{0,2},{1,3},{2,0},{3,1},{4,6},{5,7},{6,4},{7,5},{8,10},{9,11},{10,... | collective-permute-start | bytes 393224 | tf_op jit(solution)/shard_map/ppermute | solution.py:510
  19.3 1.0 collective-permute-start.2
  20.3 1.5 %collective-permute-done.c1 = bf16[512,128]{1,0:T(8,128)(2,1)S(1)} collective-permute-done((bf16[512,128]{1,0:T(8,128)(2,1)S(1)}, bf16[512,128]{1,0:T(8,128)(2,1)S(1)}, u32[]{:S(2)}, u32[]{:S(2)}) %collective-permute-start) | collective-permute-done | bytes 131104 | tf_op jit(solution)/shard_map/ppermute | solution.py:510
  21.8 4.0 %collective-permute-done.1.c2 = bf16[512,128]{1,0:T(8,128)(2,1)S(1)} collective-permute-done((bf16[512,128]{1,0:T(8,128)(2,1)S(1)}, bf16[512,128]{1,0:T(8,128)(2,1)S(1)}, u32[]{:S(2)}, u32[]{:S(2)}) %collective-permute-start.1) | collective-permute-done | bytes 131104 | tf_op jit(solution)/shard_map/ppermute | solution.py:510
  25.7 0.0 collective-permute-done.2.c3
  25.7 0.0 all-to-all-done.told
  25.8 3.6 %reply_stage.1 = (bf16[64,128,128]{2,1,0:T(8,128)(2,1)}, bf16[256,128]{1,0:T(8,128)(2,1)}, bf16[256,128]{1,0:T(8,128)(2,1)}, bf16[256,128]{1,0:T(8,128)(2,1)}, b...) custom-call(s32[1]{0:T(128)} %bitcast.z, bf16[32,48,128]{2,1,0:T(8,128)(2,1)S(1)} %all-to-all-done.told, ...), custom_call_target="tpu_custom_call" | custom-call | tf_op jit(solution)/shard_map/reply_stage/pallas_call | solution.py:293
  29.4 7.2 %all-to-all-start.1 = ((bf16[32,256,128]{2,1,0:T(8,128)(2,1)}), bf16[32,256,128]{2,1,0:T(8,128)(2,1)S(1)}, u32[]{:S(2)}, u32[]{:S(2)}) async-start(bf16[32,256,128]{2,1,0:T(8,128)(2,1)} %bitcast.9), calls=%async_computation.1 | async-start | bytes 4194304 | tf_op jit(solution)/shard_map/all_to_all | solution.py:521
  36.7 0.0 copy-start.11
  36.7 6.1 %q_stage.1 = (bf16[512,256]{1,0:T(8,128)(2,1)}, bf16[512,256]{1,0:T(8,128)(2,1)}, bf16[512,256]{1,0:T(8,128)(2,1)}, bf16[512,256]{1,0:T(8,128)(2,1)}) custom-call(s32[1]{0:T(128)} %bitcast.z, bf16[512,1024]{1,0:T(8,128)(2,1)} %get-tuple-element.31.normed_in, bf16[1024,1024]{1,0:T(8,128)(2,1)} %query_in.1), custom_call_target="tpu_custom_call" | custom-call | flops 1073741824 | bytes 4194304 | tf_op jit(solution)/shard_map/q_stage/pallas_call | solution.py:237
  42.8 1.3 %collective-permute-start.8 = (bf16[512,256]{1,0:T(8,128)(2,1)}, bf16[512,256]{1,0:T(8,128)(2,1)S(1)}, u32[]{:S(2)}, u32[]{:S(2)}) collective-permute-start(bf16[512,256]{1,0:T(8,128)(2,1)} %get-tuple-element.48), channel_id=1, source_target_pairs={{0,1},{1,2},{2,3},{3,0},{4,5},{5,6},{6,7},{7,4},{8,9},{9,10},{10,1... | collective-permute-start | bytes 786440 | tf_op jit(solution)/shard_map/ppermute | solution.py:510
  44.1 1.0 collective-permute-start.3
  45.0 2.5 %collective-permute-start.4 = (bf16[256,128]{1,0:T(8,128)(2,1)S(1)}, bf16[256,128]{1,0:T(8,128)(2,1)S(1)}, u32[]{:S(2)}, u32[]{:S(2)}) collective-permute-start(bf16[256,128]{1,0:T(8,128)(2,1)S(1)} %copy-done.19), channel_id=1, source_target_pairs={{0,2},{1,3},{2,0},{3,1},{4,6},{5,7},{6,4},{7,5},{8,10},{9,11},{10,... | collective-permute-start | bytes 196616 | tf_op jit(solution)/shard_map/ppermute | solution.py:510
  47.6 1.6 %collective-permute-start.5 = (bf16[256,128]{1,0:T(8,128)(2,1)S(1)}, bf16[256,128]{1,0:T(8,128)(2,1)S(1)}, u32[]{:S(2)}, u32[]{:S(2)}) collective-permute-start(bf16[256,128]{1,0:T(8,128)(2,1)S(1)} %copy-done.18), channel_id=1, source_target_pairs={{0,3},{1,0},{2,1},{3,2},{4,7},{5,4},{6,5},{7,6},{8,11},{9,8},{10,9... | collective-permute-start | bytes 196616 | tf_op jit(solution)/shard_map/ppermute | solution.py:510
  49.1 0.0 collective-permute-start.7
  49.1 5.3 %collective-permute-done.3.s1 = bf16[256,128]{1,0:T(8,128)(2,1)S(1)} collective-permute-done((bf16[256,128]{1,0:T(8,128)(2,1)S(1)}, bf16[256,128]{1,0:T(8,128)(2,1)S(1)}, u32[]{:S(2)}, u32[]{:S(2)}) %collective-permute-start.3) | collective-permute-done | bytes 65568 | tf_op jit(solution)/shard_map/ppermute | solution.py:510
  54.5 0.9 collective-permute-start.6
  55.4 0.6 collective-permute-done.4.s2
  55.9 0.0 collective-permute-done.5.s3
  56.0 0.9 copy-done.9
  56.9 5.1 %near_stage.4 = (f32[2,4,256,128]{3,2,1,0:T(8,128)}, bf16[2,4,256,128]{3,2,1,0:T(8,128)(2,1)}) custom-call(s32[1]{0:T(128)} %bitcast.z, f32[16]{0:T(128)S(1)} %copy-done.11, bf16[512,256]{1,0:T(8,128)(2,1)S(1)} %copy-done.9, bf16[4,4,128,128]{3,2,1,0:T(8,128)(2,1)S(1)} %copy-done.16, bf16[256,128]{1,0:T(8,128)(2,1)S(1)} %copy-done.17, ...), custom_call_target="tpu_custom_call" | custom-call | flops 1342177280 | bytes 2097152 | tf_op jit(solution)/shard_map/near_stage/pallas_call | solution.py:372
  62.0 0.0 collective-permute-done.8.q
  62.0 5.1 %near_stage.5 = (f32[2,4,256,128]{3,2,1,0:T(8,128)}, bf16[2,4,256,128]{3,2,1,0:T(8,128)(2,1)}) custom-call(s32[1]{0:T(128)} %bitcast.z, f32[16]{0:T(128)S(1)} %copy-done.11, bf16[512,256]{1,0:T(8,128)(2,1)S(1)} %collective-permute-done.8.q, bf16[4,4,128,128]{3,2,1,0:T(8,128)(2,1)S(1)} %copy-done.16, bf16[256,128]{1,0:T(8,128)(2,1)S(1)} %copy-done.17, ...), custom_call_target="tpu_custom_call" | custom-call | flops 1342177280 | bytes 2097152 | tf_op jit(solution)/shard_map/near_stage/pallas_call | solution.py:372
  67.1 0.0 collective-permute-done.7.q
  67.1 5.1 %near_stage.6 = (f32[2,4,256,128]{3,2,1,0:T(8,128)}, bf16[2,4,256,128]{3,2,1,0:T(8,128)(2,1)}) custom-call(s32[1]{0:T(128)} %bitcast.z, f32[16]{0:T(128)S(1)} %copy-done.11, bf16[512,256]{1,0:T(8,128)(2,1)S(1)} %collective-permute-done.7.q, bf16[4,4,128,128]{3,2,1,0:T(8,128)(2,1)S(1)} %copy-done.16, bf16[256,128]{1,0:T(8,128)(2,1)S(1)} %copy-done.17, ...), custom_call_target="tpu_custom_call" | custom-call | flops 1342177280 | bytes 2097152 | tf_op jit(solution)/shard_map/near_stage/pallas_call | solution.py:372
  72.2 0.0 collective-permute-done.6.q
  72.2 5.0 %near_stage.7 = (f32[2,4,256,128]{3,2,1,0:T(8,128)}, bf16[2,4,256,128]{3,2,1,0:T(8,128)(2,1)}) custom-call(s32[1]{0:T(128)} %bitcast.z, f32[16]{0:T(128)S(1)} %copy-done.11, bf16[512,256]{1,0:T(8,128)(2,1)S(1)} %collective-permute-done.6.q, bf16[4,4,128,128]{3,2,1,0:T(8,128)(2,1)S(1)} %copy-done.16, bf16[256,128]{1,0:T(8,128)(2,1)S(1)} %copy-done.17, ...), custom_call_target="tpu_custom_call" | custom-call | flops 1342177280 | bytes 2097152 | tf_op jit(solution)/shard_map/near_stage/pallas_call | solution.py:372
  77.2 0.0 all-to-all-done.1
  77.2 1.2 %copy-done = f32[2,4,256,128]{3,2,1,0:T(8,128)S(1)} copy-done((f32[2,4,256,128]{3,2,1,0:T(8,128)S(1)}, f32[2,4,256,128]{3,2,1,0:T(8,128)}, u32[]{:S(2)}) %copy-start) | copy-done | bytes 1048600
  78.5 1.0 copy-done.1
  79.5 2.3 %far_stage.6 = bf16[512,256]{1,0:T(8,128)(2,1)S(1)} custom-call(s32[1]{0:T(128)} %bitcast.z, s32[16,4]{1,0:T(8,128)S(1)} %get-tuple-element.30.slots, f32[16]{0:T(128)S(1)} %copy-done.11, bf16[512,256]{1,0:T(8,128)(2,1)S(1)} %collective-permute-done.6.q, f32[2,4,256,128]{3,2,1,0:T(8,128)S(1)} %copy-done, bf16[2,4,256,128]{3,2,1,0:T(8,128)(2,1)S(1)} %copy-done.1, ...), custom_call_target="tpu_custom_call" | custom-call | flops 536870912 | bytes 4194304 | tf_op jit(solution)/shard_map/far_stage/pallas_call | solution.py:456
  81.9 2.1 %collective-permute-start.10 = (bf16[512,256]{1,0:T(8,128)(2,1)S(1)}, bf16[512,256]{1,0:T(8,128)(2,1)S(1)}, u32[]{:S(2)}, u32[]{:S(2)}) collective-permute-start(bf16[512,256]{1,0:T(8,128)(2,1)S(1)} %far_stage.6), channel_id=1, source_target_pairs={{0,2},{1,3},{2,0},{3,1},{4,6},{5,7},{6,4},{7,5},{8,10},{9,11},{10,... | collective-permute-start | bytes 786440 | tf_op jit(solution)/shard_map/ppermute | solution.py:510
  84.0 2.3 %far_stage.5 = bf16[512,256]{1,0:T(8,128)(2,1)S(1)} custom-call(s32[1]{0:T(128)} %bitcast.z, s32[16,4]{1,0:T(8,128)S(1)} %get-tuple-element.30.slots, f32[16]{0:T(128)S(1)} %copy-done.11, bf16[512,256]{1,0:T(8,128)(2,1)S(1)} %collective-permute-done.8.q, f32[2,4,256,128]{3,2,1,0:T(8,128)S(1)} %copy-done.3, bf16[2,4,256,128]{3,2,1,0:T(8,128)(2,1)S(1)} %copy-done.7, ...), custom_call_target="tpu_custom_call" | custom-call | flops 536870912 | bytes 4194304 | tf_op jit(solution)/shard_map/far_stage/pallas_call | solution.py:456
  86.4 0.0 copy-start.2
  86.4 1.6 %collective-permute-start.9 = (bf16[512,256]{1,0:T(8,128)(2,1)S(1)}, bf16[512,256]{1,0:T(8,128)(2,1)S(1)}, u32[]{:S(2)}, u32[]{:S(2)}) collective-permute-start(bf16[512,256]{1,0:T(8,128)(2,1)S(1)} %far_stage.5), channel_id=1, source_target_pairs={{0,3},{1,0},{2,1},{3,2},{4,7},{5,4},{6,5},{7,6},{8,11},{9,8},{10,9... | collective-permute-start | bytes 786440 | tf_op jit(solution)/shard_map/ppermute | solution.py:510
  88.0 2.3 %far_stage.7 = bf16[512,256]{1,0:T(8,128)(2,1)S(1)} custom-call(s32[1]{0:T(128)} %bitcast.z, s32[16,4]{1,0:T(8,128)S(1)} %get-tuple-element.30.slots, f32[16]{0:T(128)S(1)} %copy-done.11, bf16[512,256]{1,0:T(8,128)(2,1)S(1)} %collective-permute-done.7.q, f32[2,4,256,128]{3,2,1,0:T(8,128)S(1)} %copy-done.4, bf16[2,4,256,128]{3,2,1,0:T(8,128)(2,1)S(1)} %copy-done.8, ...), custom_call_target="tpu_custom_call" | custom-call | flops 536870912 | bytes 4194304 | tf_op jit(solution)/shard_map/far_stage/pallas_call | solution.py:456
  90.4 0.0 copy-start.5
  90.4 0.0 copy-start.13
  90.4 0.8 collective-permute-start.11
  91.2 2.3 %far_stage.4.a0 = bf16[512,256]{1,0:T(8,128)(2,1)S(1)} custom-call(s32[1]{0:T(128)} %bitcast.z, s32[16,4]{1,0:T(8,128)S(1)} %get-tuple-element.30.slots, f32[16]{0:T(128)S(1)} %copy-done.11, bf16[512,256]{1,0:T(8,128)(2,1)S(1)} %copy-done.10, f32[2,4,256,128]{3,2,1,0:T(8,128)S(1)} %copy-done.2, bf16[2,4,256,128]{3,2,1,0:T(8,128)(2,1)S(1)} %copy-done.6, ...), custom_call_target="tpu_custom_call" | custom-call | flops 536870912 | bytes 4194304 | tf_op jit(solution)/shard_map/far_stage/pallas_call | solution.py:456
  93.5 0.0 collective-permute-done.10.a2
  93.5 1.1 %collective-permute-done.9.a1 = bf16[512,256]{1,0:T(8,128)(2,1)S(1)} collective-permute-done((bf16[512,256]{1,0:T(8,128)(2,1)S(1)}, bf16[512,256]{1,0:T(8,128)(2,1)S(1)}, u32[]{:S(2)}, u32[]{:S(2)}) %collective-permute-start.9) | collective-permute-done | bytes 262176 | tf_op jit(solution)/shard_map/ppermute | solution.py:510
  94.7 3.4 %collective-permute-done.11.a3 = bf16[512,256]{1,0:T(8,128)(2,1)S(1)} collective-permute-done((bf16[512,256]{1,0:T(8,128)(2,1)S(1)}, bf16[512,256]{1,0:T(8,128)(2,1)S(1)}, u32[]{:S(2)}, u32[]{:S(2)}) %collective-permute-start.11) | collective-permute-done | bytes 262176 | tf_op jit(solution)/shard_map/ppermute | solution.py:510
  98.1 11.0 %ffn_stage.1 = bf16[512,1024]{1,0:T(8,128)(2,1)} custom-call(s32[1]{0:T(128)} %bitcast.z, bf16[512,1024]{1,0:T(8,128)(2,1)S(1)} %copy-done.5, bf16[512,256]{1,0:T(8,128)(2,1)S(1)} %far_stage.4.a0, bf16[512,256]{1,0:T(8,128)(2,1)S(1)} %collective-permute-done.9.a1, bf16[512,256]{1,0:T(8,128)(2,1)S(1)} %collective-permute-done.10.a2, ...), custom_call_target="tpu_custom_call" | custom-call | flops 7516192768 | bytes 18874368 | tf_op jit(solution)/shard_map/ffn_stage/pallas_call | solution.py:491
  (34 shorter events, 0.1 us)
Async XLA Ops:
  0.0 0.7 copy-start.12
  6.3 19.5 %all-to-all-start = ((bf16[32,48,128]{2,1,0:T(8,128)(2,1)}), bf16[32,48,128]{2,1,0:T(8,128)(2,1)S(1)}, u32[]{:S(2)}, u32[]{:S(2)}) async-start(bf16[32,48,128]{2,1,0:T(8,128)(2,1)} %get-tuple-element.33), calls=%async_computation | async-start | bytes 786432 | tf_op jit(solution)/shard_map/all_to_all | solution.py:517
  13.7 8.0 %collective-permute-start = (bf16[512,128]{1,0:T(8,128)(2,1)S(1)}, bf16[512,128]{1,0:T(8,128)(2,1)S(1)}, u32[]{:S(2)}, u32[]{:S(2)}) collective-permute-start(bf16[512,128]{1,0:T(8,128)(2,1)S(1)} %get-tuple-element.35), channel_id=1, source_target_pairs={{0,1},{1,2},{2,3},{3,0},{4,5},{5,6},{6,7},{7,4},{8,9},{9,10},{10,1... | collective-permute-start | bytes 393224 | tf_op jit(solution)/shard_map/ppermute | solution.py:510
  15.7 10.0 %collective-permute-start.1 = (bf16[512,128]{1,0:T(8,128)(2,1)S(1)}, bf16[512,128]{1,0:T(8,128)(2,1)S(1)}, u32[]{:S(2)}, u32[]{:S(2)}) collective-permute-start(bf16[512,128]{1,0:T(8,128)(2,1)S(1)} %get-tuple-element.36), channel_id=1, source_target_pairs={{0,2},{1,3},{2,0},{3,1},{4,6},{5,7},{6,4},{7,5},{8,10},{9,11},{10,... | collective-permute-start | bytes 393224 | tf_op jit(solution)/shard_map/ppermute | solution.py:510
  19.3 6.5 %collective-permute-start.2 = (bf16[512,128]{1,0:T(8,128)(2,1)S(1)}, bf16[512,128]{1,0:T(8,128)(2,1)S(1)}, u32[]{:S(2)}, u32[]{:S(2)}) collective-permute-start(bf16[512,128]{1,0:T(8,128)(2,1)S(1)} %get-tuple-element.37), channel_id=1, source_target_pairs={{0,3},{1,0},{2,1},{3,2},{4,7},{5,4},{6,5},{7,6},{8,11},{9,8},{10,9... | collective-permute-start | bytes 393224 | tf_op jit(solution)/shard_map/ppermute | solution.py:510
  29.4 47.8 %all-to-all-start.1 = ((bf16[32,256,128]{2,1,0:T(8,128)(2,1)}), bf16[32,256,128]{2,1,0:T(8,128)(2,1)S(1)}, u32[]{:S(2)}, u32[]{:S(2)}) async-start(bf16[32,256,128]{2,1,0:T(8,128)(2,1)} %bitcast.9), calls=%async_computation.1 | async-start | bytes 4194304 | tf_op jit(solution)/shard_map/all_to_all | solution.py:521
  36.6 7.4 %copy-start.20 = (bf16[256,128]{1,0:T(8,128)(2,1)S(1)}, bf16[256,128]{1,0:T(8,128)(2,1)}, u32[]{:S(2)}) copy-start(bf16[256,128]{1,0:T(8,128)(2,1)} %get-tuple-element.40) | copy-start | bytes 196612
  36.6 8.4 %copy-start.19 = (bf16[256,128]{1,0:T(8,128)(2,1)S(1)}, bf16[256,128]{1,0:T(8,128)(2,1)}, u32[]{:S(2)}) copy-start(bf16[256,128]{1,0:T(8,128)(2,1)} %get-tuple-element.41) | copy-start | bytes 196612
  36.7 10.9 %copy-start.18 = (bf16[256,128]{1,0:T(8,128)(2,1)S(1)}, bf16[256,128]{1,0:T(8,128)(2,1)}, u32[]{:S(2)}) copy-start(bf16[256,128]{1,0:T(8,128)(2,1)} %get-tuple-element.42) | copy-start | bytes 196612
  36.7 19.3 %copy-start.11 = (f32[16]{0:T(128)S(1)}, f32[16]{0:T(128)}, u32[]{:S(2)}) copy-start(f32[16]{0:T(128)} %scale.15) | copy-start | bytes 196
  36.7 19.3 %copy-start.16 = (bf16[4,4,128,128]{3,2,1,0:T(8,128)(2,1)S(1)}, bf16[4,4,128,128]{3,2,1,0:T(8,128)(2,1)}, u32[]{:S(2)}) copy-start(bf16[4,4,128,128]{3,2,1,0:T(8,128)(2,1)} %get-tuple-element.38.kv) | copy-start | bytes 1572868
  36.7 19.3 %copy-start.17 = (bf16[256,128]{1,0:T(8,128)(2,1)S(1)}, bf16[256,128]{1,0:T(8,128)(2,1)}, u32[]{:S(2)}) copy-start(bf16[256,128]{1,0:T(8,128)(2,1)} %get-tuple-element.39.s0) | copy-start | bytes 196612
  42.8 19.2 %collective-permute-start.8 = (bf16[512,256]{1,0:T(8,128)(2,1)}, bf16[512,256]{1,0:T(8,128)(2,1)S(1)}, u32[]{:S(2)}, u32[]{:S(2)}) collective-permute-start(bf16[512,256]{1,0:T(8,128)(2,1)} %get-tuple-element.48), channel_id=1, source_target_pairs={{0,1},{1,2},{2,3},{3,0},{4,5},{5,6},{6,7},{7,4},{8,9},{9,10},{10,1... | collective-permute-start | bytes 786440 | tf_op jit(solution)/shard_map/ppermute | solution.py:510
  44.1 10.4 %collective-permute-start.3 = (bf16[256,128]{1,0:T(8,128)(2,1)S(1)}, bf16[256,128]{1,0:T(8,128)(2,1)S(1)}, u32[]{:S(2)}, u32[]{:S(2)}) collective-permute-start(bf16[256,128]{1,0:T(8,128)(2,1)S(1)} %copy-done.20), channel_id=1, source_target_pairs={{0,1},{1,2},{2,3},{3,0},{4,5},{5,6},{6,7},{7,4},{8,9},{9,10},{10,1... | collective-permute-start | bytes 196616 | tf_op jit(solution)/shard_map/ppermute | solution.py:510
  45.0 10.9 %collective-permute-start.4 = (bf16[256,128]{1,0:T(8,128)(2,1)S(1)}, bf16[256,128]{1,0:T(8,128)(2,1)S(1)}, u32[]{:S(2)}, u32[]{:S(2)}) collective-permute-start(bf16[256,128]{1,0:T(8,128)(2,1)S(1)} %copy-done.19), channel_id=1, source_target_pairs={{0,2},{1,3},{2,0},{3,1},{4,6},{5,7},{6,4},{7,5},{8,10},{9,11},{10,... | collective-permute-start | bytes 196616 | tf_op jit(solution)/shard_map/ppermute | solution.py:510
  47.6 8.4 %collective-permute-start.5 = (bf16[256,128]{1,0:T(8,128)(2,1)S(1)}, bf16[256,128]{1,0:T(8,128)(2,1)S(1)}, u32[]{:S(2)}, u32[]{:S(2)}) collective-permute-start(bf16[256,128]{1,0:T(8,128)(2,1)S(1)} %copy-done.18), channel_id=1, source_target_pairs={{0,3},{1,0},{2,1},{3,2},{4,7},{5,4},{6,5},{7,6},{8,11},{9,8},{10,9... | collective-permute-start | bytes 196616 | tf_op jit(solution)/shard_map/ppermute | solution.py:510
  49.1 18.0 %collective-permute-start.7 = (bf16[512,256]{1,0:T(8,128)(2,1)}, bf16[512,256]{1,0:T(8,128)(2,1)S(1)}, u32[]{:S(2)}, u32[]{:S(2)}) collective-permute-start(bf16[512,256]{1,0:T(8,128)(2,1)} %get-tuple-element.47), channel_id=1, source_target_pairs={{0,3},{1,0},{2,1},{3,2},{4,7},{5,4},{6,5},{7,6},{8,11},{9,8},{10,9... | collective-permute-start | bytes 786440 | tf_op jit(solution)/shard_map/ppermute | solution.py:510
  54.5 17.7 %collective-permute-start.6 = (bf16[512,256]{1,0:T(8,128)(2,1)}, bf16[512,256]{1,0:T(8,128)(2,1)S(1)}, u32[]{:S(2)}, u32[]{:S(2)}) collective-permute-start(bf16[512,256]{1,0:T(8,128)(2,1)} %get-tuple-element.46), channel_id=1, source_target_pairs={{0,2},{1,3},{2,0},{3,1},{4,6},{5,7},{6,4},{7,5},{8,10},{9,11},{10,... | collective-permute-start | bytes 786440 | tf_op jit(solution)/shard_map/ppermute | solution.py:510
  56.0 1.0 copy-start.9
  77.2 1.2 %copy-start = (f32[2,4,256,128]{3,2,1,0:T(8,128)S(1)}, f32[2,4,256,128]{3,2,1,0:T(8,128)}, u32[]{:S(2)}) copy-start(f32[2,4,256,128]{3,2,1,0:T(8,128)} %get-tuple-element.53.rest_0_.state) | copy-start | bytes 3145732
  78.5 1.0 copy-start.1
  79.5 4.5 %copy-start.3 = (f32[2,4,256,128]{3,2,1,0:T(8,128)S(1)}, f32[2,4,256,128]{3,2,1,0:T(8,128)}, u32[]{:S(2)}) copy-start(f32[2,4,256,128]{3,2,1,0:T(8,128)} %get-tuple-element.49.rest_0_.state) | copy-start | bytes 3145732
  79.5 4.5 %copy-start.7 = (bf16[2,4,256,128]{3,2,1,0:T(8,128)(2,1)S(1)}, bf16[2,4,256,128]{3,2,1,0:T(8,128)(2,1)}, u32[]{:S(2)}) copy-start(bf16[2,4,256,128]{3,2,1,0:T(8,128)(2,1)} %get-tuple-element.50.rest_1_.peaks) | copy-start | bytes 1572868
  81.9 6.2 %copy-start.4 = (f32[2,4,256,128]{3,2,1,0:T(8,128)S(1)}, f32[2,4,256,128]{3,2,1,0:T(8,128)}, u32[]{:S(2)}) copy-start(f32[2,4,256,128]{3,2,1,0:T(8,128)} %get-tuple-element.51.rest_0_.state) | copy-start | bytes 3145732
  81.9 6.2 %copy-start.8 = (bf16[2,4,256,128]{3,2,1,0:T(8,128)(2,1)S(1)}, bf16[2,4,256,128]{3,2,1,0:T(8,128)(2,1)}, u32[]{:S(2)}) copy-start(bf16[2,4,256,128]{3,2,1,0:T(8,128)(2,1)} %get-tuple-element.52.rest_1_.peaks) | copy-start | bytes 1572868
  81.9 11.7 %collective-permute-start.10 = (bf16[512,256]{1,0:T(8,128)(2,1)S(1)}, bf16[512,256]{1,0:T(8,128)(2,1)S(1)}, u32[]{:S(2)}, u32[]{:S(2)}) collective-permute-start(bf16[512,256]{1,0:T(8,128)(2,1)S(1)} %far_stage.6), channel_id=1, source_target_pairs={{0,2},{1,3},{2,0},{3,1},{4,6},{5,7},{6,4},{7,5},{8,10},{9,11},{10,... | collective-permute-start | bytes 786440 | tf_op jit(solution)/shard_map/ppermute | solution.py:510
  84.0 14.1 %copy-start.15 = (bf16[1024,1024]{1,0:T(8,128)(2,1)S(1)}, bf16[1024,1024]{1,0:T(8,128)(2,1)}, u32[]{:S(2)}) copy-start(bf16[1024,1024]{1,0:T(8,128)(2,1)} %w_out.1) | copy-start | bytes 6291460
  86.4 4.8 %copy-start.2 = (f32[2,4,256,128]{3,2,1,0:T(8,128)S(1)}, f32[2,4,256,128]{3,2,1,0:T(8,128)}, u32[]{:S(2)}) copy-start(f32[2,4,256,128]{3,2,1,0:T(8,128)} %get-tuple-element.43.rest_0_.state) | copy-start | bytes 3145732
  86.4 4.8 %copy-start.6 = (bf16[2,4,256,128]{3,2,1,0:T(8,128)(2,1)S(1)}, bf16[2,4,256,128]{3,2,1,0:T(8,128)(2,1)}, u32[]{:S(2)}) copy-start(bf16[2,4,256,128]{3,2,1,0:T(8,128)(2,1)} %get-tuple-element.44.rest_1_.peaks) | copy-start | bytes 1572868
  86.4 4.8 %copy-start.10 = (bf16[512,256]{1,0:T(8,128)(2,1)S(1)}, bf16[512,256]{1,0:T(8,128)(2,1)}, u32[]{:S(2)}) copy-start(bf16[512,256]{1,0:T(8,128)(2,1)} %get-tuple-element.32.q) | copy-start | bytes 786436
  86.4 8.3 %collective-permute-start.9 = (bf16[512,256]{1,0:T(8,128)(2,1)S(1)}, bf16[512,256]{1,0:T(8,128)(2,1)S(1)}, u32[]{:S(2)}, u32[]{:S(2)}) collective-permute-start(bf16[512,256]{1,0:T(8,128)(2,1)S(1)} %far_stage.5), channel_id=1, source_target_pairs={{0,3},{1,0},{2,1},{3,2},{4,7},{5,4},{6,5},{7,6},{8,11},{9,8},{10,9... | collective-permute-start | bytes 786440 | tf_op jit(solution)/shard_map/ppermute | solution.py:510
  88.0 10.0 %copy-start.14 = (bf16[1024,2048]{1,0:T(8,128)(2,1)S(1)}, bf16[1024,2048]{1,0:T(8,128)(2,1)}, u32[]{:S(2)}) copy-start(bf16[1024,2048]{1,0:T(8,128)(2,1)} %w_up.1) | copy-start | bytes 12582916
  90.4 7.7 %copy-start.5 = (bf16[512,1024]{1,0:T(8,128)(2,1)S(1)}, bf16[512,1024]{1,0:T(8,128)(2,1)}, u32[]{:S(2)}) copy-start(bf16[512,1024]{1,0:T(8,128)(2,1)} %tokens.1) | copy-start | bytes 3145732
  90.4 7.7 %copy-start.13 = (bf16[1024,2048]{1,0:T(8,128)(2,1)S(1)}, bf16[1024,2048]{1,0:T(8,128)(2,1)}, u32[]{:S(2)}) copy-start(bf16[1024,2048]{1,0:T(8,128)(2,1)} %w_gate.1) | copy-start | bytes 12582916
  90.4 7.7 %collective-permute-start.11 = (bf16[512,256]{1,0:T(8,128)(2,1)S(1)}, bf16[512,256]{1,0:T(8,128)(2,1)S(1)}, u32[]{:S(2)}, u32[]{:S(2)}) collective-permute-start(bf16[512,256]{1,0:T(8,128)(2,1)S(1)} %far_stage.7), channel_id=1, source_target_pairs={{0,1},{1,2},{2,3},{3,0},{4,5},{5,6},{6,7},{7,4},{8,9},{9,10},{10,1... | collective-permute-start | bytes 786440 | tf_op jit(solution)/shard_map/ppermute | solution.py:510

commit v3 on v2

--- a/solution.py
+++ b/solution.py
@@ -35,6 +35,7 @@
 FFN = 2048
 UNIT = 256
 STEPS = 2
+GROUPS = ((0,), (1,), (3, 2))
 
 
 bf16 = jnp.bfloat16
@@ -314,84 +315,141 @@
     return jnp.concatenate([jnp.ones((kv.shape[0], HEAD_DIM), kv.dtype), kv[:, HEAD_DIM:]], axis=1)
 
 
-def near_body(chunk, z, scale, q, kv, s0, s1, s2, s3, *rest):
-    state_out, peak_out, held, state, peaks, sems, peak_sems = rest[-7:]
+def near_body(chunks, z, scale, kv, s0, s1, s2, s3, *rest):
+    n = len(chunks)
+    qs, outs = rest[:n], rest[-6 - 2 * n : -6]
+    held, q, state, peaks, sems, peak_sems = rest[-6:]
     sums = jnp.concatenate([s0[...], s1[...], s2[...], s3[...]], axis=0)
     sum_keys = sums[:, :HEAD_DIM]
     sum_values = ones_beside(sums)
     half = BALL // BLOCK
 
-    def ball_of(b):
-        return kv[chunk, pl.ds(b * half, half)].reshape(BALL, PAIR_W)
-
-    def scores(b, r, keys):
-        here = q[pl.ds(b * BALL, BALL), r * HEAD_DIM : (r + 1) * HEAD_DIM]
-        ball = lax.dot_general(here, keys, NT, preferred_element_type=f32)
-        far = lax.dot_general(here, sum_keys, NT, preferred_element_type=f32)
-        held[r % 2, :, :BALL] = ball
-        held[r % 2, :, BALL:] = far
-        peak = jnp.maximum(
-            jnp.max(ball, axis=1, keepdims=True), jnp.max(far, axis=1, keepdims=True)
+    def copies(c, b, r):
+        return (
+            pltpu.make_async_copy(state.at[c, b, r], outs[2 * c].at[b, r], sems.at[c, b, r]),
+            pltpu.make_async_copy(peaks.at[c, b, r], outs[2 * c + 1].at[b, r], peak_sems.at[c, b, r]),
         )
-        return peak.astype(bf16).astype(f32)
-
-    def copies(b, r):
-        return (
-            pltpu.make_async_copy(state.at[b, r], state_out.at[b, r], sems.at[b, r]),
-            pltpu.make_async_copy(peaks.at[b, r], peak_out.at[b, r], peak_sems.at[b, r]),
-        )
-
-    def one_ball(b, peak):
-        ball = ball_of(b)
-        values = ones_beside(ball)
-        after = jnp.minimum(b + 1, BALLS - 1)
-        for r in range(RATIO):
-            if r + 1 < RATIO:
-                coming = scores(b, r + 1, ball[:, :HEAD_DIM])
-            else:
-                coming = scores(after, 0, ball_of(after)[:, :HEAD_DIM])
+
+    def one_chunk(c, here_of, chunk, start_copies):
+        balls = [kv[chunk, pl.ds(b * half, half)].reshape(BALL, PAIR_W) for b in range(BALLS)]
+        values = [ones_beside(ball) for ball in balls]
+        units = [(b, r) for b in range(BALLS) for r in range(RATIO)]
+
+        def scores(u):
+            b, r = units[u]
+            here = here_of(b, r)
+            ball = lax.dot_general(
+                here, balls[b][:, :HEAD_DIM], NT, preferred_element_type=f32
+            )
+            far = lax.dot_general(here, sum_keys, NT, preferred_element_type=f32)
+            held[u % 2, :, :BALL] = ball
+            held[u % 2, :, BALL:] = far
+            peak = jnp.maximum(
+                jnp.max(ball, axis=1, keepdims=True), jnp.max(far, axis=1, keepdims=True)
+            )
+            return peak.astype(bf16).astype(f32)
+
+        peak = scores(0)
+        for u, (b, r) in enumerate(units):
+            coming = scores(u + 1) if u + 1 < len(units) else None
             factor = scale[z[0] * RATIO + r] * (LOG2E / math.sqrt(HEAD_DIM))
-            w = jnp.exp2((held[r % 2] - peak) * factor).astype(bf16)
-            peaks[b, r] = jnp.broadcast_to(peak, (BALL, PAIR_W)).astype(bf16)
-            state[b, r] = jnp.dot(w[:, :BALL], values, preferred_element_type=f32) + jnp.dot(
+            w = jnp.exp2((held[u % 2] - peak) * factor).astype(bf16)
+            peaks[c, b, r] = jnp.broadcast_to(peak, (BALL, PAIR_W)).astype(bf16)
+            state[c, b, r] = jnp.dot(w[:, :BALL], values[b], preferred_element_type=f32) + jnp.dot(
                 w[:, BALL:], sum_values, preferred_element_type=f32
             )
-            for c in copies(b, r):
+            start_copies(b, r)
+            peak = coming
+
+    def part(ref):
+        def take(b, r):
+            return ref[b * BALL : (b + 1) * BALL, r * HEAD_DIM : (r + 1) * HEAD_DIM]
+
+        return take
+
+    if n == 1:
+
+        def begin(b, r):
+            for c in copies(0, b, r):
                 c.start()
-            peak = coming
-        return peak
-
-    lax.fori_loop(0, BALLS, one_ball, scores(0, 0, ball_of(0)[:, :HEAD_DIM]))
-    for b in range(BALLS):
-        for r in range(RATIO):
-            for c in copies(b, r):
-                c.wait()
-
-
-def near_stage(chunk, z, scale, q, kv, sums, others):
-    return pl.pallas_call(
-        functools.partial(near_body, chunk),
+
+        one_chunk(0, part(qs[0]), chunks[0], begin)
+    else:
+
+        def loop(c, _):
+            for i in range(n):
+
+                @pl.when(c == i)
+                def _():
+                    q[...] = qs[i][...]
+
+            chunk = jnp.where(c == 0, chunks[0], chunks[1])
+            one_chunk(c, part(q), chunk, lambda b, r: None)
+            for i in range(n):
+
+                @pl.when(c == i)
+                def _():
+                    for b in range(BALLS):
+                        for r in range(RATIO):
+                            for m in copies(i, b, r):
+                                m.start()
+
+            return 0
+
+        lax.fori_loop(0, n, loop, 0)
+    for c in range(n):
+        for b in range(BALLS):
+            for r in range(RATIO):
+                for m in copies(c, b, r):
+                    m.wait()
+
+
+def near_stage(chunks, z, scale, qs, kv, sums, others):
+    n = len(chunks)
+    shape = (BALLS, RATIO, BALL, PAIR_W)
+    outs = pl.pallas_call(
+        functools.partial(near_body, chunks),
         name="near_stage",
-        in_specs=[whole(SMEM)] * 2 + [whole(VMEM)] * 6 + [whole(pl.ANY)] * len(others),
-        out_specs=[whole(pltpu.HBM)] * 2,
-        out_shape=[
-            pltpu.HBM((BALLS, RATIO, BALL, PAIR_W), f32),
-            pltpu.HBM((BALLS, RATIO, BALL, PAIR_W), bf16),
-        ],
+        in_specs=[whole(SMEM)] * 2 + [whole(VMEM)] * (5 + n) + [whole(pl.ANY)] * len(others),
+        out_specs=[whole(pltpu.HBM)] * (2 * n),
+        out_shape=[pltpu.HBM(shape, f32), pltpu.HBM(shape, bf16)] * n,
         scratch_shapes=[
             VMEM((2, BALL, BALL + PTS * SUM_LOCAL * ZS), f32),
-            VMEM((BALLS, RATIO, BALL, PAIR_W), f32),
-            VMEM((BALLS, RATIO, BALL, PAIR_W), bf16),
-            pltpu.SemaphoreType.DMA((BALLS, RATIO)),
-            pltpu.SemaphoreType.DMA((BALLS, RATIO)),
+            VMEM((ROWS if n > 1 else 16, GROUP_W), bf16),
+            VMEM((n, *shape), f32),
+            VMEM((n, *shape), bf16),
+            pltpu.SemaphoreType.DMA((n, BALLS, RATIO)),
+            pltpu.SemaphoreType.DMA((n, BALLS, RATIO)),
         ],
-        compiler_params=params(12),
-        cost_estimate=cost(8 * 4 * ROWS * 1280 * 64, 2 << 20),
-    )(z, scale, near_core(q), near_core(kv), *[near_core(s) for s in sums], *[far_core(a) for a in others])
-
-
-def far_body(shift_by, z, slots, scale, q, state, peaks, fetched, *rest):
-    out, held = rest[-2:]
+        compiler_params=params(14),
+        cost_estimate=cost(8 * 4 * n * ROWS * 1280 * 64, 2 << 20),
+    )(
+        z,
+        scale,
+        near_core(kv),
+        *[near_core(s) for s in sums],
+        *[near_core(q) for q in qs],
+        *[far_core(a) for a in others],
+    )
+    return [outs[2 * c : 2 * c + 2] for c in range(n)]
+
+
+def far_body(shift_by, direct, z, slots, scale, q, state, peaks, fetched, *rest):
+    if direct:
+        out, held, state_held, peaks_held, sems = rest[-5:]
+        brought = []
+        for b in range(BALLS):
+            brought.append(
+                (
+                    pltpu.make_async_copy(state.at[b], state_held.at[b], sems.at[b, 0]),
+                    pltpu.make_async_copy(peaks.at[b], peaks_held.at[b], sems.at[b, 1]),
+                )
+            )
+            for c in brought[-1]:
+                c.start()
+        state, peaks = state_held, peaks_held
+    else:
+        out, held = rest[-2:]
     lane = lax.broadcasted_iota(jnp.int32, (BLOCK, PAIR_W), 1)
     first_row = ((z[0] - shift_by + ZS) % ZS) * PER
 
@@ -444,32 +502,49 @@
         coming = scores(2 * b + 1, 1)
         finish(b, 2 * b, 0, peak)
         after = scores(2 * b + 2, 0) if b + 1 < BALLS else None
+        if direct and b + 1 < BALLS:
+            for c in brought[b + 1]:
+                c.wait()
         finish(b, 2 * b + 1, 1, coming)
         return after
 
     peak = scores(0, 0)
+    if direct:
+        for c in brought[0]:
+            c.wait()
     for b in range(BALLS):
         peak = one_ball(b, peak)
 
 
-def far_stage(shift_by, z, slots, scale, q, state, fetched, others):
+def far_stage(shift_by, z, slots, scale, q, state, fetched, others, direct=False):
+    shape = (BALLS, RATIO, BALL, PAIR_W)
+    place, keep = (pltpu.HBM, far_core) if direct else (VMEM, near_core)
+    extra = [VMEM(shape, f32), VMEM(shape, bf16), pltpu.SemaphoreType.DMA((BALLS, 2))]
     return pl.pallas_call(
-        functools.partial(far_body, shift_by),
+        functools.partial(far_body, shift_by, direct),
         name="far_stage",
-        in_specs=[whole(SMEM)] * 3 + [whole(VMEM)] * 4 + [whole(pl.ANY)] * len(others),
+        in_specs=[whole(SMEM)] * 3
+        + [whole(VMEM)]
+        + [whole(place)] * 2
+        + [whole(VMEM)]
+        + [whole(pl.ANY)] * len(others),
         out_specs=whole(VMEM),
         out_shape=VMEM((ROWS, GROUP_W), bf16),
-        scratch_shapes=[VMEM((2, RATIO * BLOCK, PICKS * BLOCK), f32)],
+        scratch_shapes=[VMEM((2, RATIO * BLOCK, PICKS * BLOCK), f32)] + (extra if direct else []),
         compiler_params=params(12),
         cost_estimate=cost(8 * 4 * ROWS * 512 * 64, 4 << 20),
-    )(z, slots, scale, near_core(q), *[near_core(a) for a in state], near_core(fetched), *[far_core(a) for a in others])
-
-
-def ffn_body(
-    z, tokens, a0, a1, a2, a3, w_out, w_gate, w_up, down_in, out, mid_held, held, hidden, w_down, sem
-):
-    down = pltpu.make_async_copy(down_in, w_down, sem.at[0])
-    down.start()
+    )(
+        z,
+        slots,
+        scale,
+        near_core(q),
+        *[keep(a) for a in state],
+        near_core(fetched),
+        *[far_core(a) for a in others],
+    )
+
+
+def ffn_body(z, tokens, a0, a1, a2, a3, w_out, w_gate, w_up, w_down, out, mid_held, held, hidden):
     mid = tokens[...].astype(f32)
     for k, a in enumerate((a0, a1, a2, a3)):
         start = pl.multiple_of(((z[0] + k) % ZS) * GROUP_W, GROUP_W)
@@ -481,7 +556,6 @@
         gate = jnp.dot(held[...], w_gate[:, cols], preferred_element_type=f32)
         upward = jnp.dot(held[...], w_up[:, cols], preferred_element_type=f32)
         hidden[:, cols] = (gate / (1.0 + jnp.exp(-gate)) * upward).astype(bf16)
-    down.wait()
     out[...] = (
         mid_held[...] + jnp.dot(hidden[...], w_down[...], preferred_element_type=f32)
     ).astype(bf16)
@@ -491,19 +565,13 @@
     return pl.pallas_call(
         ffn_body,
         name="ffn_stage",
-        in_specs=[whole(SMEM)] + [whole(VMEM)] * 8 + [whole(pltpu.HBM)],
+        in_specs=[whole(SMEM)] + [whole(VMEM)] * 9,
         out_specs=whole(VMEM),
         out_shape=jax.ShapeDtypeStruct((ROWS, 1024), bf16),
-        scratch_shapes=[
-            VMEM((ROWS, 1024), f32),
-            VMEM((ROWS, 1024), bf16),
-            VMEM((ROWS, FFN), bf16),
-            VMEM((FFN, 1024), bf16),
-            pltpu.SemaphoreType.DMA((1,)),
-        ],
-        compiler_params=params(24),
+        scratch_shapes=[VMEM((ROWS, 1024), f32), VMEM((ROWS, 1024), bf16), VMEM((ROWS, FFN), bf16)],
+        compiler_params=params(14),
         cost_estimate=cost(2 * ROWS * 1024 * 7168, 18 << 20),
-    )(z, *[near_core(a) for a in (tokens, *parts, w_out, w_gate, w_up)], far_core(w_down))
+    )(z, *[near_core(a) for a in (tokens, *parts, w_out, w_gate, w_up, w_down)])
 
 
 def shift(array, k):
@@ -526,13 +594,15 @@
         q[k] = shift(query[k], k)
     states = [None] * ZS
     done = []
-    for k in (0, 1, 3, 2):
-        states[k] = near_stage(k, z, logit_scale, q[k], kv, sums, done)
-        done = states[k]
+    for group in GROUPS:
+        made = near_stage(group, z, logit_scale, [q[k] for k in group], kv, sums, done)
+        for k, one in zip(group, made):
+            states[k] = one
+        done = made[-1]
     parts = [None] * ZS
     for k in (2, 1, 3, 0):
         others = states[2] if k != 2 else []
-        attended = far_stage(k, z, slots, logit_scale, q[k], states[k], fetched, others)
+        attended = far_stage(k, z, slots, logit_scale, q[k], states[k], fetched, others, k == 2)
         parts[k] = shift(attended, ZS - k) if k else attended
     return ffn_stage(z, tokens, parts, w_out, w_gate, w_up, w_down)
 

time: 110 us -> 107 us (0.973)
  Pallas kernels: 55.9 us -> 52.2 us
    pallas_call x1, Pallas kernels: 11 us -> 9.08 us  [ffn_stage(): pl.pallas_call(ffn_body, name='ffn_stage', in_specs=[whole(SMEM)] + [whol...]
    pallas_call x8 -> x7, Pallas kernels: 29.6 us -> 27.9 us  [the longest x3 17.3 us: near_stage(): pl.pallas_call(functools.partial(near_body, chunks), name='near_stage', i...]
    unnamed x42 -> x40, local copies, waits for them, and re-layouts: 3.96 us -> 3.96 us
  transfers between devices with their start and end apart: 14 -> 14, of which waited for: 6 -> 6; matrix products, arithmetic and copies ran while one was open for 0% -> 0% of each run, Pallas kernels for 31% -> 30%
where the time goes in v3:
time: 107 us
  Pallas kernels  52.2 us (49%)
  starting transfers between devices  33.7 us (31%)
  waiting for transfers between devices  16.9 us (16%)
  local copies, waits for them, and re-layouts  3.96 us (4%)
    ppermute x12, starting transfers between devices, shift(): return lax.ppermute(array, 'head', [(i, (i + k) % ZS) for i in range(ZS)])  19 us
    pallas_call x3, Pallas kernels, near_stage(): pl.pallas_call(functools.partial(near_body, chunks), name='near_stage', i...  17.3 us
    ppermute x12, waiting for transfers between devices, shift(): return lax.ppermute(array, 'head', [(i, (i + k) % ZS) for i in range(ZS)])  16.9 us
    pallas_call x4, Pallas kernels, far_stage(): pl.pallas_call(functools.partial(far_body, shift_by, direct), name='far_s...  10.5 us
    pallas_call x1, Pallas kernels, ffn_stage(): pl.pallas_call(ffn_body, name='ffn_stage', in_specs=[whole(SMEM)] + [whol...  9.08 us
    all_to_all x1, starting transfers between devices, body(): lax.all_to_all(payload, 'pts', split_axis=0, concat_axis=0, tiled=True)  7.44 us
    all_to_all x1, starting transfers between devices, body(): lax.all_to_all(replies, 'pts', split_axis=0, concat_axis=0, tiled=True)  7.24 us
    pallas_call x1, Pallas kernels, q_stage(): pl.pallas_call(q_body, name='q_stage', in_specs=[whole(SMEM), hbm, hbm],...  6.08 us
  transfers between devices with their start and end apart: 14, of which 6 were waited for; matrix products, arithmetic and copies ran while one was open for 0% of the time, Pallas kernels for 30%

profile of v3, /device:TPU:0, one launch (start us, length us, event | category | flops | bytes accessed | tf_op | source)
XLA Modules:
  0.0 107.0 jit_solution(4791590254104666916)
XLA Ops:
  0.0 0.7 copy-done.10
  0.7 5.6 %first_stage.1 = (bf16[512,128]{1,0:T(8,128)(2,1)S(1)}, bf16[512,128]{1,0:T(8,128)(2,1)S(1)}, bf16[512,128]{1,0:T(8,128)(2,1)S(1)}, bf16[512,128]{1,0:T(8,128)(2...) custom-call(s32[1]{0:T(128)} %bitcast.z, s32[4,16]{1,0:T(4,128)S(1)} %bitcast.8, ...), custom_call_target="tpu_custom_call" | custom-call | flops 536870912 | bytes 4194304 | tf_op jit(solution)/shard_map/first_stage/pallas_call | solution.py:187
  6.3 7.4 %all-to-all-start = ((bf16[32,48,128]{2,1,0:T(8,128)(2,1)}), bf16[32,48,128]{2,1,0:T(8,128)(2,1)S(1)}, u32[]{:S(2)}, u32[]{:S(2)}) async-start(bf16[32,48,128]{2,1,0:T(8,128)(2,1)} %get-tuple-element.33), calls=%async_computation | async-start | bytes 786432 | tf_op jit(solution)/shard_map/all_to_all | solution.py:585
  13.7 2.0 %collective-permute-start = (bf16[512,128]{1,0:T(8,128)(2,1)S(1)}, bf16[512,128]{1,0:T(8,128)(2,1)S(1)}, u32[]{:S(2)}, u32[]{:S(2)}) collective-permute-start(bf16[512,128]{1,0:T(8,128)(2,1)S(1)} %get-tuple-element.35), channel_id=1, source_target_pairs={{0,1},{1,2},{2,3},{3,0},{4,5},{5,6},{6,7},{7,4},{8,9},{9,10},{10,1... | collective-permute-start | bytes 393224 | tf_op jit(solution)/shard_map/ppermute | solution.py:578
  15.7 3.6 %collective-permute-start.1 = (bf16[512,128]{1,0:T(8,128)(2,1)S(1)}, bf16[512,128]{1,0:T(8,128)(2,1)S(1)}, u32[]{:S(2)}, u32[]{:S(2)}) collective-permute-start(bf16[512,128]{1,0:T(8,128)(2,1)S(1)} %get-tuple-element.36), channel_id=1, source_target_pairs={{0,2},{1,3},{2,0},{3,1},{4,6},{5,7},{6,4},{7,5},{8,10},{9,11},{10,... | collective-permute-start | bytes 393224 | tf_op jit(solution)/shard_map/ppermute | solution.py:578
  19.3 1.0 collective-permute-start.2
  20.3 1.5 %collective-permute-done.c1 = bf16[512,128]{1,0:T(8,128)(2,1)S(1)} collective-permute-done((bf16[512,128]{1,0:T(8,128)(2,1)S(1)}, bf16[512,128]{1,0:T(8,128)(2,1)S(1)}, u32[]{:S(2)}, u32[]{:S(2)}) %collective-permute-start) | collective-permute-done | bytes 131104 | tf_op jit(solution)/shard_map/ppermute | solution.py:578
  21.8 4.0 %collective-permute-done.1.c2 = bf16[512,128]{1,0:T(8,128)(2,1)S(1)} collective-permute-done((bf16[512,128]{1,0:T(8,128)(2,1)S(1)}, bf16[512,128]{1,0:T(8,128)(2,1)S(1)}, u32[]{:S(2)}, u32[]{:S(2)}) %collective-permute-start.1) | collective-permute-done | bytes 131104 | tf_op jit(solution)/shard_map/ppermute | solution.py:578
  25.8 0.0 collective-permute-done.2.c3
  25.8 0.0 all-to-all-done.told
  25.8 3.6 %reply_stage.1 = (bf16[64,128,128]{2,1,0:T(8,128)(2,1)}, bf16[256,128]{1,0:T(8,128)(2,1)}, bf16[256,128]{1,0:T(8,128)(2,1)}, bf16[256,128]{1,0:T(8,128)(2,1)}, b...) custom-call(s32[1]{0:T(128)} %bitcast.z, bf16[32,48,128]{2,1,0:T(8,128)(2,1)S(1)} %all-to-all-done.told, ...), custom_call_target="tpu_custom_call" | custom-call | tf_op jit(solution)/shard_map/reply_stage/pallas_call | solution.py:294
  29.4 7.2 %all-to-all-start.1 = ((bf16[32,256,128]{2,1,0:T(8,128)(2,1)}), bf16[32,256,128]{2,1,0:T(8,128)(2,1)S(1)}, u32[]{:S(2)}, u32[]{:S(2)}) async-start(bf16[32,256,128]{2,1,0:T(8,128)(2,1)} %bitcast.9), calls=%async_computation.1 | async-start | bytes 4194304 | tf_op jit(solution)/shard_map/all_to_all | solution.py:589
  36.7 0.0 copy-start.9
  36.7 6.1 %q_stage.1 = (bf16[512,256]{1,0:T(8,128)(2,1)}, bf16[512,256]{1,0:T(8,128)(2,1)}, bf16[512,256]{1,0:T(8,128)(2,1)}, bf16[512,256]{1,0:T(8,128)(2,1)}) custom-call(s32[1]{0:T(128)} %bitcast.z, bf16[512,1024]{1,0:T(8,128)(2,1)} %get-tuple-element.31.normed_in, bf16[1024,1024]{1,0:T(8,128)(2,1)} %query_in.1), custom_call_target="tpu_custom_call" | custom-call | flops 1073741824 | bytes 4194304 | tf_op jit(solution)/shard_map/q_stage/pallas_call | solution.py:238
  42.8 1.3 %collective-permute-start.8 = (bf16[512,256]{1,0:T(8,128)(2,1)}, bf16[512,256]{1,0:T(8,128)(2,1)S(1)}, u32[]{:S(2)}, u32[]{:S(2)}) collective-permute-start(bf16[512,256]{1,0:T(8,128)(2,1)} %get-tuple-element.48), channel_id=1, source_target_pairs={{0,1},{1,2},{2,3},{3,0},{4,5},{5,6},{6,7},{7,4},{8,9},{9,10},{10,1... | collective-permute-start | bytes 786440 | tf_op jit(solution)/shard_map/ppermute | solution.py:578
  44.1 0.0 copy-done.19
  44.1 1.0 collective-permute-start.3
  45.1 2.5 %collective-permute-start.4 = (bf16[256,128]{1,0:T(8,128)(2,1)S(1)}, bf16[256,128]{1,0:T(8,128)(2,1)S(1)}, u32[]{:S(2)}, u32[]{:S(2)}) collective-permute-start(bf16[256,128]{1,0:T(8,128)(2,1)S(1)} %copy-done.18), channel_id=1, source_target_pairs={{0,2},{1,3},{2,0},{3,1},{4,6},{5,7},{6,4},{7,5},{8,10},{9,11},{10,... | collective-permute-start | bytes 196616 | tf_op jit(solution)/shard_map/ppermute | solution.py:578
  47.6 1.6 %collective-permute-start.5 = (bf16[256,128]{1,0:T(8,128)(2,1)S(1)}, bf16[256,128]{1,0:T(8,128)(2,1)S(1)}, u32[]{:S(2)}, u32[]{:S(2)}) collective-permute-start(bf16[256,128]{1,0:T(8,128)(2,1)S(1)} %copy-done.17), channel_id=1, source_target_pairs={{0,3},{1,0},{2,1},{3,2},{4,7},{5,4},{6,5},{7,6},{8,11},{9,8},{10,9... | collective-permute-start | bytes 196616 | tf_op jit(solution)/shard_map/ppermute | solution.py:578
  49.1 0.0 collective-permute-start.6
  49.2 5.3 %collective-permute-done.3.s1 = bf16[256,128]{1,0:T(8,128)(2,1)S(1)} collective-permute-done((bf16[256,128]{1,0:T(8,128)(2,1)S(1)}, bf16[256,128]{1,0:T(8,128)(2,1)S(1)}, u32[]{:S(2)}, u32[]{:S(2)}) %collective-permute-start.3) | collective-permute-done | bytes 65568 | tf_op jit(solution)/shard_map/ppermute | solution.py:578
  54.5 0.9 collective-permute-start.7
  55.4 0.6 collective-permute-done.4.s2
  56.0 0.0 collective-permute-done.5.s3
  56.0 0.9 copy-done.7
  56.9 4.5 %near_stage.3 = (f32[2,4,256,128]{3,2,1,0:T(8,128)}, bf16[2,4,256,128]{3,2,1,0:T(8,128)(2,1)}) custom-call(s32[1]{0:T(128)} %bitcast.z, f32[16]{0:T(128)S(1)} %copy-done.9, bf16[4,4,128,128]{3,2,1,0:T(8,128)(2,1)S(1)} %copy-done.15, bf16[256,128]{1,0:T(8,128)(2,1)S(1)} %copy-done.16, bf16[256,128]{1,0:T(8,128)(2,1)S(1)} %collective-permute-done.3.s1, ...), custom_call_target="tpu_custom_call" | custom-call | flops 1342177280 | bytes 2097152 | tf_op jit(solution)/shard_map/near_stage/pallas_call | solution.py:410
  61.5 0.0 collective-permute-done.8.rest_0_.q
  61.5 4.5 %near_stage.4 = (f32[2,4,256,128]{3,2,1,0:T(8,128)}, bf16[2,4,256,128]{3,2,1,0:T(8,128)(2,1)}) custom-call(s32[1]{0:T(128)} %bitcast.z, f32[16]{0:T(128)S(1)} %copy-done.9, bf16[4,4,128,128]{3,2,1,0:T(8,128)(2,1)S(1)} %copy-done.15, bf16[256,128]{1,0:T(8,128)(2,1)S(1)} %copy-done.16, bf16[256,128]{1,0:T(8,128)(2,1)S(1)} %collective-permute-done.3.s1, ...), custom_call_target="tpu_custom_call" | custom-call | flops 1342177280 | bytes 2097152 | tf_op jit(solution)/shard_map/near_stage/pallas_call | solution.py:410
  66.0 0.0 collective-permute-done.6.rest_0_.q
  66.0 0.0 collective-permute-done.7.rest_1_.q
  66.0 8.3 %near_stage.5 = (f32[2,4,256,128]{3,2,1,0:T(8,128)}, bf16[2,4,256,128]{3,2,1,0:T(8,128)(2,1)}, f32[2,4,256,128]{3,2,1,0:T(8,128)}, bf16[2,4,256,128]{3,2,1,0:T(8,128)(2,1)}) custom-call(s32[1]{0:T(128)} %bitcast.z, f32[16]{0:T(128)S(1)} %copy-done.9, bf16[4,4,128,128]{3,2,1,0:T(8,128)(2,1)S(1)} %copy-done.15, bf16[256,128]{1,0:T(8,128)(2,1)S(1)} %copy-done.16, ...), custom_call_target="tpu_custom_call" | custom-call | flops 2684354560 | bytes 2097152 | tf_op jit(solution)/shard_map/near_stage/pallas_call | solution.py:410
  74.3 0.0 all-to-all-done.1
  74.3 1.2 %copy-done.2 = f32[2,4,256,128]{3,2,1,0:T(8,128)S(1)} copy-done((f32[2,4,256,128]{3,2,1,0:T(8,128)S(1)}, f32[2,4,256,128]{3,2,1,0:T(8,128)}, u32[]{:S(2)}) %copy-start.2) | copy-done | bytes 1048600
  75.6 1.0 copy-done.6
  76.6 2.3 %far_stage.7 = bf16[512,256]{1,0:T(8,128)(2,1)S(1)} custom-call(s32[1]{0:T(128)} %bitcast.z, s32[16,4]{1,0:T(8,128)S(1)} %get-tuple-element.30.slots, f32[16]{0:T(128)S(1)} %copy-done.9, bf16[512,256]{1,0:T(8,128)(2,1)S(1)} %collective-permute-done.6.rest_0_.q, f32[2,4,256,128]{3,2,1,0:T(8,128)S(1)} %copy-done.2, bf16[2,4,256,128]{3,2,1,0:T(8,128)(2,1)S(1)} %copy-done.6, ...), custom_call_target="tpu_custom_call" | custom-call | flops 536870912 | bytes 4194304 | tf_op jit(solution)/shard_map/far_stage/pallas_call | solution.py:523
  79.0 1.0 collective-permute-start.11
  80.0 3.5 %far_stage.6 = bf16[512,256]{1,0:T(8,128)(2,1)S(1)} custom-call(s32[1]{0:T(128)} %bitcast.z, s32[16,4]{1,0:T(8,128)S(1)} %get-tuple-element.30.slots, f32[16]{0:T(128)S(1)} %copy-done.9, bf16[512,256]{1,0:T(8,128)(2,1)S(1)} %collective-permute-done.7.rest_1_.q, f32[2,4,256,128]{3,2,1,0:T(8,128)} %get-tuple-element.51.rest_0_.state, ...), custom_call_target="tpu_custom_call" | custom-call | flops 536870912 | bytes 4194304 | tf_op jit(solution)/shard_map/far_stage/pallas_call | solution.py:523
  83.5 0.0 copy-start
  83.5 2.4 %collective-permute-start.10 = (bf16[512,256]{1,0:T(8,128)(2,1)S(1)}, bf16[512,256]{1,0:T(8,128)(2,1)S(1)}, u32[]{:S(2)}, u32[]{:S(2)}) collective-permute-start(bf16[512,256]{1,0:T(8,128)(2,1)S(1)} %far_stage.6), channel_id=1, source_target_pairs={{0,2},{1,3},{2,0},{3,1},{4,6},{5,7},{6,4},{7,5},{8,10},{9,11},{10,... | collective-permute-start | bytes 786440 | tf_op jit(solution)/shard_map/ppermute | solution.py:578
  85.9 2.3 %far_stage.5 = bf16[512,256]{1,0:T(8,128)(2,1)S(1)} custom-call(s32[1]{0:T(128)} %bitcast.z, s32[16,4]{1,0:T(8,128)S(1)} %get-tuple-element.30.slots, f32[16]{0:T(128)S(1)} %copy-done.9, bf16[512,256]{1,0:T(8,128)(2,1)S(1)} %collective-permute-done.8.rest_0_.q, f32[2,4,256,128]{3,2,1,0:T(8,128)S(1)} %copy-done.1, bf16[2,4,256,128]{3,2,1,0:T(8,128)(2,1)S(1)} %copy-done.5, ...), custom_call_target="tpu_custom_call" | custom-call | flops 536870912 | bytes 4194304 | tf_op jit(solution)/shard_map/far_stage/pallas_call | solution.py:523
  88.3 0.0 copy-start.3
  88.3 0.0 copy-start.11
  88.3 1.7 %collective-permute-start.9 = (bf16[512,256]{1,0:T(8,128)(2,1)S(1)}, bf16[512,256]{1,0:T(8,128)(2,1)S(1)}, u32[]{:S(2)}, u32[]{:S(2)}) collective-permute-start(bf16[512,256]{1,0:T(8,128)(2,1)S(1)} %far_stage.5), channel_id=1, source_target_pairs={{0,3},{1,0},{2,1},{3,2},{4,7},{5,4},{6,5},{7,6},{8,11},{9,8},{10,9... | collective-permute-start | bytes 786440 | tf_op jit(solution)/shard_map/ppermute | solution.py:578
  90.0 2.3 %far_stage.4.a0 = bf16[512,256]{1,0:T(8,128)(2,1)S(1)} custom-call(s32[1]{0:T(128)} %bitcast.z, s32[16,4]{1,0:T(8,128)S(1)} %get-tuple-element.30.slots, f32[16]{0:T(128)S(1)} %copy-done.9, bf16[512,256]{1,0:T(8,128)(2,1)S(1)} %copy-done.8, f32[2,4,256,128]{3,2,1,0:T(8,128)S(1)} %copy-done, bf16[2,4,256,128]{3,2,1,0:T(8,128)(2,1)S(1)} %copy-done.4, ...), custom_call_target="tpu_custom_call" | custom-call | flops 536870912 | bytes 4194304 | tf_op jit(solution)/shard_map/far_stage/pallas_call | solution.py:523
  92.4 1.4 %collective-permute-done.11.a3 = bf16[512,256]{1,0:T(8,128)(2,1)S(1)} collective-permute-done((bf16[512,256]{1,0:T(8,128)(2,1)S(1)}, bf16[512,256]{1,0:T(8,128)(2,1)S(1)}, u32[]{:S(2)}, u32[]{:S(2)}) %collective-permute-start.11) | collective-permute-done | bytes 262176 | tf_op jit(solution)/shard_map/ppermute | solution.py:578
  93.7 0.0 collective-permute-done.10.a2
  93.7 4.2 %collective-permute-done.9.a1 = bf16[512,256]{1,0:T(8,128)(2,1)S(1)} collective-permute-done((bf16[512,256]{1,0:T(8,128)(2,1)S(1)}, bf16[512,256]{1,0:T(8,128)(2,1)S(1)}, u32[]{:S(2)}, u32[]{:S(2)}) %collective-permute-start.9) | collective-permute-done | bytes 262176 | tf_op jit(solution)/shard_map/ppermute | solution.py:578
  97.9 9.1 %ffn_stage.1 = bf16[512,1024]{1,0:T(8,128)(2,1)} custom-call(s32[1]{0:T(128)} %bitcast.z, bf16[512,1024]{1,0:T(8,128)(2,1)S(1)} %copy-done.3, bf16[512,256]{1,0:T(8,128)(2,1)S(1)} %far_stage.4.a0, bf16[512,256]{1,0:T(8,128)(2,1)S(1)} %collective-permute-done.9.a1, bf16[512,256]{1,0:T(8,128)(2,1)S(1)} %collective-permute-done.10.a2, ...), custom_call_target="tpu_custom_call" | custom-call | flops 7516192768 | bytes 18874368 | tf_op jit(solution)/shard_map/ffn_stage/pallas_call | solution.py:565
  (31 shorter events, 0.1 us)
Async XLA Ops:
  0.0 0.7 copy-start.10
  6.3 19.5 %all-to-all-start = ((bf16[32,48,128]{2,1,0:T(8,128)(2,1)}), bf16[32,48,128]{2,1,0:T(8,128)(2,1)S(1)}, u32[]{:S(2)}, u32[]{:S(2)}) async-start(bf16[32,48,128]{2,1,0:T(8,128)(2,1)} %get-tuple-element.33), calls=%async_computation | async-start | bytes 786432 | tf_op jit(solution)/shard_map/all_to_all | solution.py:585
  13.7 8.0 %collective-permute-start = (bf16[512,128]{1,0:T(8,128)(2,1)S(1)}, bf16[512,128]{1,0:T(8,128)(2,1)S(1)}, u32[]{:S(2)}, u32[]{:S(2)}) collective-permute-start(bf16[512,128]{1,0:T(8,128)(2,1)S(1)} %get-tuple-element.35), channel_id=1, source_target_pairs={{0,1},{1,2},{2,3},{3,0},{4,5},{5,6},{6,7},{7,4},{8,9},{9,10},{10,1... | collective-permute-start | bytes 393224 | tf_op jit(solution)/shard_map/ppermute | solution.py:578
  15.7 10.0 %collective-permute-start.1 = (bf16[512,128]{1,0:T(8,128)(2,1)S(1)}, bf16[512,128]{1,0:T(8,128)(2,1)S(1)}, u32[]{:S(2)}, u32[]{:S(2)}) collective-permute-start(bf16[512,128]{1,0:T(8,128)(2,1)S(1)} %get-tuple-element.36), channel_id=1, source_target_pairs={{0,2},{1,3},{2,0},{3,1},{4,6},{5,7},{6,4},{7,5},{8,10},{9,11},{10,... | collective-permute-start | bytes 393224 | tf_op jit(solution)/shard_map/ppermute | solution.py:578
  19.3 6.5 %collective-permute-start.2 = (bf16[512,128]{1,0:T(8,128)(2,1)S(1)}, bf16[512,128]{1,0:T(8,128)(2,1)S(1)}, u32[]{:S(2)}, u32[]{:S(2)}) collective-permute-start(bf16[512,128]{1,0:T(8,128)(2,1)S(1)} %get-tuple-element.37), channel_id=1, source_target_pairs={{0,3},{1,0},{2,1},{3,2},{4,7},{5,4},{6,5},{7,6},{8,11},{9,8},{10,9... | collective-permute-start | bytes 393224 | tf_op jit(solution)/shard_map/ppermute | solution.py:578
  29.4 44.9 %all-to-all-start.1 = ((bf16[32,256,128]{2,1,0:T(8,128)(2,1)}), bf16[32,256,128]{2,1,0:T(8,128)(2,1)S(1)}, u32[]{:S(2)}, u32[]{:S(2)}) async-start(bf16[32,256,128]{2,1,0:T(8,128)(2,1)} %bitcast.9), calls=%async_computation.1 | async-start | bytes 4194304 | tf_op jit(solution)/shard_map/all_to_all | solution.py:589
  36.6 7.4 %copy-start.19 = (bf16[256,128]{1,0:T(8,128)(2,1)S(1)}, bf16[256,128]{1,0:T(8,128)(2,1)}, u32[]{:S(2)}) copy-start(bf16[256,128]{1,0:T(8,128)(2,1)} %get-tuple-element.40) | copy-start | bytes 196612
  36.6 8.4 %copy-start.18 = (bf16[256,128]{1,0:T(8,128)(2,1)S(1)}, bf16[256,128]{1,0:T(8,128)(2,1)}, u32[]{:S(2)}) copy-start(bf16[256,128]{1,0:T(8,128)(2,1)} %get-tuple-element.41) | copy-start | bytes 196612
  36.7 10.9 %copy-start.17 = (bf16[256,128]{1,0:T(8,128)(2,1)S(1)}, bf16[256,128]{1,0:T(8,128)(2,1)}, u32[]{:S(2)}) copy-start(bf16[256,128]{1,0:T(8,128)(2,1)} %get-tuple-element.42) | copy-start | bytes 196612
  36.7 19.3 %copy-start.9 = (f32[16]{0:T(128)S(1)}, f32[16]{0:T(128)}, u32[]{:S(2)}) copy-start(f32[16]{0:T(128)} %scale.13) | copy-start | bytes 196
  36.7 19.3 %copy-start.15 = (bf16[4,4,128,128]{3,2,1,0:T(8,128)(2,1)S(1)}, bf16[4,4,128,128]{3,2,1,0:T(8,128)(2,1)}, u32[]{:S(2)}) copy-start(bf16[4,4,128,128]{3,2,1,0:T(8,128)(2,1)} %get-tuple-element.38.kv) | copy-start | bytes 1572868
  36.7 19.3 %copy-start.16 = (bf16[256,128]{1,0:T(8,128)(2,1)S(1)}, bf16[256,128]{1,0:T(8,128)(2,1)}, u32[]{:S(2)}) copy-start(bf16[256,128]{1,0:T(8,128)(2,1)} %get-tuple-element.39.s0) | copy-start | bytes 196612
  42.8 18.7 %collective-permute-start.8 = (bf16[512,256]{1,0:T(8,128)(2,1)}, bf16[512,256]{1,0:T(8,128)(2,1)S(1)}, u32[]{:S(2)}, u32[]{:S(2)}) collective-permute-start(bf16[512,256]{1,0:T(8,128)(2,1)} %get-tuple-element.48), channel_id=1, source_target_pairs={{0,1},{1,2},{2,3},{3,0},{4,5},{5,6},{6,7},{7,4},{8,9},{9,10},{10,1... | collective-permute-start | bytes 786440 | tf_op jit(solution)/shard_map/ppermute | solution.py:578
  44.1 10.4 %collective-permute-start.3 = (bf16[256,128]{1,0:T(8,128)(2,1)S(1)}, bf16[256,128]{1,0:T(8,128)(2,1)S(1)}, u32[]{:S(2)}, u32[]{:S(2)}) collective-permute-start(bf16[256,128]{1,0:T(8,128)(2,1)S(1)} %copy-done.19), channel_id=1, source_target_pairs={{0,1},{1,2},{2,3},{3,0},{4,5},{5,6},{6,7},{7,4},{8,9},{9,10},{10,1... | collective-permute-start | bytes 196616 | tf_op jit(solution)/shard_map/ppermute | solution.py:578
  45.1 10.9 %collective-permute-start.4 = (bf16[256,128]{1,0:T(8,128)(2,1)S(1)}, bf16[256,128]{1,0:T(8,128)(2,1)S(1)}, u32[]{:S(2)}, u32[]{:S(2)}) collective-permute-start(bf16[256,128]{1,0:T(8,128)(2,1)S(1)} %copy-done.18), channel_id=1, source_target_pairs={{0,2},{1,3},{2,0},{3,1},{4,6},{5,7},{6,4},{7,5},{8,10},{9,11},{10,... | collective-permute-start | bytes 196616 | tf_op jit(solution)/shard_map/ppermute | solution.py:578
  47.6 8.4 %collective-permute-start.5 = (bf16[256,128]{1,0:T(8,128)(2,1)S(1)}, bf16[256,128]{1,0:T(8,128)(2,1)S(1)}, u32[]{:S(2)}, u32[]{:S(2)}) collective-permute-start(bf16[256,128]{1,0:T(8,128)(2,1)S(1)} %copy-done.17), channel_id=1, source_target_pairs={{0,3},{1,0},{2,1},{3,2},{4,7},{5,4},{6,5},{7,6},{8,11},{9,8},{10,9... | collective-permute-start | bytes 196616 | tf_op jit(solution)/shard_map/ppermute | solution.py:578
  49.1 16.9 %collective-permute-start.6 = (bf16[512,256]{1,0:T(8,128)(2,1)}, bf16[512,256]{1,0:T(8,128)(2,1)S(1)}, u32[]{:S(2)}, u32[]{:S(2)}) collective-permute-start(bf16[512,256]{1,0:T(8,128)(2,1)} %get-tuple-element.46), channel_id=1, source_target_pairs={{0,3},{1,0},{2,1},{3,2},{4,7},{5,4},{6,5},{7,6},{8,11},{9,8},{10,9... | collective-permute-start | bytes 786440 | tf_op jit(solution)/shard_map/ppermute | solution.py:578
  54.5 11.6 %collective-permute-start.7 = (bf16[512,256]{1,0:T(8,128)(2,1)}, bf16[512,256]{1,0:T(8,128)(2,1)S(1)}, u32[]{:S(2)}, u32[]{:S(2)}) collective-permute-start(bf16[512,256]{1,0:T(8,128)(2,1)} %get-tuple-element.47), channel_id=1, source_target_pairs={{0,2},{1,3},{2,0},{3,1},{4,6},{5,7},{6,4},{7,5},{8,10},{9,11},{10,... | collective-permute-start | bytes 786440 | tf_op jit(solution)/shard_map/ppermute | solution.py:578
  56.0 1.0 copy-start.7
  74.3 1.2 %copy-start.2 = (f32[2,4,256,128]{3,2,1,0:T(8,128)S(1)}, f32[2,4,256,128]{3,2,1,0:T(8,128)}, u32[]{:S(2)}) copy-start(f32[2,4,256,128]{3,2,1,0:T(8,128)} %get-tuple-element.53.state) | copy-start | bytes 3145732
  75.6 1.0 copy-start.6
  76.6 21.3 %copy-start.13 = (bf16[2048,1024]{1,0:T(8,128)(2,1)S(1)}, bf16[2048,1024]{1,0:T(8,128)(2,1)}, u32[]{:S(2)}) copy-start(bf16[2048,1024]{1,0:T(8,128)(2,1)} %w_down.1) | copy-start | bytes 12582916
  79.0 7.0 %copy-start.1 = (f32[2,4,256,128]{3,2,1,0:T(8,128)S(1)}, f32[2,4,256,128]{3,2,1,0:T(8,128)}, u32[]{:S(2)}) copy-start(f32[2,4,256,128]{3,2,1,0:T(8,128)} %get-tuple-element.49.rest_2_.state) | copy-start | bytes 3145732
  79.0 7.0 %copy-start.5 = (bf16[2,4,256,128]{3,2,1,0:T(8,128)(2,1)S(1)}, bf16[2,4,256,128]{3,2,1,0:T(8,128)(2,1)}, u32[]{:S(2)}) copy-start(bf16[2,4,256,128]{3,2,1,0:T(8,128)(2,1)} %get-tuple-element.50.rest_3_.peaks) | copy-start | bytes 1572868
  79.0 14.8 %collective-permute-start.11 = (bf16[512,256]{1,0:T(8,128)(2,1)S(1)}, bf16[512,256]{1,0:T(8,128)(2,1)S(1)}, u32[]{:S(2)}, u32[]{:S(2)}) collective-permute-start(bf16[512,256]{1,0:T(8,128)(2,1)S(1)} %far_stage.7), channel_id=1, source_target_pairs={{0,1},{1,2},{2,3},{3,0},{4,5},{5,6},{6,7},{7,4},{8,9},{9,10},{10,1... | collective-permute-start | bytes 786440 | tf_op jit(solution)/shard_map/ppermute | solution.py:578
  80.0 17.9 %copy-start.14 = (bf16[1024,1024]{1,0:T(8,128)(2,1)S(1)}, bf16[1024,1024]{1,0:T(8,128)(2,1)}, u32[]{:S(2)}) copy-start(bf16[1024,1024]{1,0:T(8,128)(2,1)} %w_out.1) | copy-start | bytes 6291460
  83.5 6.5 %copy-start = (f32[2,4,256,128]{3,2,1,0:T(8,128)S(1)}, f32[2,4,256,128]{3,2,1,0:T(8,128)}, u32[]{:S(2)}) copy-start(f32[2,4,256,128]{3,2,1,0:T(8,128)} %get-tuple-element.43.rest_1_.state) | copy-start | bytes 3145732
  83.5 6.5 %copy-start.4 = (bf16[2,4,256,128]{3,2,1,0:T(8,128)(2,1)S(1)}, bf16[2,4,256,128]{3,2,1,0:T(8,128)(2,1)}, u32[]{:S(2)}) copy-start(bf16[2,4,256,128]{3,2,1,0:T(8,128)(2,1)} %get-tuple-element.44.rest_2_.peaks) | copy-start | bytes 1572868
  83.5 6.5 %copy-start.8 = (bf16[512,256]{1,0:T(8,128)(2,1)S(1)}, bf16[512,256]{1,0:T(8,128)(2,1)}, u32[]{:S(2)}) copy-start(bf16[512,256]{1,0:T(8,128)(2,1)} %get-tuple-element.32.rest_0_.q) | copy-start | bytes 786436
  83.5 10.2 %collective-permute-start.10 = (bf16[512,256]{1,0:T(8,128)(2,1)S(1)}, bf16[512,256]{1,0:T(8,128)(2,1)S(1)}, u32[]{:S(2)}, u32[]{:S(2)}) collective-permute-start(bf16[512,256]{1,0:T(8,128)(2,1)S(1)} %far_stage.6), channel_id=1, source_target_pairs={{0,2},{1,3},{2,0},{3,1},{4,6},{5,7},{6,4},{7,5},{8,10},{9,11},{10,... | collective-permute-start | bytes 786440 | tf_op jit(solution)/shard_map/ppermute | solution.py:578
  85.9 12.0 %copy-start.12 = (bf16[1024,2048]{1,0:T(8,128)(2,1)S(1)}, bf16[1024,2048]{1,0:T(8,128)(2,1)}, u32[]{:S(2)}) copy-start(bf16[1024,2048]{1,0:T(8,128)(2,1)} %w_up.1) | copy-start | bytes 12582916
  88.3 9.6 %copy-start.3 = (bf16[512,1024]{1,0:T(8,128)(2,1)S(1)}, bf16[512,1024]{1,0:T(8,128)(2,1)}, u32[]{:S(2)}) copy-start(bf16[512,1024]{1,0:T(8,128)(2,1)} %tokens.1) | copy-start | bytes 3145732
  88.3 9.6 %copy-start.11 = (bf16[1024,2048]{1,0:T(8,128)(2,1)S(1)}, bf16[1024,2048]{1,0:T(8,128)(2,1)}, u32[]{:S(2)}) copy-start(bf16[1024,2048]{1,0:T(8,128)(2,1)} %w_gate.1) | copy-start | bytes 12582916
  88.3 9.6 %collective-permute-start.9 = (bf16[512,256]{1,0:T(8,128)(2,1)S(1)}, bf16[512,256]{1,0:T(8,128)(2,1)S(1)}, u32[]{:S(2)}, u32[]{:S(2)}) collective-permute-start(bf16[512,256]{1,0:T(8,128)(2,1)S(1)} %far_stage.5), channel_id=1, source_target_pairs={{0,3},{1,0},{2,1},{3,2},{4,7},{5,4},{6,5},{7,6},{8,11},{9,8},{10,9... | collective-permute-start | bytes 786440 | tf_op jit(solution)/shard_map/ppermute | solution.py:578

commit v4 on v3

--- a/solution.py
+++ b/solution.py
@@ -86,9 +86,9 @@
 
 
 def first_body(
-    z, picks, tokens_in, key_in, value_in,
+    z, picks_in, tokens_in, key_in, value_in,
     c0, c1, c2, c3, payload_out, normed_out, slots,
-    table, tokens, w_key, w_value, normed, pairs, payload, sems, out_sems,
+    table, tokens, w_key, w_value, normed, keys_held, values_held, pairs, payload, picks, sems, out_sem,
 ):
     rows_n = ROWS // STEPS
     weight_copies = [
@@ -103,6 +103,8 @@
         )
         for i in range(STEPS)
     ]
+    picks_copy = pltpu.make_async_copy(picks_in, picks, out_sem.at[1])
+    picks_copy.start()
     token_copies[0].start()
     weight_copies[0].start()
     weight_copies[1].start()
@@ -127,19 +129,19 @@
         slots[row, col] = owner * CAP + slot
         return 0
 
+    picks_copy.wait()
     lax.fori_loop(0, BLK_DEV * PICKS, assign, 0, unroll=4)
 
     ones = head_ones(GROUP_W)
-    key_means, value_means, outs = [], [], []
+    key_means, value_means = [], []
     for i in range(STEPS):
         rows = pl.ds(i * rows_n, rows_n)
         token_copies[i].wait()
         here = row_norm(tokens[rows].astype(f32)).astype(bf16)
         normed[rows] = here
-        outs.append(
-            pltpu.make_async_copy(normed.at[rows], normed_out.at[rows], out_sems.at[i])
-        )
-        outs[-1].start()
+        if i == STEPS - 1:
+            normed_copy = pltpu.make_async_copy(normed, normed_out, out_sem.at[2])
+            normed_copy.start()
         if i == 0:
             weight_copies[0].wait()
         keys = jnp.dot(here, w_key[...], preferred_element_type=f32)
@@ -150,11 +152,8 @@
         runs = (rows_n // CMP, CMP, GROUP_W)
         key_means.append(jnp.mean(keys.astype(f32).reshape(runs), axis=1))
         value_means.append(jnp.mean(values.astype(f32).reshape(runs), axis=1))
-        for g in range(KV_HEADS):
-            lanes = slice(g * HEAD_DIM, (g + 1) * HEAD_DIM)
-            pairs[g, rows] = jnp.concatenate([keys[:, lanes], values[:, lanes]], axis=1)
-    for k, c in enumerate((c0, c1, c2, c3)):
-        c[...] = pairs[(z[0] + k) % ZS]
+        keys_held[rows] = keys
+        values_held[rows] = values
     summary_key = head_norm(jnp.concatenate(key_means, axis=0), ones)
     summary_value = jnp.concatenate(value_means, axis=0)
     summary = jnp.concatenate(
@@ -176,10 +175,15 @@
         first = jnp.maximum(table[o * CAP], 0)
         second = jnp.maximum(table[o * CAP + 1], 0)
         payload[o, SUM_ROWS:, :] = jnp.where(lane == 0, first, second).astype(f32).astype(bf16)
-    outs.append(pltpu.make_async_copy(payload, payload_out, out_sems.at[STEPS]))
-    outs[-1].start()
-    for c in outs:
-        c.wait()
+    told = pltpu.make_async_copy(payload, payload_out, out_sem.at[0])
+    told.start()
+    for g in range(KV_HEADS):
+        lanes = slice(g * HEAD_DIM, (g + 1) * HEAD_DIM)
+        pairs[g] = jnp.concatenate([keys_held[:, lanes], values_held[:, lanes]], axis=1)
+    for k, c in enumerate((c0, c1, c2, c3)):
+        c[...] = pairs[(z[0] + k) % ZS]
+    told.wait()
+    normed_copy.wait()
 
 
 def first_stage(z, picks, tokens, w_key, w_value):
@@ -187,8 +191,8 @@
     return pl.pallas_call(
         first_body,
         name="first_stage",
-        in_specs=[whole(SMEM), whole(SMEM), hbm, hbm, hbm],
-        out_specs=[whole(VMEM)] * ZS + [hbm] * 2 + [whole(SMEM)],
+        in_specs=[whole(SMEM)] + [hbm] * 4,
+        out_specs=[whole(VMEM)] * ZS + [hbm, hbm, whole(SMEM)],
         out_shape=[VMEM((ROWS, PAIR_W), bf16)] * ZS
         + [
             pltpu.HBM((PTS, PAY_ROWS, PAIR_W), bf16),
@@ -201,33 +205,46 @@
             VMEM((1024, GROUP_W), bf16),
             VMEM((1024, GROUP_W), bf16),
             VMEM((ROWS, 1024), bf16),
+            VMEM((ROWS, GROUP_W), bf16),
+            VMEM((ROWS, GROUP_W), bf16),
             VMEM((KV_HEADS, ROWS, PAIR_W), bf16),
             VMEM((PTS, PAY_ROWS, PAIR_W), bf16),
+            SMEM((PICKS, BLK_DEV), jnp.int32),
             pltpu.SemaphoreType.DMA((2 + STEPS,)),
-            pltpu.SemaphoreType.DMA((STEPS + 1,)),
+            pltpu.SemaphoreType.DMA((3,)),
         ],
         compiler_params=params(16),
         cost_estimate=cost(2 * ROWS * 1024 * 512, 4 << 20),
-    )(z, picks, *[far_core(a) for a in (tokens, w_key, w_value)])
-
-
-def q_body(z, normed_in, query_in, q0, q1, q2, q3, normed, w_query, queries, sems, out_sems):
-    def columns(k):
-        return pl.ds(pl.multiple_of(((z[0] + k) % ZS) * GROUP_W, GROUP_W), GROUP_W)
-
-    ins = [pltpu.make_async_copy(normed_in, normed, sems.at[ZS])]
-    for k in range(ZS):
-        ins.append(pltpu.make_async_copy(query_in.at[:, columns(k)], w_query.at[k], sems.at[k]))
+    )(z, *[far_core(a) for a in (picks, tokens, w_key, w_value)])
+
+
+def q_body(z, normed_in, w_query, q0, q1, q2, q3, normed, raw, queries, sems):
+    half = ROWS // 2
+    ins = [
+        pltpu.make_async_copy(
+            normed_in.at[pl.ds(i * half, half)], normed.at[pl.ds(i * half, half)], sems.at[ZS + i]
+        )
+        for i in range(2)
+    ]
     for c in ins:
         c.start()
     ones = head_ones(GROUP_W)
-    ins[0].wait()
+
+    def project(k, rows):
+        start = pl.multiple_of(((z[0] + k) % ZS) * GROUP_W, GROUP_W)
+        raw[k % 2, rows] = jnp.dot(
+            normed[rows], w_query[:, pl.ds(start, GROUP_W)], preferred_element_type=f32
+        )
+
+    for i in range(2):
+        ins[i].wait()
+        project(0, slice(i * half, (i + 1) * half))
     outs = []
     for k, out in enumerate((q0, q1, q2, q3)):
-        ins[k + 1].wait()
-        raw = jnp.dot(normed[...], w_query[k], preferred_element_type=f32)
-        queries[k] = head_norm(raw, ones).astype(bf16)
-        outs.append(pltpu.make_async_copy(queries.at[k], out, out_sems.at[k]))
+        if k + 1 < ZS:
+            project(k + 1, slice(0, ROWS))
+        queries[k] = head_norm(raw[k % 2], ones).astype(bf16)
+        outs.append(pltpu.make_async_copy(queries.at[k], out, sems.at[k]))
         outs[-1].start()
     for c in outs:
         c.wait()
@@ -238,19 +255,18 @@
     return pl.pallas_call(
         q_body,
         name="q_stage",
-        in_specs=[whole(SMEM), hbm, hbm],
+        in_specs=[whole(SMEM), hbm, whole(VMEM)],
         out_specs=[hbm] * ZS,
         out_shape=[pltpu.HBM((ROWS, GROUP_W), bf16)] * ZS,
         scratch_shapes=[
             VMEM((ROWS, 1024), bf16),
-            VMEM((ZS, 1024, GROUP_W), bf16),
+            VMEM((2, ROWS, GROUP_W), f32),
             VMEM((ZS, ROWS, GROUP_W), bf16),
-            pltpu.SemaphoreType.DMA((ZS + 1,)),
-            pltpu.SemaphoreType.DMA((ZS,)),
+            pltpu.SemaphoreType.DMA((ZS + 2,)),
         ],
-        compiler_params=params(16),
+        compiler_params=params(12),
         cost_estimate=cost(2 * ROWS * 1024 * 1024, 4 << 20),
-    )(z, far_core(normed), far_core(w_query))
+    )(z, far_core(normed), near_core(w_query))
 
 
 def reply_body(

time: 107 us -> 107 us (level)
  Pallas kernels: 52.2 us -> 50.5 us
    pallas_call x2, Pallas kernels: 11.7 us -> 9.95 us  [the longest x1 5.79 us: first_stage(): pl.pallas_call(first_body, name='first_stage', in_specs=[whole(SMEM)] + [...]
  transfers between devices with their start and end apart: 14 -> 14, of which waited for: 6 -> 6; matrix products, arithmetic and copies ran while one was open for 0% -> 0% of each run, Pallas kernels for 30% -> 28%
where the time goes in v4:
time: 107 us; the launch traced here: 106 us
  Pallas kernels  50.5 us (47%)
  starting transfers between devices  33.6 us (31%)
  waiting for transfers between devices  16.9 us (16%)
  local copies, waits for them, and re-layouts  4.86 us (5%)
    ppermute x12, starting transfers between devices, shift(): return lax.ppermute(array, 'head', [(i, (i + k) % ZS) for i in range(ZS)])  18.9 us
    pallas_call x3, Pallas kernels, near_stage(): pl.pallas_call(functools.partial(near_body, chunks), name='near_stage', i...  17.3 us
    ppermute x12, waiting for transfers between devices, shift(): return lax.ppermute(array, 'head', [(i, (i + k) % ZS) for i in range(ZS)])  16.9 us
    pallas_call x4, Pallas kernels, far_stage(): pl.pallas_call(functools.partial(far_body, shift_by, direct), name='far_s...  10.5 us
    pallas_call x1, Pallas kernels, ffn_stage(): pl.pallas_call(ffn_body, name='ffn_stage', in_specs=[whole(SMEM)] + [whol...  9.08 us
    all_to_all x1, starting transfers between devices, body(): lax.all_to_all(payload, 'pts', split_axis=0, concat_axis=0, tiled=True)  7.44 us
    all_to_all x1, starting transfers between devices, body(): lax.all_to_all(replies, 'pts', split_axis=0, concat_axis=0, tiled=True)  7.24 us
    pallas_call x1, Pallas kernels, first_stage(): pl.pallas_call(first_body, name='first_stage', in_specs=[whole(SMEM)] + [...  5.79 us
  transfers between devices with their start and end apart: 14, of which 6 were waited for; matrix products, arithmetic and copies ran while one was open for 0% of the time, Pallas kernels for 28%

profile of v4, /device:TPU:0, one launch (start us, length us, event | category | flops | bytes accessed | tf_op | source)
XLA Modules:
  0.0 106.2 jit_solution(11962671022194761856)
XLA Ops:
  0.0 5.8 %first_stage.1 = (bf16[512,128]{1,0:T(8,128)(2,1)S(1)}, bf16[512,128]{1,0:T(8,128)(2,1)S(1)}, bf16[512,128]{1,0:T(8,128)(2,1)S(1)}, bf16[512,128]{1,0:T(8,128)(2...) custom-call(s32[1]{0:T(128)} %bitcast.z, s32[4,16]{1,0:T(4,128)} %bitcast.9, ...), custom_call_target="tpu_custom_call" | custom-call | flops 536870912 | bytes 4194304 | tf_op jit(solution)/shard_map/first_stage/pallas_call | solution.py:191
  5.8 7.4 %all-to-all-start = ((bf16[32,48,128]{2,1,0:T(8,128)(2,1)}), bf16[32,48,128]{2,1,0:T(8,128)(2,1)S(1)}, u32[]{:S(2)}, u32[]{:S(2)}) async-start(bf16[32,48,128]{2,1,0:T(8,128)(2,1)} %get-tuple-element.33), calls=%async_computation | async-start | bytes 786432 | tf_op jit(solution)/shard_map/all_to_all | solution.py:601
  13.2 2.0 %collective-permute-start = (bf16[512,128]{1,0:T(8,128)(2,1)S(1)}, bf16[512,128]{1,0:T(8,128)(2,1)S(1)}, u32[]{:S(2)}, u32[]{:S(2)}) collective-permute-start(bf16[512,128]{1,0:T(8,128)(2,1)S(1)} %get-tuple-element.35), channel_id=1, source_target_pairs={{0,1},{1,2},{2,3},{3,0},{4,5},{5,6},{6,7},{7,4},{8,9},{9,10},{10,1... | collective-permute-start | bytes 393224 | tf_op jit(solution)/shard_map/ppermute | solution.py:594
  15.2 3.6 %collective-permute-start.1 = (bf16[512,128]{1,0:T(8,128)(2,1)S(1)}, bf16[512,128]{1,0:T(8,128)(2,1)S(1)}, u32[]{:S(2)}, u32[]{:S(2)}) collective-permute-start(bf16[512,128]{1,0:T(8,128)(2,1)S(1)} %get-tuple-element.36), channel_id=1, source_target_pairs={{0,2},{1,3},{2,0},{3,1},{4,6},{5,7},{6,4},{7,5},{8,10},{9,11},{10,... | collective-permute-start | bytes 393224 | tf_op jit(solution)/shard_map/ppermute | solution.py:594
  18.8 1.0 collective-permute-start.2
  19.8 1.5 %collective-permute-done.c1 = bf16[512,128]{1,0:T(8,128)(2,1)S(1)} collective-permute-done((bf16[512,128]{1,0:T(8,128)(2,1)S(1)}, bf16[512,128]{1,0:T(8,128)(2,1)S(1)}, u32[]{:S(2)}, u32[]{:S(2)}) %collective-permute-start) | collective-permute-done | bytes 131104 | tf_op jit(solution)/shard_map/ppermute | solution.py:594
  21.3 4.0 %collective-permute-done.1.c2 = bf16[512,128]{1,0:T(8,128)(2,1)S(1)} collective-permute-done((bf16[512,128]{1,0:T(8,128)(2,1)S(1)}, bf16[512,128]{1,0:T(8,128)(2,1)S(1)}, u32[]{:S(2)}, u32[]{:S(2)}) %collective-permute-start.1) | collective-permute-done | bytes 131104 | tf_op jit(solution)/shard_map/ppermute | solution.py:594
  25.3 0.0 collective-permute-done.2.c3
  25.3 0.0 all-to-all-done.told
  25.3 3.6 %reply_stage.1 = (bf16[64,128,128]{2,1,0:T(8,128)(2,1)}, bf16[256,128]{1,0:T(8,128)(2,1)}, bf16[256,128]{1,0:T(8,128)(2,1)}, bf16[256,128]{1,0:T(8,128)(2,1)}, b...) custom-call(s32[1]{0:T(128)} %bitcast.z, bf16[32,48,128]{2,1,0:T(8,128)(2,1)S(1)} %all-to-all-done.told, ...), custom_call_target="tpu_custom_call" | custom-call | tf_op jit(solution)/shard_map/reply_stage/pallas_call | solution.py:310
  28.9 7.2 %all-to-all-start.1 = ((bf16[32,256,128]{2,1,0:T(8,128)(2,1)}), bf16[32,256,128]{2,1,0:T(8,128)(2,1)S(1)}, u32[]{:S(2)}, u32[]{:S(2)}) async-start(bf16[32,256,128]{2,1,0:T(8,128)(2,1)} %bitcast.8), calls=%async_computation.1 | async-start | bytes 4194304 | tf_op jit(solution)/shard_map/all_to_all | solution.py:605
  36.2 0.0 copy-start.9
  36.2 0.0 copy-start.13
  36.2 1.6 %copy-done.13 = bf16[1024,1024]{1,0:T(8,128)(2,1)S(1)} copy-done((bf16[1024,1024]{1,0:T(8,128)(2,1)S(1)}, bf16[1024,1024]{1,0:T(8,128)(2,1)}, u32[]{:S(2)}) %copy-start.13) | copy-done | bytes 2097176
  37.8 4.2 %q_stage.1 = (bf16[512,256]{1,0:T(8,128)(2,1)}, bf16[512,256]{1,0:T(8,128)(2,1)}, bf16[512,256]{1,0:T(8,128)(2,1)}, bf16[512,256]{1,0:T(8,128)(2,1)}) custom-call(s32[1]{0:T(128)} %bitcast.z, bf16[512,1024]{1,0:T(8,128)(2,1)} %get-tuple-element.31.normed_in, bf16[1024,1024]{1,0:T(8,128)(2,1)S(1)} %copy-done.13), custom_call_target="tpu_custom_call" | custom-call | flops 1073741824 | bytes 4194304 | tf_op jit(solution)/shard_map/q_stage/pallas_call | solution.py:255
  42.0 1.3 %collective-permute-start.8 = (bf16[512,256]{1,0:T(8,128)(2,1)}, bf16[512,256]{1,0:T(8,128)(2,1)S(1)}, u32[]{:S(2)}, u32[]{:S(2)}) collective-permute-start(bf16[512,256]{1,0:T(8,128)(2,1)} %get-tuple-element.48), channel_id=1, source_target_pairs={{0,1},{1,2},{2,3},{3,0},{4,5},{5,6},{6,7},{7,4},{8,9},{9,10},{10,1... | collective-permute-start | bytes 786440 | tf_op jit(solution)/shard_map/ppermute | solution.py:594
  43.3 1.0 collective-permute-start.3
  44.2 2.5 %collective-permute-start.4 = (bf16[256,128]{1,0:T(8,128)(2,1)S(1)}, bf16[256,128]{1,0:T(8,128)(2,1)S(1)}, u32[]{:S(2)}, u32[]{:S(2)}) collective-permute-start(bf16[256,128]{1,0:T(8,128)(2,1)S(1)} %copy-done.18), channel_id=1, source_target_pairs={{0,2},{1,3},{2,0},{3,1},{4,6},{5,7},{6,4},{7,5},{8,10},{9,11},{10,... | collective-permute-start | bytes 196616 | tf_op jit(solution)/shard_map/ppermute | solution.py:594
  46.7 1.5 %collective-permute-start.5 = (bf16[256,128]{1,0:T(8,128)(2,1)S(1)}, bf16[256,128]{1,0:T(8,128)(2,1)S(1)}, u32[]{:S(2)}, u32[]{:S(2)}) collective-permute-start(bf16[256,128]{1,0:T(8,128)(2,1)S(1)} %copy-done.17), channel_id=1, source_target_pairs={{0,3},{1,0},{2,1},{3,2},{4,7},{5,4},{6,5},{7,6},{8,11},{9,8},{10,9... | collective-permute-start | bytes 196616 | tf_op jit(solution)/shard_map/ppermute | solution.py:594
  48.3 0.0 collective-permute-start.6
  48.3 5.3 %collective-permute-done.3.s1 = bf16[256,128]{1,0:T(8,128)(2,1)S(1)} collective-permute-done((bf16[256,128]{1,0:T(8,128)(2,1)S(1)}, bf16[256,128]{1,0:T(8,128)(2,1)S(1)}, u32[]{:S(2)}, u32[]{:S(2)}) %collective-permute-start.3) | collective-permute-done | bytes 65568 | tf_op jit(solution)/shard_map/ppermute | solution.py:594
  53.6 0.9 collective-permute-start.7
  54.5 0.6 collective-permute-done.4.s2
  55.1 0.0 collective-permute-done.5.s3
  55.2 0.9 copy-done.7
  56.1 4.5 %near_stage.3 = (f32[2,4,256,128]{3,2,1,0:T(8,128)}, bf16[2,4,256,128]{3,2,1,0:T(8,128)(2,1)}) custom-call(s32[1]{0:T(128)} %bitcast.z, f32[16]{0:T(128)S(1)} %copy-done.9, bf16[4,4,128,128]{3,2,1,0:T(8,128)(2,1)S(1)} %copy-done.15, bf16[256,128]{1,0:T(8,128)(2,1)S(1)} %copy-done.16, bf16[256,128]{1,0:T(8,128)(2,1)S(1)} %collective-permute-done.3.s1, ...), custom_call_target="tpu_custom_call" | custom-call | flops 1342177280 | bytes 2097152 | tf_op jit(solution)/shard_map/near_stage/pallas_call | solution.py:426
  60.6 0.0 collective-permute-done.8.rest_0_.q
  60.7 4.5 %near_stage.4 = (f32[2,4,256,128]{3,2,1,0:T(8,128)}, bf16[2,4,256,128]{3,2,1,0:T(8,128)(2,1)}) custom-call(s32[1]{0:T(128)} %bitcast.z, f32[16]{0:T(128)S(1)} %copy-done.9, bf16[4,4,128,128]{3,2,1,0:T(8,128)(2,1)S(1)} %copy-done.15, bf16[256,128]{1,0:T(8,128)(2,1)S(1)} %copy-done.16, bf16[256,128]{1,0:T(8,128)(2,1)S(1)} %collective-permute-done.3.s1, ...), custom_call_target="tpu_custom_call" | custom-call | flops 1342177280 | bytes 2097152 | tf_op jit(solution)/shard_map/near_stage/pallas_call | solution.py:426
  65.2 0.0 collective-permute-done.6.rest_0_.q
  65.2 0.0 collective-permute-done.7.rest_1_.q
  65.2 8.3 %near_stage.5 = (f32[2,4,256,128]{3,2,1,0:T(8,128)}, bf16[2,4,256,128]{3,2,1,0:T(8,128)(2,1)}, f32[2,4,256,128]{3,2,1,0:T(8,128)}, bf16[2,4,256,128]{3,2,1,0:T(8,128)(2,1)}) custom-call(s32[1]{0:T(128)} %bitcast.z, f32[16]{0:T(128)S(1)} %copy-done.9, bf16[4,4,128,128]{3,2,1,0:T(8,128)(2,1)S(1)} %copy-done.15, bf16[256,128]{1,0:T(8,128)(2,1)S(1)} %copy-done.16, ...), custom_call_target="tpu_custom_call" | custom-call | flops 2684354560 | bytes 2097152 | tf_op jit(solution)/shard_map/near_stage/pallas_call | solution.py:426
  73.5 0.0 all-to-all-done.1
  73.5 1.2 %copy-done.2 = f32[2,4,256,128]{3,2,1,0:T(8,128)S(1)} copy-done((f32[2,4,256,128]{3,2,1,0:T(8,128)S(1)}, f32[2,4,256,128]{3,2,1,0:T(8,128)}, u32[]{:S(2)}) %copy-start.2) | copy-done | bytes 1048600
  74.7 1.0 copy-done.6
  75.8 2.3 %far_stage.7 = bf16[512,256]{1,0:T(8,128)(2,1)S(1)} custom-call(s32[1]{0:T(128)} %bitcast.z, s32[16,4]{1,0:T(8,128)S(1)} %get-tuple-element.30.slots, f32[16]{0:T(128)S(1)} %copy-done.9, bf16[512,256]{1,0:T(8,128)(2,1)S(1)} %collective-permute-done.6.rest_0_.q, f32[2,4,256,128]{3,2,1,0:T(8,128)S(1)} %copy-done.2, bf16[2,4,256,128]{3,2,1,0:T(8,128)(2,1)S(1)} %copy-done.6, ...), custom_call_target="tpu_custom_call" | custom-call | flops 536870912 | bytes 4194304 | tf_op jit(solution)/shard_map/far_stage/pallas_call | solution.py:539
  78.2 1.0 collective-permute-start.11
  79.2 3.5 %far_stage.6 = bf16[512,256]{1,0:T(8,128)(2,1)S(1)} custom-call(s32[1]{0:T(128)} %bitcast.z, s32[16,4]{1,0:T(8,128)S(1)} %get-tuple-element.30.slots, f32[16]{0:T(128)S(1)} %copy-done.9, bf16[512,256]{1,0:T(8,128)(2,1)S(1)} %collective-permute-done.7.rest_1_.q, f32[2,4,256,128]{3,2,1,0:T(8,128)} %get-tuple-element.51.rest_0_.state, ...), custom_call_target="tpu_custom_call" | custom-call | flops 536870912 | bytes 4194304 | tf_op jit(solution)/shard_map/far_stage/pallas_call | solution.py:539
  82.6 0.0 copy-start
  82.7 2.4 %collective-permute-start.10 = (bf16[512,256]{1,0:T(8,128)(2,1)S(1)}, bf16[512,256]{1,0:T(8,128)(2,1)S(1)}, u32[]{:S(2)}, u32[]{:S(2)}) collective-permute-start(bf16[512,256]{1,0:T(8,128)(2,1)S(1)} %far_stage.6), channel_id=1, source_target_pairs={{0,2},{1,3},{2,0},{3,1},{4,6},{5,7},{6,4},{7,5},{8,10},{9,11},{10,... | collective-permute-start | bytes 786440 | tf_op jit(solution)/shard_map/ppermute | solution.py:594
  85.1 2.3 %far_stage.5 = bf16[512,256]{1,0:T(8,128)(2,1)S(1)} custom-call(s32[1]{0:T(128)} %bitcast.z, s32[16,4]{1,0:T(8,128)S(1)} %get-tuple-element.30.slots, f32[16]{0:T(128)S(1)} %copy-done.9, bf16[512,256]{1,0:T(8,128)(2,1)S(1)} %collective-permute-done.8.rest_0_.q, f32[2,4,256,128]{3,2,1,0:T(8,128)S(1)} %copy-done.1, bf16[2,4,256,128]{3,2,1,0:T(8,128)(2,1)S(1)} %copy-done.5, ...), custom_call_target="tpu_custom_call" | custom-call | flops 536870912 | bytes 4194304 | tf_op jit(solution)/shard_map/far_stage/pallas_call | solution.py:539
  87.5 0.0 copy-start.3
  87.5 0.0 copy-start.10
  87.5 1.7 %collective-permute-start.9 = (bf16[512,256]{1,0:T(8,128)(2,1)S(1)}, bf16[512,256]{1,0:T(8,128)(2,1)S(1)}, u32[]{:S(2)}, u32[]{:S(2)}) collective-permute-start(bf16[512,256]{1,0:T(8,128)(2,1)S(1)} %far_stage.5), channel_id=1, source_target_pairs={{0,3},{1,0},{2,1},{3,2},{4,7},{5,4},{6,5},{7,6},{8,11},{9,8},{10,9... | collective-permute-start | bytes 786440 | tf_op jit(solution)/shard_map/ppermute | solution.py:594
  89.2 2.3 %far_stage.4.a0 = bf16[512,256]{1,0:T(8,128)(2,1)S(1)} custom-call(s32[1]{0:T(128)} %bitcast.z, s32[16,4]{1,0:T(8,128)S(1)} %get-tuple-element.30.slots, f32[16]{0:T(128)S(1)} %copy-done.9, bf16[512,256]{1,0:T(8,128)(2,1)S(1)} %copy-done.8, f32[2,4,256,128]{3,2,1,0:T(8,128)S(1)} %copy-done, bf16[2,4,256,128]{3,2,1,0:T(8,128)(2,1)S(1)} %copy-done.4, ...), custom_call_target="tpu_custom_call" | custom-call | flops 536870912 | bytes 4194304 | tf_op jit(solution)/shard_map/far_stage/pallas_call | solution.py:539
  91.5 1.4 %collective-permute-done.11.a3 = bf16[512,256]{1,0:T(8,128)(2,1)S(1)} collective-permute-done((bf16[512,256]{1,0:T(8,128)(2,1)S(1)}, bf16[512,256]{1,0:T(8,128)(2,1)S(1)}, u32[]{:S(2)}, u32[]{:S(2)}) %collective-permute-start.11) | collective-permute-done | bytes 262176 | tf_op jit(solution)/shard_map/ppermute | solution.py:594
  92.9 0.0 collective-permute-done.10.a2
  92.9 4.2 %collective-permute-done.9.a1 = bf16[512,256]{1,0:T(8,128)(2,1)S(1)} collective-permute-done((bf16[512,256]{1,0:T(8,128)(2,1)S(1)}, bf16[512,256]{1,0:T(8,128)(2,1)S(1)}, u32[]{:S(2)}, u32[]{:S(2)}) %collective-permute-start.9) | collective-permute-done | bytes 262176 | tf_op jit(solution)/shard_map/ppermute | solution.py:594
  97.1 9.1 %ffn_stage.1 = bf16[512,1024]{1,0:T(8,128)(2,1)} custom-call(s32[1]{0:T(128)} %bitcast.z, bf16[512,1024]{1,0:T(8,128)(2,1)S(1)} %copy-done.3, bf16[512,256]{1,0:T(8,128)(2,1)S(1)} %far_stage.4.a0, bf16[512,256]{1,0:T(8,128)(2,1)S(1)} %collective-permute-done.9.a1, bf16[512,256]{1,0:T(8,128)(2,1)S(1)} %collective-permute-done.10.a2, ...), custom_call_target="tpu_custom_call" | custom-call | flops 7516192768 | bytes 18874368 | tf_op jit(solution)/shard_map/ffn_stage/pallas_call | solution.py:581
  (31 shorter events, 0.1 us)
Async XLA Ops:
  5.8 19.5 %all-to-all-start = ((bf16[32,48,128]{2,1,0:T(8,128)(2,1)}), bf16[32,48,128]{2,1,0:T(8,128)(2,1)S(1)}, u32[]{:S(2)}, u32[]{:S(2)}) async-start(bf16[32,48,128]{2,1,0:T(8,128)(2,1)} %get-tuple-element.33), calls=%async_computation | async-start | bytes 786432 | tf_op jit(solution)/shard_map/all_to_all | solution.py:601
  13.2 8.0 %collective-permute-start = (bf16[512,128]{1,0:T(8,128)(2,1)S(1)}, bf16[512,128]{1,0:T(8,128)(2,1)S(1)}, u32[]{:S(2)}, u32[]{:S(2)}) collective-permute-start(bf16[512,128]{1,0:T(8,128)(2,1)S(1)} %get-tuple-element.35), channel_id=1, source_target_pairs={{0,1},{1,2},{2,3},{3,0},{4,5},{5,6},{6,7},{7,4},{8,9},{9,10},{10,1... | collective-permute-start | bytes 393224 | tf_op jit(solution)/shard_map/ppermute | solution.py:594
  15.2 10.0 %collective-permute-start.1 = (bf16[512,128]{1,0:T(8,128)(2,1)S(1)}, bf16[512,128]{1,0:T(8,128)(2,1)S(1)}, u32[]{:S(2)}, u32[]{:S(2)}) collective-permute-start(bf16[512,128]{1,0:T(8,128)(2,1)S(1)} %get-tuple-element.36), channel_id=1, source_target_pairs={{0,2},{1,3},{2,0},{3,1},{4,6},{5,7},{6,4},{7,5},{8,10},{9,11},{10,... | collective-permute-start | bytes 393224 | tf_op jit(solution)/shard_map/ppermute | solution.py:594
  18.8 6.5 %collective-permute-start.2 = (bf16[512,128]{1,0:T(8,128)(2,1)S(1)}, bf16[512,128]{1,0:T(8,128)(2,1)S(1)}, u32[]{:S(2)}, u32[]{:S(2)}) collective-permute-start(bf16[512,128]{1,0:T(8,128)(2,1)S(1)} %get-tuple-element.37), channel_id=1, source_target_pairs={{0,3},{1,0},{2,1},{3,2},{4,7},{5,4},{6,5},{7,6},{8,11},{9,8},{10,9... | collective-permute-start | bytes 393224 | tf_op jit(solution)/shard_map/ppermute | solution.py:594
  28.9 44.6 %all-to-all-start.1 = ((bf16[32,256,128]{2,1,0:T(8,128)(2,1)}), bf16[32,256,128]{2,1,0:T(8,128)(2,1)S(1)}, u32[]{:S(2)}, u32[]{:S(2)}) async-start(bf16[32,256,128]{2,1,0:T(8,128)(2,1)} %bitcast.8), calls=%async_computation.1 | async-start | bytes 4194304 | tf_op jit(solution)/shard_map/all_to_all | solution.py:605
  36.2 19.0 %copy-start.9 = (f32[16]{0:T(128)S(1)}, f32[16]{0:T(128)}, u32[]{:S(2)}) copy-start(f32[16]{0:T(128)} %scale.13) | copy-start | bytes 196
  36.2 1.6 %copy-start.13 = (bf16[1024,1024]{1,0:T(8,128)(2,1)S(1)}, bf16[1024,1024]{1,0:T(8,128)(2,1)}, u32[]{:S(2)}) copy-start(bf16[1024,1024]{1,0:T(8,128)(2,1)} %w_query.1) | copy-start | bytes 6291460
  37.8 5.5 %copy-start.19 = (bf16[256,128]{1,0:T(8,128)(2,1)S(1)}, bf16[256,128]{1,0:T(8,128)(2,1)}, u32[]{:S(2)}) copy-start(bf16[256,128]{1,0:T(8,128)(2,1)} %get-tuple-element.40) | copy-start | bytes 196612
  37.8 6.4 %copy-start.18 = (bf16[256,128]{1,0:T(8,128)(2,1)S(1)}, bf16[256,128]{1,0:T(8,128)(2,1)}, u32[]{:S(2)}) copy-start(bf16[256,128]{1,0:T(8,128)(2,1)} %get-tuple-element.41) | copy-start | bytes 196612
  37.8 9.0 %copy-start.17 = (bf16[256,128]{1,0:T(8,128)(2,1)S(1)}, bf16[256,128]{1,0:T(8,128)(2,1)}, u32[]{:S(2)}) copy-start(bf16[256,128]{1,0:T(8,128)(2,1)} %get-tuple-element.42) | copy-start | bytes 196612
  37.8 17.4 %copy-start.15 = (bf16[4,4,128,128]{3,2,1,0:T(8,128)(2,1)S(1)}, bf16[4,4,128,128]{3,2,1,0:T(8,128)(2,1)}, u32[]{:S(2)}) copy-start(bf16[4,4,128,128]{3,2,1,0:T(8,128)(2,1)} %get-tuple-element.38.kv) | copy-start | bytes 1572868
  37.8 17.4 %copy-start.16 = (bf16[256,128]{1,0:T(8,128)(2,1)S(1)}, bf16[256,128]{1,0:T(8,128)(2,1)}, u32[]{:S(2)}) copy-start(bf16[256,128]{1,0:T(8,128)(2,1)} %get-tuple-element.39.s0) | copy-start | bytes 196612
  42.0 18.7 %collective-permute-start.8 = (bf16[512,256]{1,0:T(8,128)(2,1)}, bf16[512,256]{1,0:T(8,128)(2,1)S(1)}, u32[]{:S(2)}, u32[]{:S(2)}) collective-permute-start(bf16[512,256]{1,0:T(8,128)(2,1)} %get-tuple-element.48), channel_id=1, source_target_pairs={{0,1},{1,2},{2,3},{3,0},{4,5},{5,6},{6,7},{7,4},{8,9},{9,10},{10,1... | collective-permute-start | bytes 786440 | tf_op jit(solution)/shard_map/ppermute | solution.py:594
  43.3 10.4 %collective-permute-start.3 = (bf16[256,128]{1,0:T(8,128)(2,1)S(1)}, bf16[256,128]{1,0:T(8,128)(2,1)S(1)}, u32[]{:S(2)}, u32[]{:S(2)}) collective-permute-start(bf16[256,128]{1,0:T(8,128)(2,1)S(1)} %copy-done.19), channel_id=1, source_target_pairs={{0,1},{1,2},{2,3},{3,0},{4,5},{5,6},{6,7},{7,4},{8,9},{9,10},{10,1... | collective-permute-start | bytes 196616 | tf_op jit(solution)/shard_map/ppermute | solution.py:594
  44.2 10.9 %collective-permute-start.4 = (bf16[256,128]{1,0:T(8,128)(2,1)S(1)}, bf16[256,128]{1,0:T(8,128)(2,1)S(1)}, u32[]{:S(2)}, u32[]{:S(2)}) collective-permute-start(bf16[256,128]{1,0:T(8,128)(2,1)S(1)} %copy-done.18), channel_id=1, source_target_pairs={{0,2},{1,3},{2,0},{3,1},{4,6},{5,7},{6,4},{7,5},{8,10},{9,11},{10,... | collective-permute-start | bytes 196616 | tf_op jit(solution)/shard_map/ppermute | solution.py:594
  46.7 8.4 %collective-permute-start.5 = (bf16[256,128]{1,0:T(8,128)(2,1)S(1)}, bf16[256,128]{1,0:T(8,128)(2,1)S(1)}, u32[]{:S(2)}, u32[]{:S(2)}) collective-permute-start(bf16[256,128]{1,0:T(8,128)(2,1)S(1)} %copy-done.17), channel_id=1, source_target_pairs={{0,3},{1,0},{2,1},{3,2},{4,7},{5,4},{6,5},{7,6},{8,11},{9,8},{10,9... | collective-permute-start | bytes 196616 | tf_op jit(solution)/shard_map/ppermute | solution.py:594
  48.3 16.9 %collective-permute-start.6 = (bf16[512,256]{1,0:T(8,128)(2,1)}, bf16[512,256]{1,0:T(8,128)(2,1)S(1)}, u32[]{:S(2)}, u32[]{:S(2)}) collective-permute-start(bf16[512,256]{1,0:T(8,128)(2,1)} %get-tuple-element.46), channel_id=1, source_target_pairs={{0,3},{1,0},{2,1},{3,2},{4,7},{5,4},{6,5},{7,6},{8,11},{9,8},{10,9... | collective-permute-start | bytes 786440 | tf_op jit(solution)/shard_map/ppermute | solution.py:594
  53.6 11.6 %collective-permute-start.7 = (bf16[512,256]{1,0:T(8,128)(2,1)}, bf16[512,256]{1,0:T(8,128)(2,1)S(1)}, u32[]{:S(2)}, u32[]{:S(2)}) collective-permute-start(bf16[512,256]{1,0:T(8,128)(2,1)} %get-tuple-element.47), channel_id=1, source_target_pairs={{0,2},{1,3},{2,0},{3,1},{4,6},{5,7},{6,4},{7,5},{8,10},{9,11},{10,... | collective-permute-start | bytes 786440 | tf_op jit(solution)/shard_map/ppermute | solution.py:594
  55.1 1.0 copy-start.7
  73.5 1.2 %copy-start.2 = (f32[2,4,256,128]{3,2,1,0:T(8,128)S(1)}, f32[2,4,256,128]{3,2,1,0:T(8,128)}, u32[]{:S(2)}) copy-start(f32[2,4,256,128]{3,2,1,0:T(8,128)} %get-tuple-element.53.state) | copy-start | bytes 3145732
  74.7 1.0 copy-start.6
  75.8 21.3 %copy-start.12 = (bf16[2048,1024]{1,0:T(8,128)(2,1)S(1)}, bf16[2048,1024]{1,0:T(8,128)(2,1)}, u32[]{:S(2)}) copy-start(bf16[2048,1024]{1,0:T(8,128)(2,1)} %w_down.1) | copy-start | bytes 12582916
  78.1 7.0 %copy-start.1 = (f32[2,4,256,128]{3,2,1,0:T(8,128)S(1)}, f32[2,4,256,128]{3,2,1,0:T(8,128)}, u32[]{:S(2)}) copy-start(f32[2,4,256,128]{3,2,1,0:T(8,128)} %get-tuple-element.49.rest_2_.state) | copy-start | bytes 3145732
  78.1 7.0 %copy-start.5 = (bf16[2,4,256,128]{3,2,1,0:T(8,128)(2,1)S(1)}, bf16[2,4,256,128]{3,2,1,0:T(8,128)(2,1)}, u32[]{:S(2)}) copy-start(bf16[2,4,256,128]{3,2,1,0:T(8,128)(2,1)} %get-tuple-element.50.rest_3_.peaks) | copy-start | bytes 1572868
  78.2 14.7 %collective-permute-start.11 = (bf16[512,256]{1,0:T(8,128)(2,1)S(1)}, bf16[512,256]{1,0:T(8,128)(2,1)S(1)}, u32[]{:S(2)}, u32[]{:S(2)}) collective-permute-start(bf16[512,256]{1,0:T(8,128)(2,1)S(1)} %far_stage.7), channel_id=1, source_target_pairs={{0,1},{1,2},{2,3},{3,0},{4,5},{5,6},{6,7},{7,4},{8,9},{9,10},{10,1... | collective-permute-start | bytes 786440 | tf_op jit(solution)/shard_map/ppermute | solution.py:594
  79.2 17.9 %copy-start.14 = (bf16[1024,1024]{1,0:T(8,128)(2,1)S(1)}, bf16[1024,1024]{1,0:T(8,128)(2,1)}, u32[]{:S(2)}) copy-start(bf16[1024,1024]{1,0:T(8,128)(2,1)} %w_out.1) | copy-start | bytes 6291460
  82.6 6.5 %copy-start = (f32[2,4,256,128]{3,2,1,0:T(8,128)S(1)}, f32[2,4,256,128]{3,2,1,0:T(8,128)}, u32[]{:S(2)}) copy-start(f32[2,4,256,128]{3,2,1,0:T(8,128)} %get-tuple-element.43.rest_1_.state) | copy-start | bytes 3145732
  82.6 6.5 %copy-start.4 = (bf16[2,4,256,128]{3,2,1,0:T(8,128)(2,1)S(1)}, bf16[2,4,256,128]{3,2,1,0:T(8,128)(2,1)}, u32[]{:S(2)}) copy-start(bf16[2,4,256,128]{3,2,1,0:T(8,128)(2,1)} %get-tuple-element.44.rest_2_.peaks) | copy-start | bytes 1572868
  82.7 6.5 %copy-start.8 = (bf16[512,256]{1,0:T(8,128)(2,1)S(1)}, bf16[512,256]{1,0:T(8,128)(2,1)}, u32[]{:S(2)}) copy-start(bf16[512,256]{1,0:T(8,128)(2,1)} %get-tuple-element.32.rest_0_.q) | copy-start | bytes 786436
  82.7 10.2 %collective-permute-start.10 = (bf16[512,256]{1,0:T(8,128)(2,1)S(1)}, bf16[512,256]{1,0:T(8,128)(2,1)S(1)}, u32[]{:S(2)}, u32[]{:S(2)}) collective-permute-start(bf16[512,256]{1,0:T(8,128)(2,1)S(1)} %far_stage.6), channel_id=1, source_target_pairs={{0,2},{1,3},{2,0},{3,1},{4,6},{5,7},{6,4},{7,5},{8,10},{9,11},{10,... | collective-permute-start | bytes 786440 | tf_op jit(solution)/shard_map/ppermute | solution.py:594
  85.1 12.0 %copy-start.11 = (bf16[1024,2048]{1,0:T(8,128)(2,1)S(1)}, bf16[1024,2048]{1,0:T(8,128)(2,1)}, u32[]{:S(2)}) copy-start(bf16[1024,2048]{1,0:T(8,128)(2,1)} %w_up.1) | copy-start | bytes 12582916
  87.5 9.6 %copy-start.3 = (bf16[512,1024]{1,0:T(8,128)(2,1)S(1)}, bf16[512,1024]{1,0:T(8,128)(2,1)}, u32[]{:S(2)}) copy-start(bf16[512,1024]{1,0:T(8,128)(2,1)} %tokens.1) | copy-start | bytes 3145732
  87.5 9.6 %copy-start.10 = (bf16[1024,2048]{1,0:T(8,128)(2,1)S(1)}, bf16[1024,2048]{1,0:T(8,128)(2,1)}, u32[]{:S(2)}) copy-start(bf16[1024,2048]{1,0:T(8,128)(2,1)} %w_gate.1) | copy-start | bytes 12582916
  87.5 9.6 %collective-permute-start.9 = (bf16[512,256]{1,0:T(8,128)(2,1)S(1)}, bf16[512,256]{1,0:T(8,128)(2,1)S(1)}, u32[]{:S(2)}, u32[]{:S(2)}) collective-permute-start(bf16[512,256]{1,0:T(8,128)(2,1)S(1)} %far_stage.5), channel_id=1, source_target_pairs={{0,3},{1,0},{2,1},{3,2},{4,7},{5,4},{6,5},{7,6},{8,11},{9,8},{10,9... | collective-permute-start | bytes 786440 | tf_op jit(solution)/shard_map/ppermute | solution.py:594

commit v5 on v4

--- a/solution.py
+++ b/solution.py
@@ -560,11 +560,32 @@
     )
 
 
-def ffn_body(z, tokens, a0, a1, a2, a3, w_out, w_gate, w_up, w_down, out, mid_held, held, hidden):
+def projected(z, k, part, w_out):
+    start = pl.multiple_of(((z[0] + k) % ZS) * GROUP_W, GROUP_W)
+    return jnp.dot(part[...], w_out[pl.ds(start, GROUP_W), :], preferred_element_type=f32)
+
+
+def mid_body(z, tokens, a0, a1, a2, w_out, out):
     mid = tokens[...].astype(f32)
-    for k, a in enumerate((a0, a1, a2, a3)):
-        start = pl.multiple_of(((z[0] + k) % ZS) * GROUP_W, GROUP_W)
-        mid = mid + jnp.dot(a[...], w_out[pl.ds(start, GROUP_W), :], preferred_element_type=f32)
+    for k, a in enumerate((a0, a1, a2)):
+        mid = mid + projected(z, k, a, w_out)
+    out[...] = mid
+
+
+def mid_stage(z, tokens, parts, w_out):
+    return pl.pallas_call(
+        mid_body,
+        name="mid_stage",
+        in_specs=[whole(SMEM)] + [whole(VMEM)] * 5,
+        out_specs=whole(VMEM),
+        out_shape=VMEM((ROWS, 1024), f32),
+        compiler_params=params(8),
+        cost_estimate=cost(2 * ROWS * 1024 * 768, 4 << 20),
+    )(z, *[near_core(a) for a in (tokens, *parts, w_out)])
+
+
+def ffn_body(z, mid_in, a3, w_out, w_gate, w_up, w_down, out, mid_held, held, hidden):
+    mid = mid_in[...] + projected(z, 3, a3, w_out)
     mid_held[...] = mid
     held[...] = row_norm(mid).astype(bf16)
     for j in range(FFN // UNIT):
@@ -577,17 +598,17 @@
     ).astype(bf16)
 
 
-def ffn_stage(z, tokens, parts, w_out, w_gate, w_up, w_down):
+def ffn_stage(z, mid, part, w_out, w_gate, w_up, w_down):
     return pl.pallas_call(
         ffn_body,
         name="ffn_stage",
-        in_specs=[whole(SMEM)] + [whole(VMEM)] * 9,
+        in_specs=[whole(SMEM)] + [whole(VMEM)] * 6,
         out_specs=whole(VMEM),
         out_shape=jax.ShapeDtypeStruct((ROWS, 1024), bf16),
         scratch_shapes=[VMEM((ROWS, 1024), f32), VMEM((ROWS, 1024), bf16), VMEM((ROWS, FFN), bf16)],
         compiler_params=params(14),
-        cost_estimate=cost(2 * ROWS * 1024 * 7168, 18 << 20),
-    )(z, *[near_core(a) for a in (tokens, *parts, w_out, w_gate, w_up, w_down)])
+        cost_estimate=cost(2 * ROWS * 1024 * 6400, 18 << 20),
+    )(z, *[near_core(a) for a in (mid, part, w_out, w_gate, w_up, w_down)])
 
 
 def shift(array, k):
@@ -597,7 +618,9 @@
 def body(tokens, w_query, w_key, w_value, w_out, logit_scale, w_gate, w_up, w_down, picks):
     z = lax.axis_index("head").astype(jnp.int32).reshape(1)
     *pairs, payload, normed, slots = first_stage(z, picks.T, tokens, w_key, w_value)
-    chunks = [pairs[0]] + [shift(pairs[k], k) for k in (1, 2, 3)]
+    chunks = [pairs[0], None, None, None]
+    for k in (2, 1, 3):
+        chunks[k] = shift(pairs[k], k)
     told = lax.all_to_all(payload, "pts", split_axis=0, concat_axis=0, tiled=True)
     query = q_stage(z, normed, w_query)
     replies, *sums, kv = reply_stage(z, told, chunks)
@@ -620,7 +643,8 @@
         others = states[2] if k != 2 else []
         attended = far_stage(k, z, slots, logit_scale, q[k], states[k], fetched, others, k == 2)
         parts[k] = shift(attended, ZS - k) if k else attended
-    return ffn_stage(z, tokens, parts, w_out, w_gate, w_up, w_down)
+    mid = mid_stage(z, tokens, parts[:3], w_out)
+    return ffn_stage(z, mid, parts[3], w_out, w_gate, w_up, w_down)
 
 
 def solution(mesh):

time: 107 us -> 102 us (0.953)
  local copies, waits for them, and re-layouts: 4.86 us -> 2.62 us
  waiting for transfers between devices: 16.9 us -> 14.9 us
    unnamed x40, local copies, waits for them, and re-layouts: 4.86 us -> 2.62 us
    ppermute x12, waiting for transfers between devices: 16.9 us -> 14.9 us  [shift(): return lax.ppermute(array, 'head', [(i, (i + k) % ZS) for i in range(ZS)])]
  transfers between devices with their start and end apart: 14 -> 14, of which waited for: 6 -> 6; matrix products, arithmetic and copies ran while one was open for 0% -> 0% of each run, Pallas kernels for 28% -> 29%
where the time goes in v5:
time: 102 us; the launch traced here: 101 us
  Pallas kernels  50.7 us (50%)
  starting transfers between devices  33 us (32%)
  waiting for transfers between devices  14.9 us (15%)
  local copies, waits for them, and re-layouts  2.62 us (3%)
    ppermute x12, starting transfers between devices, shift(): return lax.ppermute(array, 'head', [(i, (i + k) % ZS) for i in range(ZS)])  18.4 us
    pallas_call x3, Pallas kernels, near_stage(): pl.pallas_call(functools.partial(near_body, chunks), name='near_stage', i...  17.4 us
    ppermute x12, waiting for transfers between devices, shift(): return lax.ppermute(array, 'head', [(i, (i + k) % ZS) for i in range(ZS)])  14.9 us
    pallas_call x4, Pallas kernels, far_stage(): pl.pallas_call(functools.partial(far_body, shift_by, direct), name='far_s...  10.5 us
    pallas_call x1, Pallas kernels, ffn_stage(): pl.pallas_call(ffn_body, name='ffn_stage', in_specs=[whole(SMEM)] + [whol...  8.25 us
    all_to_all x1, starting transfers between devices, body(): lax.all_to_all(payload, 'pts', split_axis=0, concat_axis=0, tiled=True)  7.44 us
    all_to_all x1, starting transfers between devices, body(): lax.all_to_all(replies, 'pts', split_axis=0, concat_axis=0, tiled=True)  7.24 us
    pallas_call x1, Pallas kernels, first_stage(): pl.pallas_call(first_body, name='first_stage', in_specs=[whole(SMEM)] + [...  5.79 us
  transfers between devices with their start and end apart: 14, of which 6 were waited for; matrix products, arithmetic and copies ran while one was open for 0% of the time, Pallas kernels for 29%

profile of v5, /device:TPU:0, one launch (start us, length us, event | category | flops | bytes accessed | tf_op | source)
XLA Modules:
  0.0 101.5 jit_solution(13858965500664084882)
XLA Ops:
  0.0 5.8 %first_stage.1 = (bf16[512,128]{1,0:T(8,128)(2,1)S(1)}, bf16[512,128]{1,0:T(8,128)(2,1)S(1)}, bf16[512,128]{1,0:T(8,128)(2,1)S(1)}, bf16[512,128]{1,0:T(8,128)(2...) custom-call(s32[1]{0:T(128)} %bitcast.z, s32[4,16]{1,0:T(4,128)} %bitcast.9, ...), custom_call_target="tpu_custom_call" | custom-call | flops 536870912 | bytes 4194304 | tf_op jit(solution)/shard_map/first_stage/pallas_call | solution.py:191
  5.8 7.4 %all-to-all-start = ((bf16[32,48,128]{2,1,0:T(8,128)(2,1)}), bf16[32,48,128]{2,1,0:T(8,128)(2,1)S(1)}, u32[]{:S(2)}, u32[]{:S(2)}) async-start(bf16[32,48,128]{2,1,0:T(8,128)(2,1)} %get-tuple-element.33), calls=%async_computation | async-start | bytes 786432 | tf_op jit(solution)/shard_map/all_to_all | solution.py:624
  13.2 2.0 %collective-permute-start = (bf16[512,128]{1,0:T(8,128)(2,1)S(1)}, bf16[512,128]{1,0:T(8,128)(2,1)S(1)}, u32[]{:S(2)}, u32[]{:S(2)}) collective-permute-start(bf16[512,128]{1,0:T(8,128)(2,1)S(1)} %get-tuple-element.35), channel_id=1, source_target_pairs={{0,1},{1,2},{2,3},{3,0},{4,5},{5,6},{6,7},{7,4},{8,9},{9,10},{10,1... | collective-permute-start | bytes 393224 | tf_op jit(solution)/shard_map/ppermute | solution.py:615
  15.2 3.6 %collective-permute-start.1 = (bf16[512,128]{1,0:T(8,128)(2,1)S(1)}, bf16[512,128]{1,0:T(8,128)(2,1)S(1)}, u32[]{:S(2)}, u32[]{:S(2)}) collective-permute-start(bf16[512,128]{1,0:T(8,128)(2,1)S(1)} %get-tuple-element.36), channel_id=1, source_target_pairs={{0,2},{1,3},{2,0},{3,1},{4,6},{5,7},{6,4},{7,5},{8,10},{9,11},{10,... | collective-permute-start | bytes 393224 | tf_op jit(solution)/shard_map/ppermute | solution.py:615
  18.8 1.0 collective-permute-start.2
  19.8 1.5 %collective-permute-done.c1 = bf16[512,128]{1,0:T(8,128)(2,1)S(1)} collective-permute-done((bf16[512,128]{1,0:T(8,128)(2,1)S(1)}, bf16[512,128]{1,0:T(8,128)(2,1)S(1)}, u32[]{:S(2)}, u32[]{:S(2)}) %collective-permute-start) | collective-permute-done | bytes 131104 | tf_op jit(solution)/shard_map/ppermute | solution.py:615
  21.3 4.0 %collective-permute-done.1.c2 = bf16[512,128]{1,0:T(8,128)(2,1)S(1)} collective-permute-done((bf16[512,128]{1,0:T(8,128)(2,1)S(1)}, bf16[512,128]{1,0:T(8,128)(2,1)S(1)}, u32[]{:S(2)}, u32[]{:S(2)}) %collective-permute-start.1) | collective-permute-done | bytes 131104 | tf_op jit(solution)/shard_map/ppermute | solution.py:615
  25.3 0.0 collective-permute-done.2.c3
  25.3 0.0 all-to-all-done.told
  25.3 3.6 %reply_stage.1 = (bf16[64,128,128]{2,1,0:T(8,128)(2,1)}, bf16[256,128]{1,0:T(8,128)(2,1)}, bf16[256,128]{1,0:T(8,128)(2,1)}, bf16[256,128]{1,0:T(8,128)(2,1)}, b...) custom-call(s32[1]{0:T(128)} %bitcast.z, bf16[32,48,128]{2,1,0:T(8,128)(2,1)S(1)} %all-to-all-done.told, ...), custom_call_target="tpu_custom_call" | custom-call | tf_op jit(solution)/shard_map/reply_stage/pallas_call | solution.py:310
  28.9 7.2 %all-to-all-start.1 = ((bf16[32,256,128]{2,1,0:T(8,128)(2,1)}), bf16[32,256,128]{2,1,0:T(8,128)(2,1)S(1)}, u32[]{:S(2)}, u32[]{:S(2)}) async-start(bf16[32,256,128]{2,1,0:T(8,128)(2,1)} %bitcast.8), calls=%async_computation.1 | async-start | bytes 4194304 | tf_op jit(solution)/shard_map/all_to_all | solution.py:628
  36.2 0.0 copy-start.10
  36.2 0.0 copy-start.14
  36.2 1.6 %copy-done.14 = bf16[1024,1024]{1,0:T(8,128)(2,1)S(1)} copy-done((bf16[1024,1024]{1,0:T(8,128)(2,1)S(1)}, bf16[1024,1024]{1,0:T(8,128)(2,1)}, u32[]{:S(2)}) %copy-start.14) | copy-done | bytes 2097176
  37.8 4.2 %q_stage.1 = (bf16[512,256]{1,0:T(8,128)(2,1)}, bf16[512,256]{1,0:T(8,128)(2,1)}, bf16[512,256]{1,0:T(8,128)(2,1)}, bf16[512,256]{1,0:T(8,128)(2,1)}) custom-call(s32[1]{0:T(128)} %bitcast.z, bf16[512,1024]{1,0:T(8,128)(2,1)} %get-tuple-element.31.normed_in, bf16[1024,1024]{1,0:T(8,128)(2,1)S(1)} %copy-done.14), custom_call_target="tpu_custom_call" | custom-call | flops 1073741824 | bytes 4194304 | tf_op jit(solution)/shard_map/q_stage/pallas_call | solution.py:255
  42.0 1.3 %collective-permute-start.8 = (bf16[512,256]{1,0:T(8,128)(2,1)}, bf16[512,256]{1,0:T(8,128)(2,1)S(1)}, u32[]{:S(2)}, u32[]{:S(2)}) collective-permute-start(bf16[512,256]{1,0:T(8,128)(2,1)} %get-tuple-element.48), channel_id=1, source_target_pairs={{0,1},{1,2},{2,3},{3,0},{4,5},{5,6},{6,7},{7,4},{8,9},{9,10},{10,1... | collective-permute-start | bytes 786440 | tf_op jit(solution)/shard_map/ppermute | solution.py:615
  43.3 1.0 collective-permute-start.3
  44.2 2.5 %collective-permute-start.4 = (bf16[256,128]{1,0:T(8,128)(2,1)S(1)}, bf16[256,128]{1,0:T(8,128)(2,1)S(1)}, u32[]{:S(2)}, u32[]{:S(2)}) collective-permute-start(bf16[256,128]{1,0:T(8,128)(2,1)S(1)} %copy-done.18), channel_id=1, source_target_pairs={{0,2},{1,3},{2,0},{3,1},{4,6},{5,7},{6,4},{7,5},{8,10},{9,11},{10,... | collective-permute-start | bytes 196616 | tf_op jit(solution)/shard_map/ppermute | solution.py:615
  46.7 1.6 %collective-permute-start.5 = (bf16[256,128]{1,0:T(8,128)(2,1)S(1)}, bf16[256,128]{1,0:T(8,128)(2,1)S(1)}, u32[]{:S(2)}, u32[]{:S(2)}) collective-permute-start(bf16[256,128]{1,0:T(8,128)(2,1)S(1)} %copy-done.17), channel_id=1, source_target_pairs={{0,3},{1,0},{2,1},{3,2},{4,7},{5,4},{6,5},{7,6},{8,11},{9,8},{10,9... | collective-permute-start | bytes 196616 | tf_op jit(solution)/shard_map/ppermute | solution.py:615
  48.3 0.0 collective-permute-start.6
  48.3 5.3 %collective-permute-done.3.s1 = bf16[256,128]{1,0:T(8,128)(2,1)S(1)} collective-permute-done((bf16[256,128]{1,0:T(8,128)(2,1)S(1)}, bf16[256,128]{1,0:T(8,128)(2,1)S(1)}, u32[]{:S(2)}, u32[]{:S(2)}) %collective-permute-start.3) | collective-permute-done | bytes 65568 | tf_op jit(solution)/shard_map/ppermute | solution.py:615
  53.6 0.9 collective-permute-start.7
  54.6 0.6 collective-permute-done.4.s2
  55.1 0.0 collective-permute-done.5.s3
  55.2 0.9 copy-done.8
  56.1 4.6 %near_stage.3 = (f32[2,4,256,128]{3,2,1,0:T(8,128)}, bf16[2,4,256,128]{3,2,1,0:T(8,128)(2,1)}) custom-call(s32[1]{0:T(128)} %bitcast.z, f32[16]{0:T(128)S(1)} %copy-done.10, bf16[4,4,128,128]{3,2,1,0:T(8,128)(2,1)S(1)} %copy-done.15, bf16[256,128]{1,0:T(8,128)(2,1)S(1)} %copy-done.16, bf16[256,128]{1,0:T(8,128)(2,1)S(1)} %collective-permute-done.3.s1, ...), custom_call_target="tpu_custom_call" | custom-call | flops 1342177280 | bytes 2097152 | tf_op jit(solution)/shard_map/near_stage/pallas_call | solution.py:426
  60.7 0.0 collective-permute-done.8.rest_0_.q
  60.7 4.5 %near_stage.4 = (f32[2,4,256,128]{3,2,1,0:T(8,128)}, bf16[2,4,256,128]{3,2,1,0:T(8,128)(2,1)}) custom-call(s32[1]{0:T(128)} %bitcast.z, f32[16]{0:T(128)S(1)} %copy-done.10, bf16[4,4,128,128]{3,2,1,0:T(8,128)(2,1)S(1)} %copy-done.15, bf16[256,128]{1,0:T(8,128)(2,1)S(1)} %copy-done.16, bf16[256,128]{1,0:T(8,128)(2,1)S(1)} %collective-permute-done.3.s1, ...), custom_call_target="tpu_custom_call" | custom-call | flops 1342177280 | bytes 2097152 | tf_op jit(solution)/shard_map/near_stage/pallas_call | solution.py:426
  65.2 0.0 collective-permute-done.6.rest_0_.q
  65.2 0.0 collective-permute-done.7.rest_1_.q
  65.2 8.3 %near_stage.5 = (f32[2,4,256,128]{3,2,1,0:T(8,128)}, bf16[2,4,256,128]{3,2,1,0:T(8,128)(2,1)}, f32[2,4,256,128]{3,2,1,0:T(8,128)}, bf16[2,4,256,128]{3,2,1,0:T(8,128)(2,1)}) custom-call(s32[1]{0:T(128)} %bitcast.z, f32[16]{0:T(128)S(1)} %copy-done.10, bf16[4,4,128,128]{3,2,1,0:T(8,128)(2,1)S(1)} %copy-done.15, bf16[256,128]{1,0:T(8,128)(2,1)S(1)} %copy-done.16, ...), custom_call_target="tpu_custom_call" | custom-call | flops 2684354560 | bytes 2097152 | tf_op jit(solution)/shard_map/near_stage/pallas_call | solution.py:426
  73.5 0.0 all-to-all-done.1
  73.6 3.5 %far_stage.6 = bf16[512,256]{1,0:T(8,128)(2,1)S(1)} custom-call(s32[1]{0:T(128)} %bitcast.z, s32[16,4]{1,0:T(8,128)S(1)} %get-tuple-element.30.slots, f32[16]{0:T(128)S(1)} %copy-done.10, bf16[512,256]{1,0:T(8,128)(2,1)S(1)} %collective-permute-done.7.rest_1_.q, f32[2,4,256,128]{3,2,1,0:T(8,128)} %get-tuple-element.51.rest_0_.state, ...), custom_call_target="tpu_custom_call" | custom-call | flops 536870912 | bytes 4194304 | tf_op jit(solution)/shard_map/far_stage/pallas_call | solution.py:539
  77.1 2.4 %collective-permute-start.10 = (bf16[512,256]{1,0:T(8,128)(2,1)S(1)}, bf16[512,256]{1,0:T(8,128)(2,1)S(1)}, u32[]{:S(2)}, u32[]{:S(2)}) collective-permute-start(bf16[512,256]{1,0:T(8,128)(2,1)S(1)} %far_stage.6), channel_id=1, source_target_pairs={{0,2},{1,3},{2,0},{3,1},{4,6},{5,7},{6,4},{7,5},{8,10},{9,11},{10,... | collective-permute-start | bytes 786440 | tf_op jit(solution)/shard_map/ppermute | solution.py:615
  79.4 2.3 %far_stage.5 = bf16[512,256]{1,0:T(8,128)(2,1)S(1)} custom-call(s32[1]{0:T(128)} %bitcast.z, s32[16,4]{1,0:T(8,128)S(1)} %get-tuple-element.30.slots, f32[16]{0:T(128)S(1)} %copy-done.10, bf16[512,256]{1,0:T(8,128)(2,1)S(1)} %collective-permute-done.8.rest_0_.q, f32[2,4,256,128]{3,2,1,0:T(8,128)S(1)} %copy-done.3, bf16[2,4,256,128]{3,2,1,0:T(8,128)(2,1)S(1)} %copy-done.6, ...), custom_call_target="tpu_custom_call" | custom-call | flops 536870912 | bytes 4194304 | tf_op jit(solution)/shard_map/far_stage/pallas_call | solution.py:539
  81.8 1.4 %collective-permute-start.9 = (bf16[512,256]{1,0:T(8,128)(2,1)S(1)}, bf16[512,256]{1,0:T(8,128)(2,1)S(1)}, u32[]{:S(2)}, u32[]{:S(2)}) collective-permute-start(bf16[512,256]{1,0:T(8,128)(2,1)S(1)} %far_stage.5), channel_id=1, source_target_pairs={{0,3},{1,0},{2,1},{3,2},{4,7},{5,4},{6,5},{7,6},{8,11},{9,8},{10,9... | collective-permute-start | bytes 786440 | tf_op jit(solution)/shard_map/ppermute | solution.py:615
  83.2 0.0 copy-start.13
  83.2 2.3 %far_stage.7 = bf16[512,256]{1,0:T(8,128)(2,1)S(1)} custom-call(s32[1]{0:T(128)} %bitcast.z, s32[16,4]{1,0:T(8,128)S(1)} %get-tuple-element.30.slots, f32[16]{0:T(128)S(1)} %copy-done.10, bf16[512,256]{1,0:T(8,128)(2,1)S(1)} %collective-permute-done.6.rest_0_.q, f32[2,4,256,128]{3,2,1,0:T(8,128)S(1)} %copy-done.4, bf16[2,4,256,128]{3,2,1,0:T(8,128)(2,1)S(1)} %copy-done.7, ...), custom_call_target="tpu_custom_call" | custom-call | flops 536870912 | bytes 4194304 | tf_op jit(solution)/shard_map/far_stage/pallas_call | solution.py:539
  85.6 0.0 copy-start
  85.6 0.0 copy-start.1
  85.6 0.8 collective-permute-start.11
  86.4 2.3 %far_stage.4.a0 = bf16[512,256]{1,0:T(8,128)(2,1)S(1)} custom-call(s32[1]{0:T(128)} %bitcast.z, s32[16,4]{1,0:T(8,128)S(1)} %get-tuple-element.30.slots, f32[16]{0:T(128)S(1)} %copy-done.10, bf16[512,256]{1,0:T(8,128)(2,1)S(1)} %copy-done.9, f32[2,4,256,128]{3,2,1,0:T(8,128)S(1)} %copy-done.2, bf16[2,4,256,128]{3,2,1,0:T(8,128)(2,1)S(1)} %copy-done.5, ...), custom_call_target="tpu_custom_call" | custom-call | flops 536870912 | bytes 4194304 | tf_op jit(solution)/shard_map/far_stage/pallas_call | solution.py:539
  88.7 0.0 copy-start.11
  88.7 0.0 collective-permute-done.10.a2
  88.7 1.3 %collective-permute-done.9.a1 = bf16[512,256]{1,0:T(8,128)(2,1)S(1)} collective-permute-done((bf16[512,256]{1,0:T(8,128)(2,1)S(1)}, bf16[512,256]{1,0:T(8,128)(2,1)S(1)}, u32[]{:S(2)}, u32[]{:S(2)}) %collective-permute-start.9) | collective-permute-done | bytes 262176 | tf_op jit(solution)/shard_map/ppermute | solution.py:615
  90.1 1.0 mid_stage.1.mid_in
  91.1 2.2 %collective-permute-done.11.a3 = bf16[512,256]{1,0:T(8,128)(2,1)S(1)} collective-permute-done((bf16[512,256]{1,0:T(8,128)(2,1)S(1)}, bf16[512,256]{1,0:T(8,128)(2,1)S(1)}, u32[]{:S(2)}, u32[]{:S(2)}) %collective-permute-start.11) | collective-permute-done | bytes 262176 | tf_op jit(solution)/shard_map/ppermute | solution.py:615
  93.2 8.2 %ffn_stage.1 = bf16[512,1024]{1,0:T(8,128)(2,1)} custom-call(s32[1]{0:T(128)} %bitcast.z, f32[512,1024]{1,0:T(8,128)S(1)} %mid_stage.1.mid_in, bf16[512,256]{1,0:T(8,128)(2,1)S(1)} %collective-permute-done.11.a3, bf16[1024,1024]{1,0:T(8,128)(2,1)S(1)} %copy-done.1, bf16[1024,2048]{1,0:T(8,128)(2,1)S(1)} %copy-done.11, bf16[1024,2048]{1,0:T(8,128)(2,1)S(1)} %copy-done.12, ...), custom_call_target="tpu_custom_call" | custom-call | flops 6710886400 | bytes 18874368 | tf_op jit(solution)/shard_map/ffn_stage/pallas_call | solution.py:602
  (32 shorter events, 0.1 us)
Async XLA Ops:
  5.8 19.5 %all-to-all-start = ((bf16[32,48,128]{2,1,0:T(8,128)(2,1)}), bf16[32,48,128]{2,1,0:T(8,128)(2,1)S(1)}, u32[]{:S(2)}, u32[]{:S(2)}) async-start(bf16[32,48,128]{2,1,0:T(8,128)(2,1)} %get-tuple-element.33), calls=%async_computation | async-start | bytes 786432 | tf_op jit(solution)/shard_map/all_to_all | solution.py:624
  13.2 8.0 %collective-permute-start = (bf16[512,128]{1,0:T(8,128)(2,1)S(1)}, bf16[512,128]{1,0:T(8,128)(2,1)S(1)}, u32[]{:S(2)}, u32[]{:S(2)}) collective-permute-start(bf16[512,128]{1,0:T(8,128)(2,1)S(1)} %get-tuple-element.35), channel_id=1, source_target_pairs={{0,1},{1,2},{2,3},{3,0},{4,5},{5,6},{6,7},{7,4},{8,9},{9,10},{10,1... | collective-permute-start | bytes 393224 | tf_op jit(solution)/shard_map/ppermute | solution.py:615
  15.2 10.0 %collective-permute-start.1 = (bf16[512,128]{1,0:T(8,128)(2,1)S(1)}, bf16[512,128]{1,0:T(8,128)(2,1)S(1)}, u32[]{:S(2)}, u32[]{:S(2)}) collective-permute-start(bf16[512,128]{1,0:T(8,128)(2,1)S(1)} %get-tuple-element.36), channel_id=1, source_target_pairs={{0,2},{1,3},{2,0},{3,1},{4,6},{5,7},{6,4},{7,5},{8,10},{9,11},{10,... | collective-permute-start | bytes 393224 | tf_op jit(solution)/shard_map/ppermute | solution.py:615
  18.8 6.5 %collective-permute-start.2 = (bf16[512,128]{1,0:T(8,128)(2,1)S(1)}, bf16[512,128]{1,0:T(8,128)(2,1)S(1)}, u32[]{:S(2)}, u32[]{:S(2)}) collective-permute-start(bf16[512,128]{1,0:T(8,128)(2,1)S(1)} %get-tuple-element.37), channel_id=1, source_target_pairs={{0,3},{1,0},{2,1},{3,2},{4,7},{5,4},{6,5},{7,6},{8,11},{9,8},{10,9... | collective-permute-start | bytes 393224 | tf_op jit(solution)/shard_map/ppermute | solution.py:615
  28.9 44.6 %all-to-all-start.1 = ((bf16[32,256,128]{2,1,0:T(8,128)(2,1)}), bf16[32,256,128]{2,1,0:T(8,128)(2,1)S(1)}, u32[]{:S(2)}, u32[]{:S(2)}) async-start(bf16[32,256,128]{2,1,0:T(8,128)(2,1)} %bitcast.8), calls=%async_computation.1 | async-start | bytes 4194304 | tf_op jit(solution)/shard_map/all_to_all | solution.py:628
  36.2 19.0 %copy-start.10 = (f32[16]{0:T(128)S(1)}, f32[16]{0:T(128)}, u32[]{:S(2)}) copy-start(f32[16]{0:T(128)} %scale.13) | copy-start | bytes 196
  36.2 1.6 %copy-start.14 = (bf16[1024,1024]{1,0:T(8,128)(2,1)S(1)}, bf16[1024,1024]{1,0:T(8,128)(2,1)}, u32[]{:S(2)}) copy-start(bf16[1024,1024]{1,0:T(8,128)(2,1)} %w_query.1) | copy-start | bytes 6291460
  37.8 5.5 %copy-start.19 = (bf16[256,128]{1,0:T(8,128)(2,1)S(1)}, bf16[256,128]{1,0:T(8,128)(2,1)}, u32[]{:S(2)}) copy-start(bf16[256,128]{1,0:T(8,128)(2,1)} %get-tuple-element.40) | copy-start | bytes 196612
  37.8 6.5 %copy-start.18 = (bf16[256,128]{1,0:T(8,128)(2,1)S(1)}, bf16[256,128]{1,0:T(8,128)(2,1)}, u32[]{:S(2)}) copy-start(bf16[256,128]{1,0:T(8,128)(2,1)} %get-tuple-element.41) | copy-start | bytes 196612
  37.8 9.0 %copy-start.17 = (bf16[256,128]{1,0:T(8,128)(2,1)S(1)}, bf16[256,128]{1,0:T(8,128)(2,1)}, u32[]{:S(2)}) copy-start(bf16[256,128]{1,0:T(8,128)(2,1)} %get-tuple-element.42) | copy-start | bytes 196612
  37.8 17.4 %copy-start.15 = (bf16[4,4,128,128]{3,2,1,0:T(8,128)(2,1)S(1)}, bf16[4,4,128,128]{3,2,1,0:T(8,128)(2,1)}, u32[]{:S(2)}) copy-start(bf16[4,4,128,128]{3,2,1,0:T(8,128)(2,1)} %get-tuple-element.38.kv) | copy-start | bytes 1572868
  37.8 17.4 %copy-start.16 = (bf16[256,128]{1,0:T(8,128)(2,1)S(1)}, bf16[256,128]{1,0:T(8,128)(2,1)}, u32[]{:S(2)}) copy-start(bf16[256,128]{1,0:T(8,128)(2,1)} %get-tuple-element.39.s0) | copy-start | bytes 196612
  42.0 18.7 %collective-permute-start.8 = (bf16[512,256]{1,0:T(8,128)(2,1)}, bf16[512,256]{1,0:T(8,128)(2,1)S(1)}, u32[]{:S(2)}, u32[]{:S(2)}) collective-permute-start(bf16[512,256]{1,0:T(8,128)(2,1)} %get-tuple-element.48), channel_id=1, source_target_pairs={{0,1},{1,2},{2,3},{3,0},{4,5},{5,6},{6,7},{7,4},{8,9},{9,10},{10,1... | collective-permute-start | bytes 786440 | tf_op jit(solution)/shard_map/ppermute | solution.py:615
  43.3 10.4 %collective-permute-start.3 = (bf16[256,128]{1,0:T(8,128)(2,1)S(1)}, bf16[256,128]{1,0:T(8,128)(2,1)S(1)}, u32[]{:S(2)}, u32[]{:S(2)}) collective-permute-start(bf16[256,128]{1,0:T(8,128)(2,1)S(1)} %copy-done.19), channel_id=1, source_target_pairs={{0,1},{1,2},{2,3},{3,0},{4,5},{5,6},{6,7},{7,4},{8,9},{9,10},{10,1... | collective-permute-start | bytes 196616 | tf_op jit(solution)/shard_map/ppermute | solution.py:615
  44.2 10.9 %collective-permute-start.4 = (bf16[256,128]{1,0:T(8,128)(2,1)S(1)}, bf16[256,128]{1,0:T(8,128)(2,1)S(1)}, u32[]{:S(2)}, u32[]{:S(2)}) collective-permute-start(bf16[256,128]{1,0:T(8,128)(2,1)S(1)} %copy-done.18), channel_id=1, source_target_pairs={{0,2},{1,3},{2,0},{3,1},{4,6},{5,7},{6,4},{7,5},{8,10},{9,11},{10,... | collective-permute-start | bytes 196616 | tf_op jit(solution)/shard_map/ppermute | solution.py:615
  46.7 8.4 %collective-permute-start.5 = (bf16[256,128]{1,0:T(8,128)(2,1)S(1)}, bf16[256,128]{1,0:T(8,128)(2,1)S(1)}, u32[]{:S(2)}, u32[]{:S(2)}) collective-permute-start(bf16[256,128]{1,0:T(8,128)(2,1)S(1)} %copy-done.17), channel_id=1, source_target_pairs={{0,3},{1,0},{2,1},{3,2},{4,7},{5,4},{6,5},{7,6},{8,11},{9,8},{10,9... | collective-permute-start | bytes 196616 | tf_op jit(solution)/shard_map/ppermute | solution.py:615
  48.3 16.9 %collective-permute-start.6 = (bf16[512,256]{1,0:T(8,128)(2,1)}, bf16[512,256]{1,0:T(8,128)(2,1)S(1)}, u32[]{:S(2)}, u32[]{:S(2)}) collective-permute-start(bf16[512,256]{1,0:T(8,128)(2,1)} %get-tuple-element.46), channel_id=1, source_target_pairs={{0,3},{1,0},{2,1},{3,2},{4,7},{5,4},{6,5},{7,6},{8,11},{9,8},{10,9... | collective-permute-start | bytes 786440 | tf_op jit(solution)/shard_map/ppermute | solution.py:615
  53.6 11.6 %collective-permute-start.7 = (bf16[512,256]{1,0:T(8,128)(2,1)}, bf16[512,256]{1,0:T(8,128)(2,1)S(1)}, u32[]{:S(2)}, u32[]{:S(2)}) collective-permute-start(bf16[512,256]{1,0:T(8,128)(2,1)} %get-tuple-element.47), channel_id=1, source_target_pairs={{0,2},{1,3},{2,0},{3,1},{4,6},{5,7},{6,4},{7,5},{8,10},{9,11},{10,... | collective-permute-start | bytes 786440 | tf_op jit(solution)/shard_map/ppermute | solution.py:615
  55.1 1.0 copy-start.8
  73.5 5.9 %copy-start.3 = (f32[2,4,256,128]{3,2,1,0:T(8,128)S(1)}, f32[2,4,256,128]{3,2,1,0:T(8,128)}, u32[]{:S(2)}) copy-start(f32[2,4,256,128]{3,2,1,0:T(8,128)} %get-tuple-element.49.rest_2_.state) | copy-start | bytes 3145732
  73.5 5.9 %copy-start.6 = (bf16[2,4,256,128]{3,2,1,0:T(8,128)(2,1)S(1)}, bf16[2,4,256,128]{3,2,1,0:T(8,128)(2,1)}, u32[]{:S(2)}) copy-start(bf16[2,4,256,128]{3,2,1,0:T(8,128)(2,1)} %get-tuple-element.50.rest_3_.peaks) | copy-start | bytes 1572868
  77.0 6.1 %copy-start.4 = (f32[2,4,256,128]{3,2,1,0:T(8,128)S(1)}, f32[2,4,256,128]{3,2,1,0:T(8,128)}, u32[]{:S(2)}) copy-start(f32[2,4,256,128]{3,2,1,0:T(8,128)} %get-tuple-element.53.state) | copy-start | bytes 3145732
  77.0 6.1 %copy-start.7 = (bf16[2,4,256,128]{3,2,1,0:T(8,128)(2,1)S(1)}, bf16[2,4,256,128]{3,2,1,0:T(8,128)(2,1)}, u32[]{:S(2)}) copy-start(bf16[2,4,256,128]{3,2,1,0:T(8,128)(2,1)} %get-tuple-element.54.peaks) | copy-start | bytes 1572868
  77.1 11.7 %collective-permute-start.10 = (bf16[512,256]{1,0:T(8,128)(2,1)S(1)}, bf16[512,256]{1,0:T(8,128)(2,1)S(1)}, u32[]{:S(2)}, u32[]{:S(2)}) collective-permute-start(bf16[512,256]{1,0:T(8,128)(2,1)S(1)} %far_stage.6), channel_id=1, source_target_pairs={{0,2},{1,3},{2,0},{3,1},{4,6},{5,7},{6,4},{7,5},{8,10},{9,11},{10,... | collective-permute-start | bytes 786440 | tf_op jit(solution)/shard_map/ppermute | solution.py:615
  81.8 8.3 %collective-permute-start.9 = (bf16[512,256]{1,0:T(8,128)(2,1)S(1)}, bf16[512,256]{1,0:T(8,128)(2,1)S(1)}, u32[]{:S(2)}, u32[]{:S(2)}) collective-permute-start(bf16[512,256]{1,0:T(8,128)(2,1)S(1)} %far_stage.5), channel_id=1, source_target_pairs={{0,3},{1,0},{2,1},{3,2},{4,7},{5,4},{6,5},{7,6},{8,11},{9,8},{10,9... | collective-permute-start | bytes 786440 | tf_op jit(solution)/shard_map/ppermute | solution.py:615
  83.2 3.2 %copy-start.2 = (f32[2,4,256,128]{3,2,1,0:T(8,128)S(1)}, f32[2,4,256,128]{3,2,1,0:T(8,128)}, u32[]{:S(2)}) copy-start(f32[2,4,256,128]{3,2,1,0:T(8,128)} %get-tuple-element.43.rest_1_.state) | copy-start | bytes 3145732
  83.2 3.2 %copy-start.5 = (bf16[2,4,256,128]{3,2,1,0:T(8,128)(2,1)S(1)}, bf16[2,4,256,128]{3,2,1,0:T(8,128)(2,1)}, u32[]{:S(2)}) copy-start(bf16[2,4,256,128]{3,2,1,0:T(8,128)(2,1)} %get-tuple-element.44.rest_2_.peaks) | copy-start | bytes 1572868
  83.2 3.2 %copy-start.9 = (bf16[512,256]{1,0:T(8,128)(2,1)S(1)}, bf16[512,256]{1,0:T(8,128)(2,1)}, u32[]{:S(2)}) copy-start(bf16[512,256]{1,0:T(8,128)(2,1)} %get-tuple-element.32.rest_0_.q) | copy-start | bytes 786436
  83.2 10.0 %copy-start.13 = (bf16[2048,1024]{1,0:T(8,128)(2,1)S(1)}, bf16[2048,1024]{1,0:T(8,128)(2,1)}, u32[]{:S(2)}) copy-start(bf16[2048,1024]{1,0:T(8,128)(2,1)} %w_down.1) | copy-start | bytes 12582916
  85.6 4.5 %copy-start = (bf16[512,1024]{1,0:T(8,128)(2,1)S(1)}, bf16[512,1024]{1,0:T(8,128)(2,1)}, u32[]{:S(2)}) copy-start(bf16[512,1024]{1,0:T(8,128)(2,1)} %tokens.1) | copy-start | bytes 3145732
  85.6 4.5 %copy-start.1 = (bf16[1024,1024]{1,0:T(8,128)(2,1)S(1)}, bf16[1024,1024]{1,0:T(8,128)(2,1)}, u32[]{:S(2)}) copy-start(bf16[1024,1024]{1,0:T(8,128)(2,1)} %w_out.3) | copy-start | bytes 6291460
  85.6 7.7 %collective-permute-start.11 = (bf16[512,256]{1,0:T(8,128)(2,1)S(1)}, bf16[512,256]{1,0:T(8,128)(2,1)S(1)}, u32[]{:S(2)}, u32[]{:S(2)}) collective-permute-start(bf16[512,256]{1,0:T(8,128)(2,1)S(1)} %far_stage.7), channel_id=1, source_target_pairs={{0,1},{1,2},{2,3},{3,0},{4,5},{5,6},{6,7},{7,4},{8,9},{9,10},{10,1... | collective-permute-start | bytes 786440 | tf_op jit(solution)/shard_map/ppermute | solution.py:615
  86.4 6.9 %copy-start.12 = (bf16[1024,2048]{1,0:T(8,128)(2,1)S(1)}, bf16[1024,2048]{1,0:T(8,128)(2,1)}, u32[]{:S(2)}) copy-start(bf16[1024,2048]{1,0:T(8,128)(2,1)} %w_up.1) | copy-start | bytes 12582916
  88.7 4.5 %copy-start.11 = (bf16[1024,2048]{1,0:T(8,128)(2,1)S(1)}, bf16[1024,2048]{1,0:T(8,128)(2,1)}, u32[]{:S(2)}) copy-start(bf16[1024,2048]{1,0:T(8,128)(2,1)} %w_gate.1) | copy-start | bytes 12582916

commit v6 on v5

--- a/solution.py
+++ b/solution.py
@@ -278,6 +278,12 @@
     for k, c in enumerate((c0, c1, c2, c3)):
         held[k] = c[...].reshape(PER, BLOCK, PAIR_W)
     outs = [pltpu.make_async_copy(held, kv_out, sum_sems.at[ZS + 1])]
+    outs[0].start()
+    for k, s in enumerate((s0, s1, s2, s3)):
+        start = pl.multiple_of(((z[0] + k) % ZS) * SUM_LOCAL, SUM_LOCAL)
+        sums[k] = told[:, pl.ds(start, SUM_LOCAL), :].reshape(PTS * SUM_LOCAL, PAIR_W)
+        outs.append(pltpu.make_async_copy(sums.at[k], s, sum_sems.at[k]))
+        outs[-1].start()
     fetch.wait()
 
     def copy(i):
@@ -294,12 +300,6 @@
         return 0
 
     lax.fori_loop(0, PTS * CAP, start_one, 0, unroll=4)
-    for k, s in enumerate((s0, s1, s2, s3)):
-        start = pl.multiple_of(((z[0] + k) % ZS) * SUM_LOCAL, SUM_LOCAL)
-        sums[k] = told[:, pl.ds(start, SUM_LOCAL), :].reshape(PTS * SUM_LOCAL, PAIR_W)
-        outs.append(pltpu.make_async_copy(sums.at[k], s, sum_sems.at[k]))
-    for c in outs:
-        c.start()
     lax.fori_loop(0, PTS * CAP, wait_one, 0, unroll=4)
     for c in outs:
         c.wait()
@@ -634,7 +634,8 @@
     states = [None] * ZS
     done = []
     for group in GROUPS:
-        made = near_stage(group, z, logit_scale, [q[k] for k in group], kv, sums, done)
+        rows = pairs[0].reshape(1, PER, BLOCK, PAIR_W) if group == (0,) else kv
+        made = near_stage(group, z, logit_scale, [q[k] for k in group], rows, sums, done)
         for k, one in zip(group, made):
             states[k] = one
         done = made[-1]

time: 102 us -> 102 us (level)
  no operation moved by 1% of the time
where the time goes in v6:
time: 102 us; the launch traced here: 101 us
  Pallas kernels  50.3 us (49%)
  starting transfers between devices  33 us (32%)
  waiting for transfers between devices  14.9 us (15%)
  local copies, waits for them, and re-layouts  2.62 us (3%)
    ppermute x12, starting transfers between devices, shift(): return lax.ppermute(array, 'head', [(i, (i + k) % ZS) for i in range(ZS)])  18.4 us
    pallas_call x3, Pallas kernels, near_stage(): pl.pallas_call(functools.partial(near_body, chunks), name='near_stage', i...  17.4 us
    ppermute x12, waiting for transfers between devices, shift(): return lax.ppermute(array, 'head', [(i, (i + k) % ZS) for i in range(ZS)])  14.9 us
    pallas_call x4, Pallas kernels, far_stage(): pl.pallas_call(functools.partial(far_body, shift_by, direct), name='far_s...  10.5 us
    pallas_call x1, Pallas kernels, ffn_stage(): pl.pallas_call(ffn_body, name='ffn_stage', in_specs=[whole(SMEM)] + [whol...  8.24 us
    all_to_all x1, starting transfers between devices, body(): lax.all_to_all(payload, 'pts', split_axis=0, concat_axis=0, tiled=True)  7.44 us
    all_to_all x1, starting transfers between devices, body(): lax.all_to_all(replies, 'pts', split_axis=0, concat_axis=0, tiled=True)  7.24 us
    pallas_call x1, Pallas kernels, first_stage(): pl.pallas_call(first_body, name='first_stage', in_specs=[whole(SMEM)] + [...  5.79 us
  transfers between devices with their start and end apart: 14, of which 6 were waited for; matrix products, arithmetic and copies ran while one was open for 0% of the time, Pallas kernels for 29%

profile of v6, /device:TPU:0, one launch (start us, length us, event | category | flops | bytes accessed | tf_op | source)
XLA Modules:
  0.0 101.1 jit_solution(12988851672266244583)
XLA Ops:
  0.0 5.8 %first_stage.1 = (bf16[512,128]{1,0:T(8,128)(2,1)S(1)}, bf16[512,128]{1,0:T(8,128)(2,1)S(1)}, bf16[512,128]{1,0:T(8,128)(2,1)S(1)}, bf16[512,128]{1,0:T(8,128)(2...) custom-call(s32[1]{0:T(128)} %bitcast.z, s32[4,16]{1,0:T(4,128)} %bitcast.11, ...), custom_call_target="tpu_custom_call" | custom-call | flops 536870912 | bytes 4194304 | tf_op jit(solution)/shard_map/first_stage/pallas_call | solution.py:191
  5.8 7.4 %all-to-all-start = ((bf16[32,48,128]{2,1,0:T(8,128)(2,1)}), bf16[32,48,128]{2,1,0:T(8,128)(2,1)S(1)}, u32[]{:S(2)}, u32[]{:S(2)}) async-start(bf16[32,48,128]{2,1,0:T(8,128)(2,1)} %get-tuple-element.34), calls=%async_computation | async-start | bytes 786432 | tf_op jit(solution)/shard_map/all_to_all | solution.py:624
  13.2 2.0 %collective-permute-start = (bf16[512,128]{1,0:T(8,128)(2,1)S(1)}, bf16[512,128]{1,0:T(8,128)(2,1)S(1)}, u32[]{:S(2)}, u32[]{:S(2)}) collective-permute-start(bf16[512,128]{1,0:T(8,128)(2,1)S(1)} %get-tuple-element.35), channel_id=1, source_target_pairs={{0,1},{1,2},{2,3},{3,0},{4,5},{5,6},{6,7},{7,4},{8,9},{9,10},{10,1... | collective-permute-start | bytes 393224 | tf_op jit(solution)/shard_map/ppermute | solution.py:615
  15.2 3.6 %collective-permute-start.1 = (bf16[512,128]{1,0:T(8,128)(2,1)S(1)}, bf16[512,128]{1,0:T(8,128)(2,1)S(1)}, u32[]{:S(2)}, u32[]{:S(2)}) collective-permute-start(bf16[512,128]{1,0:T(8,128)(2,1)S(1)} %get-tuple-element.36), channel_id=1, source_target_pairs={{0,2},{1,3},{2,0},{3,1},{4,6},{5,7},{6,4},{7,5},{8,10},{9,11},{10,... | collective-permute-start | bytes 393224 | tf_op jit(solution)/shard_map/ppermute | solution.py:615
  18.8 1.0 collective-permute-start.2
  19.8 1.5 %collective-permute-done.c1 = bf16[512,128]{1,0:T(8,128)(2,1)S(1)} collective-permute-done((bf16[512,128]{1,0:T(8,128)(2,1)S(1)}, bf16[512,128]{1,0:T(8,128)(2,1)S(1)}, u32[]{:S(2)}, u32[]{:S(2)}) %collective-permute-start) | collective-permute-done | bytes 131104 | tf_op jit(solution)/shard_map/ppermute | solution.py:615
  21.3 4.0 %collective-permute-done.1.c2 = bf16[512,128]{1,0:T(8,128)(2,1)S(1)} collective-permute-done((bf16[512,128]{1,0:T(8,128)(2,1)S(1)}, bf16[512,128]{1,0:T(8,128)(2,1)S(1)}, u32[]{:S(2)}, u32[]{:S(2)}) %collective-permute-start.1) | collective-permute-done | bytes 131104 | tf_op jit(solution)/shard_map/ppermute | solution.py:615
  25.3 0.0 collective-permute-done.2.c3
  25.3 0.0 all-to-all-done.told
  25.3 3.3 %reply_stage.1 = (bf16[64,128,128]{2,1,0:T(8,128)(2,1)}, bf16[256,128]{1,0:T(8,128)(2,1)}, bf16[256,128]{1,0:T(8,128)(2,1)}, bf16[256,128]{1,0:T(8,128)(2,1)}, b...) custom-call(s32[1]{0:T(128)} %bitcast.z, bf16[32,48,128]{2,1,0:T(8,128)(2,1)S(1)} %all-to-all-done.told, ...), custom_call_target="tpu_custom_call" | custom-call | tf_op jit(solution)/shard_map/reply_stage/pallas_call | solution.py:310
  28.6 7.2 %all-to-all-start.1 = ((bf16[32,256,128]{2,1,0:T(8,128)(2,1)}), bf16[32,256,128]{2,1,0:T(8,128)(2,1)S(1)}, u32[]{:S(2)}, u32[]{:S(2)}) async-start(bf16[32,256,128]{2,1,0:T(8,128)(2,1)} %bitcast.10), calls=%async_computation.1 | async-start | bytes 4194304 | tf_op jit(solution)/shard_map/all_to_all | solution.py:628
  35.8 0.0 copy-start.10
  35.9 0.0 copy-start.14
  35.9 1.6 %copy-done.14 = bf16[1024,1024]{1,0:T(8,128)(2,1)S(1)} copy-done((bf16[1024,1024]{1,0:T(8,128)(2,1)S(1)}, bf16[1024,1024]{1,0:T(8,128)(2,1)}, u32[]{:S(2)}) %copy-start.14) | copy-done | bytes 2097176
  37.5 4.1 %q_stage.1 = (bf16[512,256]{1,0:T(8,128)(2,1)}, bf16[512,256]{1,0:T(8,128)(2,1)}, bf16[512,256]{1,0:T(8,128)(2,1)}, bf16[512,256]{1,0:T(8,128)(2,1)}) custom-call(s32[1]{0:T(128)} %bitcast.z, bf16[512,1024]{1,0:T(8,128)(2,1)} %get-tuple-element.31.normed_in, bf16[1024,1024]{1,0:T(8,128)(2,1)S(1)} %copy-done.14), custom_call_target="tpu_custom_call" | custom-call | flops 1073741824 | bytes 4194304 | tf_op jit(solution)/shard_map/q_stage/pallas_call | solution.py:255
  41.6 1.3 %collective-permute-start.8 = (bf16[512,256]{1,0:T(8,128)(2,1)}, bf16[512,256]{1,0:T(8,128)(2,1)S(1)}, u32[]{:S(2)}, u32[]{:S(2)}) collective-permute-start(bf16[512,256]{1,0:T(8,128)(2,1)} %get-tuple-element.48), channel_id=1, source_target_pairs={{0,1},{1,2},{2,3},{3,0},{4,5},{5,6},{6,7},{7,4},{8,9},{9,10},{10,1... | collective-permute-start | bytes 786440 | tf_op jit(solution)/shard_map/ppermute | solution.py:615
  42.9 1.0 collective-permute-start.3
  43.9 2.5 %collective-permute-start.4 = (bf16[256,128]{1,0:T(8,128)(2,1)S(1)}, bf16[256,128]{1,0:T(8,128)(2,1)S(1)}, u32[]{:S(2)}, u32[]{:S(2)}) collective-permute-start(bf16[256,128]{1,0:T(8,128)(2,1)S(1)} %copy-done.18), channel_id=1, source_target_pairs={{0,2},{1,3},{2,0},{3,1},{4,6},{5,7},{6,4},{7,5},{8,10},{9,11},{10,... | collective-permute-start | bytes 196616 | tf_op jit(solution)/shard_map/ppermute | solution.py:615
  46.4 1.6 %collective-permute-start.5 = (bf16[256,128]{1,0:T(8,128)(2,1)S(1)}, bf16[256,128]{1,0:T(8,128)(2,1)S(1)}, u32[]{:S(2)}, u32[]{:S(2)}) collective-permute-start(bf16[256,128]{1,0:T(8,128)(2,1)S(1)} %copy-done.17), channel_id=1, source_target_pairs={{0,3},{1,0},{2,1},{3,2},{4,7},{5,4},{6,5},{7,6},{8,11},{9,8},{10,9... | collective-permute-start | bytes 196616 | tf_op jit(solution)/shard_map/ppermute | solution.py:615
  47.9 0.0 collective-permute-start.6
  48.0 5.3 %collective-permute-done.3.s1 = bf16[256,128]{1,0:T(8,128)(2,1)S(1)} collective-permute-done((bf16[256,128]{1,0:T(8,128)(2,1)S(1)}, bf16[256,128]{1,0:T(8,128)(2,1)S(1)}, u32[]{:S(2)}, u32[]{:S(2)}) %collective-permute-start.3) | collective-permute-done | bytes 65568 | tf_op jit(solution)/shard_map/ppermute | solution.py:615
  53.3 0.9 collective-permute-start.7
  54.2 0.6 collective-permute-done.4.s2
  54.8 0.0 collective-permute-done.5.s3
  54.8 0.9 copy-done.8
  55.7 4.6 %near_stage.3 = (f32[2,4,256,128]{3,2,1,0:T(8,128)}, bf16[2,4,256,128]{3,2,1,0:T(8,128)(2,1)}) custom-call(s32[1]{0:T(128)} %bitcast.z, f32[16]{0:T(128)S(1)} %copy-done.10, bf16[1,4,128,128]{3,2,1,0:T(8,128)(2,1)S(1)} %bitcast.9, bf16[256,128]{1,0:T(8,128)(2,1)S(1)} %copy-done.16, bf16[256,128]{1,0:T(8,128)(2,1)S(1)} %collective-permute-done.3.s1, ...), custom_call_target="tpu_custom_call" | custom-call | flops 1342177280 | bytes 2097152 | tf_op jit(solution)/shard_map/near_stage/pallas_call | solution.py:426
  60.3 0.0 collective-permute-done.8.rest_0_.q
  60.3 4.5 %near_stage.4 = (f32[2,4,256,128]{3,2,1,0:T(8,128)}, bf16[2,4,256,128]{3,2,1,0:T(8,128)(2,1)}) custom-call(s32[1]{0:T(128)} %bitcast.z, f32[16]{0:T(128)S(1)} %copy-done.10, bf16[4,4,128,128]{3,2,1,0:T(8,128)(2,1)S(1)} %copy-done.15, bf16[256,128]{1,0:T(8,128)(2,1)S(1)} %copy-done.16, bf16[256,128]{1,0:T(8,128)(2,1)S(1)} %collective-permute-done.3.s1, ...), custom_call_target="tpu_custom_call" | custom-call | flops 1342177280 | bytes 2097152 | tf_op jit(solution)/shard_map/near_stage/pallas_call | solution.py:426
  64.9 0.0 collective-permute-done.6.rest_0_.q
  64.9 0.0 collective-permute-done.7.rest_1_.q
  64.9 8.3 %near_stage.5 = (f32[2,4,256,128]{3,2,1,0:T(8,128)}, bf16[2,4,256,128]{3,2,1,0:T(8,128)(2,1)}, f32[2,4,256,128]{3,2,1,0:T(8,128)}, bf16[2,4,256,128]{3,2,1,0:T(8,128)(2,1)}) custom-call(s32[1]{0:T(128)} %bitcast.z, f32[16]{0:T(128)S(1)} %copy-done.10, bf16[4,4,128,128]{3,2,1,0:T(8,128)(2,1)S(1)} %copy-done.15, bf16[256,128]{1,0:T(8,128)(2,1)S(1)} %copy-done.16, ...), custom_call_target="tpu_custom_call" | custom-call | flops 2684354560 | bytes 2097152 | tf_op jit(solution)/shard_map/near_stage/pallas_call | solution.py:426
  73.2 0.0 all-to-all-done.1
  73.2 3.5 %far_stage.6 = bf16[512,256]{1,0:T(8,128)(2,1)S(1)} custom-call(s32[1]{0:T(128)} %bitcast.z, s32[16,4]{1,0:T(8,128)S(1)} %get-tuple-element.30.slots, f32[16]{0:T(128)S(1)} %copy-done.10, bf16[512,256]{1,0:T(8,128)(2,1)S(1)} %collective-permute-done.7.rest_1_.q, f32[2,4,256,128]{3,2,1,0:T(8,128)} %get-tuple-element.51.rest_0_.state, ...), custom_call_target="tpu_custom_call" | custom-call | flops 536870912 | bytes 4194304 | tf_op jit(solution)/shard_map/far_stage/pallas_call | solution.py:539
  76.7 2.4 %collective-permute-start.10 = (bf16[512,256]{1,0:T(8,128)(2,1)S(1)}, bf16[512,256]{1,0:T(8,128)(2,1)S(1)}, u32[]{:S(2)}, u32[]{:S(2)}) collective-permute-start(bf16[512,256]{1,0:T(8,128)(2,1)S(1)} %far_stage.6), channel_id=1, source_target_pairs={{0,2},{1,3},{2,0},{3,1},{4,6},{5,7},{6,4},{7,5},{8,10},{9,11},{10,... | collective-permute-start | bytes 786440 | tf_op jit(solution)/shard_map/ppermute | solution.py:615
  79.1 2.3 %far_stage.5 = bf16[512,256]{1,0:T(8,128)(2,1)S(1)} custom-call(s32[1]{0:T(128)} %bitcast.z, s32[16,4]{1,0:T(8,128)S(1)} %get-tuple-element.30.slots, f32[16]{0:T(128)S(1)} %copy-done.10, bf16[512,256]{1,0:T(8,128)(2,1)S(1)} %collective-permute-done.8.rest_0_.q, f32[2,4,256,128]{3,2,1,0:T(8,128)S(1)} %copy-done.3, bf16[2,4,256,128]{3,2,1,0:T(8,128)(2,1)S(1)} %copy-done.6, ...), custom_call_target="tpu_custom_call" | custom-call | flops 536870912 | bytes 4194304 | tf_op jit(solution)/shard_map/far_stage/pallas_call | solution.py:539
  81.4 1.4 %collective-permute-start.9 = (bf16[512,256]{1,0:T(8,128)(2,1)S(1)}, bf16[512,256]{1,0:T(8,128)(2,1)S(1)}, u32[]{:S(2)}, u32[]{:S(2)}) collective-permute-start(bf16[512,256]{1,0:T(8,128)(2,1)S(1)} %far_stage.5), channel_id=1, source_target_pairs={{0,3},{1,0},{2,1},{3,2},{4,7},{5,4},{6,5},{7,6},{8,11},{9,8},{10,9... | collective-permute-start | bytes 786440 | tf_op jit(solution)/shard_map/ppermute | solution.py:615
  82.8 0.0 copy-start.13
  82.9 2.3 %far_stage.7 = bf16[512,256]{1,0:T(8,128)(2,1)S(1)} custom-call(s32[1]{0:T(128)} %bitcast.z, s32[16,4]{1,0:T(8,128)S(1)} %get-tuple-element.30.slots, f32[16]{0:T(128)S(1)} %copy-done.10, bf16[512,256]{1,0:T(8,128)(2,1)S(1)} %collective-permute-done.6.rest_0_.q, f32[2,4,256,128]{3,2,1,0:T(8,128)S(1)} %copy-done.4, bf16[2,4,256,128]{3,2,1,0:T(8,128)(2,1)S(1)} %copy-done.7, ...), custom_call_target="tpu_custom_call" | custom-call | flops 536870912 | bytes 4194304 | tf_op jit(solution)/shard_map/far_stage/pallas_call | solution.py:539
  85.2 0.0 copy-start
  85.2 0.0 copy-start.1
  85.2 0.8 collective-permute-start.11
  86.0 2.3 %far_stage.4.a0 = bf16[512,256]{1,0:T(8,128)(2,1)S(1)} custom-call(s32[1]{0:T(128)} %bitcast.z, s32[16,4]{1,0:T(8,128)S(1)} %get-tuple-element.30.slots, f32[16]{0:T(128)S(1)} %copy-done.10, bf16[512,256]{1,0:T(8,128)(2,1)S(1)} %copy-done.9, f32[2,4,256,128]{3,2,1,0:T(8,128)S(1)} %copy-done.2, bf16[2,4,256,128]{3,2,1,0:T(8,128)(2,1)S(1)} %copy-done.5, ...), custom_call_target="tpu_custom_call" | custom-call | flops 536870912 | bytes 4194304 | tf_op jit(solution)/shard_map/far_stage/pallas_call | solution.py:539
  88.4 0.0 copy-start.11
  88.4 0.0 collective-permute-done.10.a2
  88.4 1.3 %collective-permute-done.9.a1 = bf16[512,256]{1,0:T(8,128)(2,1)S(1)} collective-permute-done((bf16[512,256]{1,0:T(8,128)(2,1)S(1)}, bf16[512,256]{1,0:T(8,128)(2,1)S(1)}, u32[]{:S(2)}, u32[]{:S(2)}) %collective-permute-start.9) | collective-permute-done | bytes 262176 | tf_op jit(solution)/shard_map/ppermute | solution.py:615
  89.7 1.0 mid_stage.1.mid_in
  90.7 2.2 %collective-permute-done.11.a3 = bf16[512,256]{1,0:T(8,128)(2,1)S(1)} collective-permute-done((bf16[512,256]{1,0:T(8,128)(2,1)S(1)}, bf16[512,256]{1,0:T(8,128)(2,1)S(1)}, u32[]{:S(2)}, u32[]{:S(2)}) %collective-permute-start.11) | collective-permute-done | bytes 262176 | tf_op jit(solution)/shard_map/ppermute | solution.py:615
  92.9 8.2 %ffn_stage.1 = bf16[512,1024]{1,0:T(8,128)(2,1)} custom-call(s32[1]{0:T(128)} %bitcast.z, f32[512,1024]{1,0:T(8,128)S(1)} %mid_stage.1.mid_in, bf16[512,256]{1,0:T(8,128)(2,1)S(1)} %collective-permute-done.11.a3, bf16[1024,1024]{1,0:T(8,128)(2,1)S(1)} %copy-done.1, bf16[1024,2048]{1,0:T(8,128)(2,1)S(1)} %copy-done.11, bf16[1024,2048]{1,0:T(8,128)(2,1)S(1)} %copy-done.12, ...), custom_call_target="tpu_custom_call" | custom-call | flops 6710886400 | bytes 18874368 | tf_op jit(solution)/shard_map/ffn_stage/pallas_call | solution.py:602
  (32 shorter events, 0.1 us)
Async XLA Ops:
  5.8 19.5 %all-to-all-start = ((bf16[32,48,128]{2,1,0:T(8,128)(2,1)}), bf16[32,48,128]{2,1,0:T(8,128)(2,1)S(1)}, u32[]{:S(2)}, u32[]{:S(2)}) async-start(bf16[32,48,128]{2,1,0:T(8,128)(2,1)} %get-tuple-element.34), calls=%async_computation | async-start | bytes 786432 | tf_op jit(solution)/shard_map/all_to_all | solution.py:624
  13.2 8.0 %collective-permute-start = (bf16[512,128]{1,0:T(8,128)(2,1)S(1)}, bf16[512,128]{1,0:T(8,128)(2,1)S(1)}, u32[]{:S(2)}, u32[]{:S(2)}) collective-permute-start(bf16[512,128]{1,0:T(8,128)(2,1)S(1)} %get-tuple-element.35), channel_id=1, source_target_pairs={{0,1},{1,2},{2,3},{3,0},{4,5},{5,6},{6,7},{7,4},{8,9},{9,10},{10,1... | collective-permute-start | bytes 393224 | tf_op jit(solution)/shard_map/ppermute | solution.py:615
  15.2 10.0 %collective-permute-start.1 = (bf16[512,128]{1,0:T(8,128)(2,1)S(1)}, bf16[512,128]{1,0:T(8,128)(2,1)S(1)}, u32[]{:S(2)}, u32[]{:S(2)}) collective-permute-start(bf16[512,128]{1,0:T(8,128)(2,1)S(1)} %get-tuple-element.36), channel_id=1, source_target_pairs={{0,2},{1,3},{2,0},{3,1},{4,6},{5,7},{6,4},{7,5},{8,10},{9,11},{10,... | collective-permute-start | bytes 393224 | tf_op jit(solution)/shard_map/ppermute | solution.py:615
  18.8 6.5 %collective-permute-start.2 = (bf16[512,128]{1,0:T(8,128)(2,1)S(1)}, bf16[512,128]{1,0:T(8,128)(2,1)S(1)}, u32[]{:S(2)}, u32[]{:S(2)}) collective-permute-start(bf16[512,128]{1,0:T(8,128)(2,1)S(1)} %get-tuple-element.37), channel_id=1, source_target_pairs={{0,3},{1,0},{2,1},{3,2},{4,7},{5,4},{6,5},{7,6},{8,11},{9,8},{10,9... | collective-permute-start | bytes 393224 | tf_op jit(solution)/shard_map/ppermute | solution.py:615
  28.6 44.6 %all-to-all-start.1 = ((bf16[32,256,128]{2,1,0:T(8,128)(2,1)}), bf16[32,256,128]{2,1,0:T(8,128)(2,1)S(1)}, u32[]{:S(2)}, u32[]{:S(2)}) async-start(bf16[32,256,128]{2,1,0:T(8,128)(2,1)} %bitcast.10), calls=%async_computation.1 | async-start | bytes 4194304 | tf_op jit(solution)/shard_map/all_to_all | solution.py:628
  35.8 18.9 %copy-start.10 = (f32[16]{0:T(128)S(1)}, f32[16]{0:T(128)}, u32[]{:S(2)}) copy-start(f32[16]{0:T(128)} %scale.13) | copy-start | bytes 196
  35.9 1.6 %copy-start.14 = (bf16[1024,1024]{1,0:T(8,128)(2,1)S(1)}, bf16[1024,1024]{1,0:T(8,128)(2,1)}, u32[]{:S(2)}) copy-start(bf16[1024,1024]{1,0:T(8,128)(2,1)} %w_query.1) | copy-start | bytes 6291460
  37.5 5.5 %copy-start.19 = (bf16[256,128]{1,0:T(8,128)(2,1)S(1)}, bf16[256,128]{1,0:T(8,128)(2,1)}, u32[]{:S(2)}) copy-start(bf16[256,128]{1,0:T(8,128)(2,1)} %get-tuple-element.39) | copy-start | bytes 196612
  37.5 6.4 %copy-start.18 = (bf16[256,128]{1,0:T(8,128)(2,1)S(1)}, bf16[256,128]{1,0:T(8,128)(2,1)}, u32[]{:S(2)}) copy-start(bf16[256,128]{1,0:T(8,128)(2,1)} %get-tuple-element.40) | copy-start | bytes 196612
  37.5 8.9 %copy-start.17 = (bf16[256,128]{1,0:T(8,128)(2,1)S(1)}, bf16[256,128]{1,0:T(8,128)(2,1)}, u32[]{:S(2)}) copy-start(bf16[256,128]{1,0:T(8,128)(2,1)} %get-tuple-element.41) | copy-start | bytes 196612
  37.5 17.3 %copy-start.16 = (bf16[256,128]{1,0:T(8,128)(2,1)S(1)}, bf16[256,128]{1,0:T(8,128)(2,1)}, u32[]{:S(2)}) copy-start(bf16[256,128]{1,0:T(8,128)(2,1)} %get-tuple-element.38.s0) | copy-start | bytes 196612
  41.6 18.7 %collective-permute-start.8 = (bf16[512,256]{1,0:T(8,128)(2,1)}, bf16[512,256]{1,0:T(8,128)(2,1)S(1)}, u32[]{:S(2)}, u32[]{:S(2)}) collective-permute-start(bf16[512,256]{1,0:T(8,128)(2,1)} %get-tuple-element.48), channel_id=1, source_target_pairs={{0,1},{1,2},{2,3},{3,0},{4,5},{5,6},{6,7},{7,4},{8,9},{9,10},{10,1... | collective-permute-start | bytes 786440 | tf_op jit(solution)/shard_map/ppermute | solution.py:615
  42.9 10.4 %collective-permute-start.3 = (bf16[256,128]{1,0:T(8,128)(2,1)S(1)}, bf16[256,128]{1,0:T(8,128)(2,1)S(1)}, u32[]{:S(2)}, u32[]{:S(2)}) collective-permute-start(bf16[256,128]{1,0:T(8,128)(2,1)S(1)} %copy-done.19), channel_id=1, source_target_pairs={{0,1},{1,2},{2,3},{3,0},{4,5},{5,6},{6,7},{7,4},{8,9},{9,10},{10,1... | collective-permute-start | bytes 196616 | tf_op jit(solution)/shard_map/ppermute | solution.py:615
  43.9 10.9 %collective-permute-start.4 = (bf16[256,128]{1,0:T(8,128)(2,1)S(1)}, bf16[256,128]{1,0:T(8,128)(2,1)S(1)}, u32[]{:S(2)}, u32[]{:S(2)}) collective-permute-start(bf16[256,128]{1,0:T(8,128)(2,1)S(1)} %copy-done.18), channel_id=1, source_target_pairs={{0,2},{1,3},{2,0},{3,1},{4,6},{5,7},{6,4},{7,5},{8,10},{9,11},{10,... | collective-permute-start | bytes 196616 | tf_op jit(solution)/shard_map/ppermute | solution.py:615
  46.4 8.4 %collective-permute-start.5 = (bf16[256,128]{1,0:T(8,128)(2,1)S(1)}, bf16[256,128]{1,0:T(8,128)(2,1)S(1)}, u32[]{:S(2)}, u32[]{:S(2)}) collective-permute-start(bf16[256,128]{1,0:T(8,128)(2,1)S(1)} %copy-done.17), channel_id=1, source_target_pairs={{0,3},{1,0},{2,1},{3,2},{4,7},{5,4},{6,5},{7,6},{8,11},{9,8},{10,9... | collective-permute-start | bytes 196616 | tf_op jit(solution)/shard_map/ppermute | solution.py:615
  47.9 16.9 %collective-permute-start.6 = (bf16[512,256]{1,0:T(8,128)(2,1)}, bf16[512,256]{1,0:T(8,128)(2,1)S(1)}, u32[]{:S(2)}, u32[]{:S(2)}) collective-permute-start(bf16[512,256]{1,0:T(8,128)(2,1)} %get-tuple-element.46), channel_id=1, source_target_pairs={{0,3},{1,0},{2,1},{3,2},{4,7},{5,4},{6,5},{7,6},{8,11},{9,8},{10,9... | collective-permute-start | bytes 786440 | tf_op jit(solution)/shard_map/ppermute | solution.py:615
  53.3 11.6 %collective-permute-start.7 = (bf16[512,256]{1,0:T(8,128)(2,1)}, bf16[512,256]{1,0:T(8,128)(2,1)S(1)}, u32[]{:S(2)}, u32[]{:S(2)}) collective-permute-start(bf16[512,256]{1,0:T(8,128)(2,1)} %get-tuple-element.47), channel_id=1, source_target_pairs={{0,2},{1,3},{2,0},{3,1},{4,6},{5,7},{6,4},{7,5},{8,10},{9,11},{10,... | collective-permute-start | bytes 786440 | tf_op jit(solution)/shard_map/ppermute | solution.py:615
  54.8 1.0 copy-start.8
  55.7 4.6 %copy-start.15 = (bf16[4,4,128,128]{3,2,1,0:T(8,128)(2,1)S(1)}, bf16[4,4,128,128]{3,2,1,0:T(8,128)(2,1)}, u32[]{:S(2)}) copy-start(bf16[4,4,128,128]{3,2,1,0:T(8,128)(2,1)} %get-tuple-element.45.kv) | copy-start | bytes 1572868
  73.2 5.9 %copy-start.3 = (f32[2,4,256,128]{3,2,1,0:T(8,128)S(1)}, f32[2,4,256,128]{3,2,1,0:T(8,128)}, u32[]{:S(2)}) copy-start(f32[2,4,256,128]{3,2,1,0:T(8,128)} %get-tuple-element.49.rest_2_.state) | copy-start | bytes 3145732
  73.2 5.9 %copy-start.6 = (bf16[2,4,256,128]{3,2,1,0:T(8,128)(2,1)S(1)}, bf16[2,4,256,128]{3,2,1,0:T(8,128)(2,1)}, u32[]{:S(2)}) copy-start(bf16[2,4,256,128]{3,2,1,0:T(8,128)(2,1)} %get-tuple-element.50.rest_3_.peaks) | copy-start | bytes 1572868
  76.7 6.1 %copy-start.4 = (f32[2,4,256,128]{3,2,1,0:T(8,128)S(1)}, f32[2,4,256,128]{3,2,1,0:T(8,128)}, u32[]{:S(2)}) copy-start(f32[2,4,256,128]{3,2,1,0:T(8,128)} %get-tuple-element.53.state) | copy-start | bytes 3145732
  76.7 6.1 %copy-start.7 = (bf16[2,4,256,128]{3,2,1,0:T(8,128)(2,1)S(1)}, bf16[2,4,256,128]{3,2,1,0:T(8,128)(2,1)}, u32[]{:S(2)}) copy-start(bf16[2,4,256,128]{3,2,1,0:T(8,128)(2,1)} %get-tuple-element.54.peaks) | copy-start | bytes 1572868
  76.7 11.7 %collective-permute-start.10 = (bf16[512,256]{1,0:T(8,128)(2,1)S(1)}, bf16[512,256]{1,0:T(8,128)(2,1)S(1)}, u32[]{:S(2)}, u32[]{:S(2)}) collective-permute-start(bf16[512,256]{1,0:T(8,128)(2,1)S(1)} %far_stage.6), channel_id=1, source_target_pairs={{0,2},{1,3},{2,0},{3,1},{4,6},{5,7},{6,4},{7,5},{8,10},{9,11},{10,... | collective-permute-start | bytes 786440 | tf_op jit(solution)/shard_map/ppermute | solution.py:615
  81.4 8.3 %collective-permute-start.9 = (bf16[512,256]{1,0:T(8,128)(2,1)S(1)}, bf16[512,256]{1,0:T(8,128)(2,1)S(1)}, u32[]{:S(2)}, u32[]{:S(2)}) collective-permute-start(bf16[512,256]{1,0:T(8,128)(2,1)S(1)} %far_stage.5), channel_id=1, source_target_pairs={{0,3},{1,0},{2,1},{3,2},{4,7},{5,4},{6,5},{7,6},{8,11},{9,8},{10,9... | collective-permute-start | bytes 786440 | tf_op jit(solution)/shard_map/ppermute | solution.py:615
  82.8 3.2 %copy-start.2 = (f32[2,4,256,128]{3,2,1,0:T(8,128)S(1)}, f32[2,4,256,128]{3,2,1,0:T(8,128)}, u32[]{:S(2)}) copy-start(f32[2,4,256,128]{3,2,1,0:T(8,128)} %get-tuple-element.42.rest_1_.state) | copy-start | bytes 3145732
  82.8 3.2 %copy-start.5 = (bf16[2,4,256,128]{3,2,1,0:T(8,128)(2,1)S(1)}, bf16[2,4,256,128]{3,2,1,0:T(8,128)(2,1)}, u32[]{:S(2)}) copy-start(bf16[2,4,256,128]{3,2,1,0:T(8,128)(2,1)} %get-tuple-element.43.rest_2_.peaks) | copy-start | bytes 1572868
  82.8 3.2 %copy-start.9 = (bf16[512,256]{1,0:T(8,128)(2,1)S(1)}, bf16[512,256]{1,0:T(8,128)(2,1)}, u32[]{:S(2)}) copy-start(bf16[512,256]{1,0:T(8,128)(2,1)} %get-tuple-element.32.rest_0_.q) | copy-start | bytes 786436
  82.8 10.0 %copy-start.13 = (bf16[2048,1024]{1,0:T(8,128)(2,1)S(1)}, bf16[2048,1024]{1,0:T(8,128)(2,1)}, u32[]{:S(2)}) copy-start(bf16[2048,1024]{1,0:T(8,128)(2,1)} %w_down.1) | copy-start | bytes 12582916
  85.2 4.5 %copy-start = (bf16[512,1024]{1,0:T(8,128)(2,1)S(1)}, bf16[512,1024]{1,0:T(8,128)(2,1)}, u32[]{:S(2)}) copy-start(bf16[512,1024]{1,0:T(8,128)(2,1)} %tokens.1) | copy-start | bytes 3145732
  85.2 4.5 %copy-start.1 = (bf16[1024,1024]{1,0:T(8,128)(2,1)S(1)}, bf16[1024,1024]{1,0:T(8,128)(2,1)}, u32[]{:S(2)}) copy-start(bf16[1024,1024]{1,0:T(8,128)(2,1)} %w_out.3) | copy-start | bytes 6291460
  85.2 7.7 %collective-permute-start.11 = (bf16[512,256]{1,0:T(8,128)(2,1)S(1)}, bf16[512,256]{1,0:T(8,128)(2,1)S(1)}, u32[]{:S(2)}, u32[]{:S(2)}) collective-permute-start(bf16[512,256]{1,0:T(8,128)(2,1)S(1)} %far_stage.7), channel_id=1, source_target_pairs={{0,1},{1,2},{2,3},{3,0},{4,5},{5,6},{6,7},{7,4},{8,9},{9,10},{10,1... | collective-permute-start | bytes 786440 | tf_op jit(solution)/shard_map/ppermute | solution.py:615
  86.0 6.9 %copy-start.12 = (bf16[1024,2048]{1,0:T(8,128)(2,1)S(1)}, bf16[1024,2048]{1,0:T(8,128)(2,1)}, u32[]{:S(2)}) copy-start(bf16[1024,2048]{1,0:T(8,128)(2,1)} %w_up.1) | copy-start | bytes 12582916
  88.4 4.5 %copy-start.11 = (bf16[1024,2048]{1,0:T(8,128)(2,1)S(1)}, bf16[1024,2048]{1,0:T(8,128)(2,1)}, u32[]{:S(2)}) copy-start(bf16[1024,2048]{1,0:T(8,128)(2,1)} %w_gate.1) | copy-start | bytes 12582916
